TPU v7x, 256 devices: a whole 4x4x8 slice. The times are simulated.
256 devices in a mesh: gx: 16 (over x, z_lo), gy: 16 (over z_hi, y, core).
Axes of the slice: x: 4, y: 4, z: 8 (z_hi: 2, z_lo: 4; z = z_hi * 4 + z_lo), core: 2. Of those that a mesh axis runs over, the one named last changes fastest.
Arguments:
- right_side: float32 [3, 448, 49728], P(None, 'gx', 'gy'), may hold values from -6 to 6
- guess: float32 [3, 448, 49728], P(None, 'gx', 'gy'), may hold values from -6 to 6
- material: int32 [64, 64, 16], P('gx', 'gy'), may hold values from 0 to 7
- lame: float32 [2, 8], replicated, may hold values from 0.5 to 2
- upper: float32 [1], replicated, may hold values from 3 to 6
- lower_ratio: float32 [1], replicated, may hold values from 0.05 to 0.3
Outputs:
- smoothed: float32 [3, 448, 49728], P(None, 'gx', 'gy')
- residual: float32 [3, 448, 49728], P(None, 'gx', 'gy')
All inputs are finite; a program needn't handle non-finite values.
Results may differ from a plain program's by a relative error of at most 0.0003.
Values sent between devices are 32-bit elements; how exact they have to be, the bound alone decides.
No kernel may reach another device: no remote copies, remote signals or barrier semaphores. Data moves between devices by JAX's collectives and lax.ppermute only.
A program may use at most 128 MiB of HBM per device.

v0:
```python
import jax
import jax.numpy as jnp
import numpy as np
from jax import lax
from jax.sharding import PartitionSpec as P

DEG = 7
SWEEPS = 2
CHEB = 3


highest = lax.Precision.HIGHEST


def from_behind(value, axis, by):
    size = lax.axis_size(axis)
    return lax.ppermute(value, axis, [(i, (i + by) % size) for i in range(size)])


def legendre_pair(points, degree):
    prev_poly = points * 0.0 + 1.0
    this_poly = points * 1.0
    for order in range(2, degree + 1):
        next_poly = ((2 * order - 1) * points * this_poly - (order - 1) * prev_poly) / order
        prev_poly = this_poly
        this_poly = next_poly
    return (this_poly, prev_poly)


def gll_tables(degree):
    count = degree + 1
    points = -np.cos(np.pi * np.arange(count) / degree)
    for newton_step in range(60):
        this_poly, prev_poly = legendre_pair(points, degree)
        points = points - (points * this_poly - prev_poly) / (count * this_poly)
    values, unused_poly = legendre_pair(points, degree)
    weights = 2.0 / (degree * (degree + 1) * values**2)
    identity_np = np.eye(count)
    spacing = points[:, None] - points[None, :] + identity_np
    derivative = values[:, None] / (values[None, :] * spacing) * (1.0 - identity_np)
    derivative[0, 0] = -degree * (degree + 1) / 4.0
    derivative[degree, degree] = degree * (degree + 1) / 4.0
    stiff_ratio = (weights[:, None] * derivative**2).sum(0) / weights
    return (weights, derivative, stiff_ratio)


def clamped_gather(blocks):
    free_nodes = DEG * blocks - 1
    selector = np.zeros((free_nodes, blocks * (DEG + 1)), np.float32)
    for element in range(blocks):
        for node_idx in range(DEG + 1):
            target = DEG * element + node_idx - 1
            if 0 <= target < free_nodes:
                selector[target, element * (DEG + 1) + node_idx] = 1.0
    return selector


def split_open(field_in, dim_index):
    layout = field_in.shape
    blocks = (layout[dim_index] - 1) // DEG
    leading = lax.slice_in_dim(field_in, 0, blocks * DEG, axis=dim_index)
    leading = leading.reshape(layout[:dim_index] + (blocks, DEG) + layout[dim_index + 1 :])
    trailing = lax.slice_in_dim(field_in, DEG, blocks * DEG + 1, stride=DEG, axis=dim_index)
    trailing = jnp.expand_dims(trailing, dim_index + 1)
    return jnp.concatenate([leading, trailing], axis=dim_index + 1)


def fold_open(element_vals, dim_index):
    layout = element_vals.shape
    blocks = layout[dim_index]
    merged = layout[:dim_index] + (blocks * DEG,) + layout[dim_index + 2 :]
    leading = lax.slice_in_dim(element_vals, 0, DEG, axis=dim_index + 1).reshape(merged)
    trailing = lax.slice_in_dim(element_vals, DEG, DEG + 1, axis=dim_index + 1)
    widths = [(0, 0)] * len(layout)
    widths[dim_index + 1] = (DEG - 1, 0)
    spread_tail = jnp.pad(trailing, widths).reshape(merged)
    after_pad = [(0, 0)] * len(merged)
    after_pad[dim_index] = (0, 1)
    before_pad = [(0, 0)] * len(merged)
    before_pad[dim_index] = (1, 0)
    return jnp.pad(leading, after_pad) + jnp.pad(spread_tail, before_pad)


def along_z(field_in, matrix):
    layout = field_in.shape
    block_size = matrix.shape[0]
    pieces = field_in.reshape(layout[:-1] + (layout[-1] // block_size, block_size))
    return jnp.matmul(pieces, matrix, precision=highest).reshape(layout)


def element_forces(element_vals, lam_w, mu_w, derivative, z_grad, z_back):
    grad_x = jnp.einsum("pi,cxiyjz->cxpyjz", derivative, element_vals, precision=highest)
    grad_y = jnp.einsum("pj,cxiyjz->cxiypz", derivative, element_vals, precision=highest)
    grad_z = along_z(element_vals, z_grad)
    gradients = jnp.stack([grad_x, grad_y, grad_z])
    divergence = gradients[0, 0] + gradients[1, 1] + gradients[2, 2]
    identity = jnp.eye(3, dtype=jnp.float32).reshape(3, 3, 1, 1, 1, 1, 1)
    stress = mu_w * (gradients + jnp.swapaxes(gradients, 0, 1)) + lam_w * divergence * identity
    forces = jnp.einsum("pi,cxpyjz->cxiyjz", derivative, stress[0], precision=highest)
    forces = forces + jnp.einsum("pj,cxiypz->cxiyjz", derivative, stress[1], precision=highest)
    return forces + along_z(stress[2], z_back)


def element_diagonal(lam_w, mu_w, ratio_x, ratio_y, ratio_z):
    ratio_sum = ratio_x + ratio_y + ratio_z
    pieces = [
        lam_w * own_ratio + mu_w * (ratio_sum + own_ratio)
        for own_ratio in (ratio_x, ratio_y, ratio_z)
    ]
    return jnp.stack(pieces)


def point_coeffs(lam_el, mu_el, point_w):
    lam_rep = jnp.repeat(lam_el, DEG + 1, axis=2)[:, None, :, None, :]
    mu_rep = jnp.repeat(mu_el, DEG + 1, axis=2)[:, None, :, None, :]
    return (lam_rep * point_w, mu_rep * point_w)


def lame_fields(material, lame):
    labels = jnp.arange(lame.shape[1], dtype=jnp.int32)
    onehot = (material[..., None] == labels).astype(jnp.float32)
    coeffs = jnp.einsum("xyzm,km->kxyz", onehot, lame, precision=highest)
    return (coeffs[0], coeffs[1])


def gather_near(field_in):
    next_x = from_behind(field_in[:, :1], "gx", -1)
    wider_x = jnp.concatenate([field_in, next_x], 1)
    next_y = from_behind(wider_x[:, :, :1], "gy", -1)
    return jnp.concatenate([wider_x, next_y], 2)


def return_sums(partial_value, width_x, width_y):
    from_y = from_behind(partial_value[:, :, width_y:], "gy", 1)
    part_y = partial_value[:, :, :width_y].at[:, :, :1].add(from_y)
    from_x = from_behind(part_y[:, width_x:], "gx", 1)
    return part_y[:, :width_x].at[:, :1].add(from_x)


def local(right_side, guess, material, lame, upper, lower_ratio):
    elems_x, elems_y, elems_z = material.shape
    nodes_x = DEG * elems_x
    nodes_y = DEG * elems_y
    nodes_z = DEG * elems_z - 1
    shape_four = (3, nodes_x, nodes_y, nodes_z)
    source = right_side.reshape(shape_four)
    solution = guess.reshape(shape_four)
    weights_np, derivative_np, ratio_np = gll_tables(DEG)
    weights = jnp.asarray(weights_np, dtype=jnp.float32)
    derivative = jnp.asarray(derivative_np, dtype=jnp.float32)
    stiff_ratio = jnp.asarray(ratio_np, dtype=jnp.float32)
    block_size = min(128, (DEG + 1) * elems_z)
    z_grad = jnp.asarray(
        np.kron(np.eye(block_size // (DEG + 1)), derivative_np.T), dtype=jnp.float32
    )
    z_back = jnp.asarray(np.kron(np.eye(block_size // (DEG + 1)), derivative_np), dtype=jnp.float32)
    gather_z = jnp.asarray(clamped_gather(elems_z), dtype=jnp.float32)
    gather_t = jnp.asarray(clamped_gather(elems_z).T, dtype=jnp.float32)
    weights_z = jnp.tile(weights, elems_z)
    point_w = (
        weights[None, :, None, None, None]
        * weights[None, None, None, :, None]
        * weights_z[None, None, None, None, :]
    )
    ratio_x = stiff_ratio.reshape(1, DEG + 1, 1, 1, 1)
    ratio_y = stiff_ratio.reshape(1, 1, 1, DEG + 1, 1)
    ratio_z = jnp.tile(stiff_ratio, elems_z).reshape(1, 1, 1, 1, -1)

    def local_operator(extended, lam_w, mu_w):
        z_local = jnp.matmul(extended, gather_z, precision=highest)
        element_vals = split_open(split_open(z_local, 1), 3)
        forces = element_forces(element_vals, lam_w, mu_w, derivative, z_grad, z_back)
        return jnp.matmul(fold_open(fold_open(forces, 3), 1), gather_t, precision=highest)

    lam_el, mu_el = lame_fields(material, lame)
    lam_w, mu_w = point_coeffs(lam_el, mu_el, point_w)
    pieces = element_diagonal(lam_w, mu_w, ratio_x, ratio_y, ratio_z)
    diagonal = return_sums(
        jnp.matmul(fold_open(fold_open(pieces, 3), 1), gather_t, precision=highest),
        nodes_x,
        nodes_y,
    )

    def apply_operator(field_in):
        partial_value = local_operator(gather_near(field_in), lam_w, mu_w)
        return return_sums(partial_value, nodes_x, nodes_y)

    inverse = 1.0 / diagonal
    upper_edge = upper[0]
    lower_edge = lower_ratio[0] * upper_edge
    center = (upper_edge + lower_edge) / 2.0
    radius = (upper_edge - lower_edge) / 2.0
    sigma_ratio = center / radius
    for sweep_index in range(SWEEPS):
        residual = source - apply_operator(solution)
        change = inverse * residual / center
        solution = solution + change
        factor = 1.0 / sigma_ratio
        for step_index in range(CHEB - 1):
            factor_next = 1.0 / (2.0 * sigma_ratio - factor)
            residual = source - apply_operator(solution)
            change = factor_next * factor * change + 2.0 * factor_next / radius * inverse * residual
            solution = solution + change
            factor = factor_next
    residual = source - apply_operator(solution)
    flat_shape = (3, nodes_x, nodes_y * nodes_z)
    return (solution.reshape(flat_shape), residual.reshape(flat_shape))


def solution(mesh):
    placed = (P(None, "gx", "gy"), P(None, "gx", "gy"), P("gx", "gy", None), P(), P(), P())
    return jax.shard_map(
        local,
        mesh=mesh,
        in_specs=placed,
        out_specs=(P(None, "gx", "gy"), P(None, "gx", "gy")),
        check_vma=False,
    )
```

profile of v0, /device:TPU:0, one launch (start us, length us, event | category | flops | bytes accessed | tf_op | source)
XLA Modules:
  0.0 372.8 jit_solution(13379757365346901346)
XLA Ops:
  0.7 3.6 reshape.920
  4.9 5.1 %collective-permute-start.2 = (f32[3,1,28,111]{3,2,1,0:T(8,128)}, f32[3,1,28,111]{3,2,1,0:T(8,128)}, u32[]{:S(2)}, u32[]{:S(2)}) collective-permute-start(f32[3,1,28,111]{3,2,1,0:T(8,128)} %slice.1107), channel_id=1, source_target_pairs={{0,240},{16,0},{32,16},{48,32},{64,48},{80,64},{96,80},{112,96},{1... | collective-permute-start | bytes 111896 | tf_op jit(solution)/shard_map/ppermute | solution.py:17
  17.1 8.1 %collective-permute-start.3 = (f32[3,29,1,111]{3,2,1,0:T(1,128)S(1)}, f32[3,29,1,111]{3,2,1,0:T(1,128)S(1)}, u32[]{:S(2)}, u32[]{:S(2)}) collective-permute-start(f32[3,29,1,111]{3,2,1,0:T(1,128)S(1)} %slice.1108), channel_id=1, source_target_pairs={{0,15},{1,0},{2,1},{3,2},{4,3},{5,4},{6,5},{7,6},{8,7},{9,8},{10,9... | collective-permute-start | bytes 115892 | tf_op jit(solution)/shard_map/ppermute | solution.py:17
  28.8 2.7 fusion.63
  58.0 4.4 %collective-permute-done.4 = f32[3,29,1,111]{3,2,1,0:T(1,128)} collective-permute-done((f32[3,29,1,111]{3,2,1,0:T(1,128)}, f32[3,29,1,111]{3,2,1,0:T(1,128)}, u32[]{:S(2)}, u32[]{:S(2)}) %collective-permute-start.4) | collective-permute-done | bytes 38660 | tf_op jit(solution)/shard_map/ppermute | solution.py:17
  68.7 5.5 %collective-permute-done.5 = f32[3,1,28,111]{3,2,1,0:T(8,128)S(1)} collective-permute-done((f32[3,1,28,111]{3,2,1,0:T(8,128)S(1)}, f32[3,1,28,111]{3,2,1,0:T(8,128)S(1)}, u32[]{:S(2)}, u32[]{:S(2)}) %collective-permute-start.5) | collective-permute-done | bytes 37328 | tf_op jit(solution)/shard_map/ppermute | solution.py:17
  76.6 3.7 %collective-permute-done.6 = f32[3,1,28,111]{3,2,1,0:T(8,128)S(1)} collective-permute-done((f32[3,1,28,111]{3,2,1,0:T(8,128)S(1)}, f32[3,1,28,111]{3,2,1,0:T(8,128)S(1)}, u32[]{:S(2)}, u32[]{:S(2)}) %collective-permute-start.6) | collective-permute-done | bytes 37328 | tf_op jit(solution)/shard_map/ppermute | solution.py:17
  102.5 9.6 %collective-permute-done.8 = f32[3,29,1,111]{3,2,1,0:T(1,128)S(1)} collective-permute-done((f32[3,29,1,111]{3,2,1,0:T(1,128)S(1)}, f32[3,29,1,111]{3,2,1,0:T(1,128)S(1)}, u32[]{:S(2)}, u32[]{:S(2)}) %collective-permute-start.8) | collective-permute-done | bytes 38660 | tf_op jit(solution)/shard_map/ppermute | solution.py:17
  117.3 6.5 %collective-permute-done.9 = f32[3,1,28,111]{3,2,1,0:T(8,128)} collective-permute-done((f32[3,1,28,111]{3,2,1,0:T(8,128)}, f32[3,1,28,111]{3,2,1,0:T(8,128)}, u32[]{:S(2)}, u32[]{:S(2)}) %collective-permute-start.9) | collective-permute-done | bytes 37328 | tf_op jit(solution)/shard_map/ppermute | solution.py:17
  127.7 2.4 collective-permute-done.10
  151.4 9.5 %collective-permute-done.12 = f32[3,29,1,111]{3,2,1,0:T(1,128)S(1)} collective-permute-done((f32[3,29,1,111]{3,2,1,0:T(1,128)S(1)}, f32[3,29,1,111]{3,2,1,0:T(1,128)S(1)}, u32[]{:S(2)}, u32[]{:S(2)}) %collective-permute-start.12) | collective-permute-done | bytes 38660 | tf_op jit(solution)/shard_map/ppermute | solution.py:17
  166.5 6.3 %collective-permute-done.13 = f32[3,1,28,111]{3,2,1,0:T(8,128)} collective-permute-done((f32[3,1,28,111]{3,2,1,0:T(8,128)}, f32[3,1,28,111]{3,2,1,0:T(8,128)}, u32[]{:S(2)}, u32[]{:S(2)}) %collective-permute-start.13) | collective-permute-done | bytes 37328 | tf_op jit(solution)/shard_map/ppermute | solution.py:17
  173.6 2.4 add_add_fusion.1
  201.6 9.5 %collective-permute-done.16 = f32[3,29,1,111]{3,2,1,0:T(1,128)S(1)} collective-permute-done((f32[3,29,1,111]{3,2,1,0:T(1,128)S(1)}, f32[3,29,1,111]{3,2,1,0:T(1,128)S(1)}, u32[]{:S(2)}, u32[]{:S(2)}) %collective-permute-start.16) | collective-permute-done | bytes 38660 | tf_op jit(solution)/shard_map/ppermute | solution.py:17
  215.4 6.7 %collective-permute-done.17 = f32[3,1,28,111]{3,2,1,0:T(8,128)S(1)} collective-permute-done((f32[3,1,28,111]{3,2,1,0:T(8,128)S(1)}, f32[3,1,28,111]{3,2,1,0:T(8,128)S(1)}, u32[]{:S(2)}, u32[]{:S(2)}) %collective-permute-start.17) | collective-permute-done | bytes 37328 | tf_op jit(solution)/shard_map/ppermute | solution.py:17
  249.4 9.6 %collective-permute-done.20 = f32[3,29,1,111]{3,2,1,0:T(1,128)S(1)} collective-permute-done((f32[3,29,1,111]{3,2,1,0:T(1,128)S(1)}, f32[3,29,1,111]{3,2,1,0:T(1,128)S(1)}, u32[]{:S(2)}, u32[]{:S(2)}) %collective-permute-start.20) | collective-permute-done | bytes 38660 | tf_op jit(solution)/shard_map/ppermute | solution.py:17
  263.3 6.4 %collective-permute-done.21 = f32[3,1,28,111]{3,2,1,0:T(8,128)S(1)} collective-permute-done((f32[3,1,28,111]{3,2,1,0:T(8,128)S(1)}, f32[3,1,28,111]{3,2,1,0:T(8,128)S(1)}, u32[]{:S(2)}, u32[]{:S(2)}) %collective-permute-start.21) | collective-permute-done | bytes 37328 | tf_op jit(solution)/shard_map/ppermute | solution.py:17
  297.3 9.5 %collective-permute-done.24 = f32[3,29,1,111]{3,2,1,0:T(1,128)S(1)} collective-permute-done((f32[3,29,1,111]{3,2,1,0:T(1,128)S(1)}, f32[3,29,1,111]{3,2,1,0:T(1,128)S(1)}, u32[]{:S(2)}, u32[]{:S(2)}) %collective-permute-start.24) | collective-permute-done | bytes 38660 | tf_op jit(solution)/shard_map/ppermute | solution.py:17
  311.2 6.4 %collective-permute-done.25 = f32[3,1,28,111]{3,2,1,0:T(8,128)S(1)} collective-permute-done((f32[3,1,28,111]{3,2,1,0:T(8,128)S(1)}, f32[3,1,28,111]{3,2,1,0:T(8,128)S(1)}, u32[]{:S(2)}, u32[]{:S(2)}) %collective-permute-start.25) | collective-permute-done | bytes 37328 | tf_op jit(solution)/shard_map/ppermute | solution.py:17
  318.4 2.4 add_add_fusion
  341.4 2.3 fusion.28
  346.3 9.5 %collective-permute-done.28 = f32[3,29,1,111]{3,2,1,0:T(1,128)S(1)} collective-permute-done((f32[3,29,1,111]{3,2,1,0:T(1,128)S(1)}, f32[3,29,1,111]{3,2,1,0:T(1,128)S(1)}, u32[]{:S(2)}, u32[]{:S(2)}) %collective-permute-start.28) | collective-permute-done | bytes 38660 | tf_op jit(solution)/shard_map/ppermute | solution.py:17
  362.3 4.3 %collective-permute-done.29 = f32[3,1,28,111]{3,2,1,0:T(8,128)S(1)} collective-permute-done((f32[3,1,28,111]{3,2,1,0:T(8,128)S(1)}, f32[3,1,28,111]{3,2,1,0:T(8,128)S(1)}, u32[]{:S(2)}, u32[]{:S(2)}) %collective-permute-start.29) | collective-permute-done | bytes 37328 | tf_op jit(solution)/shard_map/ppermute | solution.py:17
  368.8 3.6 reshape.976
  (441 shorter events, 227.9 us)
Async XLA Ops:
  4.9 11.2 %collective-permute-start.2 = (f32[3,1,28,111]{3,2,1,0:T(8,128)}, f32[3,1,28,111]{3,2,1,0:T(8,128)}, u32[]{:S(2)}, u32[]{:S(2)}) collective-permute-start(f32[3,1,28,111]{3,2,1,0:T(8,128)} %slice.1107), channel_id=1, source_target_pairs={{0,240},{16,0},{32,16},{48,32},{64,48},{80,64},{96,80},{112,96},{1... | collective-permute-start | bytes 111896 | tf_op jit(solution)/shard_map/ppermute | solution.py:17
  16.0 36.2 %collective-permute-start = (f32[3,29,1,111]{3,2,1,0:T(1,128)}, f32[3,29,1,111]{3,2,1,0:T(1,128)S(1)}, u32[]{:S(2)}, u32[]{:S(2)}) collective-permute-start(f32[3,29,1,111]{3,2,1,0:T(1,128)} %slice.1103), channel_id=1, source_target_pairs={{0,1},{1,2},{2,3},{3,4},{4,5},{5,6},{6,7},{7,8},{8,9},{9,10},{10,1... | collective-permute-start | bytes 115892 | tf_op jit(solution)/shard_map/ppermute | solution.py:17
  17.1 11.7 %collective-permute-start.3 = (f32[3,29,1,111]{3,2,1,0:T(1,128)S(1)}, f32[3,29,1,111]{3,2,1,0:T(1,128)S(1)}, u32[]{:S(2)}, u32[]{:S(2)}) collective-permute-start(f32[3,29,1,111]{3,2,1,0:T(1,128)S(1)} %slice.1108), channel_id=1, source_target_pairs={{0,15},{1,0},{2,1},{3,2},{4,3},{5,4},{6,5},{7,6},{8,7},{9,8},{10,9... | collective-permute-start | bytes 115892 | tf_op jit(solution)/shard_map/ppermute | solution.py:17
  52.1 10.3 %collective-permute-start.4 = (f32[3,29,1,111]{3,2,1,0:T(1,128)}, f32[3,29,1,111]{3,2,1,0:T(1,128)}, u32[]{:S(2)}, u32[]{:S(2)}) collective-permute-start(f32[3,29,1,111]{3,2,1,0:T(1,128)} %slice.1124), channel_id=1, source_target_pairs={{0,1},{1,2},{2,3},{3,4},{4,5},{5,6},{6,7},{7,8},{8,9},{9,10},{10,1... | collective-permute-start | bytes 115892 | tf_op jit(solution)/shard_map/ppermute | solution.py:17
  58.0 8.4 %collective-permute-start.1 = (f32[3,1,28,111]{3,2,1,0:T(8,128)}, f32[3,1,28,111]{3,2,1,0:T(8,128)}, u32[]{:S(2)}, u32[]{:S(2)}) collective-permute-start(f32[3,1,28,111]{3,2,1,0:T(8,128)} %slice.1106), channel_id=1, source_target_pairs={{0,16},{16,32},{32,48},{48,64},{64,80},{80,96},{96,112},{112,128},... | collective-permute-start | bytes 111896 | tf_op jit(solution)/shard_map/ppermute | solution.py:17
  66.2 8.0 %collective-permute-start.5 = (f32[3,1,28,111]{3,2,1,0:T(8,128)S(1)}, f32[3,1,28,111]{3,2,1,0:T(8,128)S(1)}, u32[]{:S(2)}, u32[]{:S(2)}) collective-permute-start(f32[3,1,28,111]{3,2,1,0:T(8,128)S(1)} %slice.1127), channel_id=1, source_target_pairs={{0,16},{16,32},{32,48},{48,64},{64,80},{80,96},{96,112},{112,128},... | collective-permute-start | bytes 111896 | tf_op jit(solution)/shard_map/ppermute | solution.py:17
  76.1 4.2 %collective-permute-start.6 = (f32[3,1,28,111]{3,2,1,0:T(8,128)S(1)}, f32[3,1,28,111]{3,2,1,0:T(8,128)S(1)}, u32[]{:S(2)}, u32[]{:S(2)}) collective-permute-start(f32[3,1,28,111]{3,2,1,0:T(8,128)S(1)} %slice.1128), channel_id=1, source_target_pairs={{0,240},{16,0},{32,16},{48,32},{64,48},{80,64},{96,80},{112,96},{1... | collective-permute-start | bytes 111896 | tf_op jit(solution)/shard_map/ppermute | solution.py:17
  102.4 9.7 %collective-permute-start.8 = (f32[3,29,1,111]{3,2,1,0:T(1,128)S(1)}, f32[3,29,1,111]{3,2,1,0:T(1,128)S(1)}, u32[]{:S(2)}, u32[]{:S(2)}) collective-permute-start(f32[3,29,1,111]{3,2,1,0:T(1,128)S(1)} %slice.1144), channel_id=1, source_target_pairs={{0,1},{1,2},{2,3},{3,4},{4,5},{5,6},{6,7},{7,8},{8,9},{9,10},{10,1... | collective-permute-start | bytes 115892 | tf_op jit(solution)/shard_map/ppermute | solution.py:17
  115.5 8.3 %collective-permute-start.9 = (f32[3,1,28,111]{3,2,1,0:T(8,128)}, f32[3,1,28,111]{3,2,1,0:T(8,128)}, u32[]{:S(2)}, u32[]{:S(2)}) collective-permute-start(f32[3,1,28,111]{3,2,1,0:T(8,128)} %slice.1147), channel_id=1, source_target_pairs={{0,16},{16,32},{32,48},{48,64},{64,80},{80,96},{96,112},{112,128},... | collective-permute-start | bytes 111896 | tf_op jit(solution)/shard_map/ppermute | solution.py:17
  126.0 4.1 %collective-permute-start.10 = (f32[3,1,28,111]{3,2,1,0:T(8,128)S(1)}, f32[3,1,28,111]{3,2,1,0:T(8,128)S(1)}, u32[]{:S(2)}, u32[]{:S(2)}) collective-permute-start(f32[3,1,28,111]{3,2,1,0:T(8,128)S(1)} %slice.1148), channel_id=1, source_target_pairs={{0,240},{16,0},{32,16},{48,32},{64,48},{80,64},{96,80},{112,96},{1... | collective-permute-start | bytes 111896 | tf_op jit(solution)/shard_map/ppermute | solution.py:17
  151.3 9.6 %collective-permute-start.12 = (f32[3,29,1,111]{3,2,1,0:T(1,128)S(1)}, f32[3,29,1,111]{3,2,1,0:T(1,128)S(1)}, u32[]{:S(2)}, u32[]{:S(2)}) collective-permute-start(f32[3,29,1,111]{3,2,1,0:T(1,128)S(1)} %slice.1164), channel_id=1, source_target_pairs={{0,1},{1,2},{2,3},{3,4},{4,5},{5,6},{6,7},{7,8},{8,9},{9,10},{10,1... | collective-permute-start | bytes 115892 | tf_op jit(solution)/shard_map/ppermute | solution.py:17
  164.3 8.5 %collective-permute-start.13 = (f32[3,1,28,111]{3,2,1,0:T(8,128)}, f32[3,1,28,111]{3,2,1,0:T(8,128)}, u32[]{:S(2)}, u32[]{:S(2)}) collective-permute-start(f32[3,1,28,111]{3,2,1,0:T(8,128)} %slice.1167), channel_id=1, source_target_pairs={{0,16},{16,32},{32,48},{48,64},{64,80},{80,96},{96,112},{112,128},... | collective-permute-start | bytes 111896 | tf_op jit(solution)/shard_map/ppermute | solution.py:17
  176.0 4.2 %collective-permute-start.14 = (f32[3,1,28,111]{3,2,1,0:T(8,128)S(1)}, f32[3,1,28,111]{3,2,1,0:T(8,128)S(1)}, u32[]{:S(2)}, u32[]{:S(2)}) collective-permute-start(f32[3,1,28,111]{3,2,1,0:T(8,128)S(1)} %slice.1168), channel_id=1, source_target_pairs={{0,240},{16,0},{32,16},{48,32},{64,48},{80,64},{96,80},{112,96},{1... | collective-permute-start | bytes 111896 | tf_op jit(solution)/shard_map/ppermute | solution.py:17
  201.5 9.6 %collective-permute-start.16 = (f32[3,29,1,111]{3,2,1,0:T(1,128)S(1)}, f32[3,29,1,111]{3,2,1,0:T(1,128)S(1)}, u32[]{:S(2)}, u32[]{:S(2)}) collective-permute-start(f32[3,29,1,111]{3,2,1,0:T(1,128)S(1)} %slice.1184), channel_id=1, source_target_pairs={{0,1},{1,2},{2,3},{3,4},{4,5},{5,6},{6,7},{7,8},{8,9},{9,10},{10,1... | collective-permute-start | bytes 115892 | tf_op jit(solution)/shard_map/ppermute | solution.py:17
  213.9 8.3 %collective-permute-start.17 = (f32[3,1,28,111]{3,2,1,0:T(8,128)S(1)}, f32[3,1,28,111]{3,2,1,0:T(8,128)S(1)}, u32[]{:S(2)}, u32[]{:S(2)}) collective-permute-start(f32[3,1,28,111]{3,2,1,0:T(8,128)S(1)} %slice.1187), channel_id=1, source_target_pairs={{0,16},{16,32},{32,48},{48,64},{64,80},{80,96},{96,112},{112,128},... | collective-permute-start | bytes 111896 | tf_op jit(solution)/shard_map/ppermute | solution.py:17
  224.0 4.1 %collective-permute-start.18 = (f32[3,1,28,111]{3,2,1,0:T(8,128)S(1)}, f32[3,1,28,111]{3,2,1,0:T(8,128)S(1)}, u32[]{:S(2)}, u32[]{:S(2)}) collective-permute-start(f32[3,1,28,111]{3,2,1,0:T(8,128)S(1)} %slice.1188), channel_id=1, source_target_pairs={{0,240},{16,0},{32,16},{48,32},{64,48},{80,64},{96,80},{112,96},{1... | collective-permute-start | bytes 111896 | tf_op jit(solution)/shard_map/ppermute | solution.py:17
  249.3 9.7 %collective-permute-start.20 = (f32[3,29,1,111]{3,2,1,0:T(1,128)S(1)}, f32[3,29,1,111]{3,2,1,0:T(1,128)S(1)}, u32[]{:S(2)}, u32[]{:S(2)}) collective-permute-start(f32[3,29,1,111]{3,2,1,0:T(1,128)S(1)} %slice.1204), channel_id=1, source_target_pairs={{0,1},{1,2},{2,3},{3,4},{4,5},{5,6},{6,7},{7,8},{8,9},{9,10},{10,1... | collective-permute-start | bytes 115892 | tf_op jit(solution)/shard_map/ppermute | solution.py:17
  261.7 8.0 %collective-permute-start.21 = (f32[3,1,28,111]{3,2,1,0:T(8,128)S(1)}, f32[3,1,28,111]{3,2,1,0:T(8,128)S(1)}, u32[]{:S(2)}, u32[]{:S(2)}) collective-permute-start(f32[3,1,28,111]{3,2,1,0:T(8,128)S(1)} %slice.1207), channel_id=1, source_target_pairs={{0,16},{16,32},{32,48},{48,64},{64,80},{80,96},{96,112},{112,128},... | collective-permute-start | bytes 111896 | tf_op jit(solution)/shard_map/ppermute | solution.py:17
  271.8 4.1 %collective-permute-start.22 = (f32[3,1,28,111]{3,2,1,0:T(8,128)S(1)}, f32[3,1,28,111]{3,2,1,0:T(8,128)S(1)}, u32[]{:S(2)}, u32[]{:S(2)}) collective-permute-start(f32[3,1,28,111]{3,2,1,0:T(8,128)S(1)} %slice.1208), channel_id=1, source_target_pairs={{0,240},{16,0},{32,16},{48,32},{64,48},{80,64},{96,80},{112,96},{1... | collective-permute-start | bytes 111896 | tf_op jit(solution)/shard_map/ppermute | solution.py:17
  297.2 9.6 %collective-permute-start.24 = (f32[3,29,1,111]{3,2,1,0:T(1,128)S(1)}, f32[3,29,1,111]{3,2,1,0:T(1,128)S(1)}, u32[]{:S(2)}, u32[]{:S(2)}) collective-permute-start(f32[3,29,1,111]{3,2,1,0:T(1,128)S(1)} %slice.1224), channel_id=1, source_target_pairs={{0,1},{1,2},{2,3},{3,4},{4,5},{5,6},{6,7},{7,8},{8,9},{9,10},{10,1... | collective-permute-start | bytes 115892 | tf_op jit(solution)/shard_map/ppermute | solution.py:17
  309.6 8.0 %collective-permute-start.25 = (f32[3,1,28,111]{3,2,1,0:T(8,128)S(1)}, f32[3,1,28,111]{3,2,1,0:T(8,128)S(1)}, u32[]{:S(2)}, u32[]{:S(2)}) collective-permute-start(f32[3,1,28,111]{3,2,1,0:T(8,128)S(1)} %slice.1227), channel_id=1, source_target_pairs={{0,16},{16,32},{32,48},{48,64},{64,80},{80,96},{96,112},{112,128},... | collective-permute-start | bytes 111896 | tf_op jit(solution)/shard_map/ppermute | solution.py:17
  320.8 4.2 %collective-permute-start.26 = (f32[3,1,28,111]{3,2,1,0:T(8,128)S(1)}, f32[3,1,28,111]{3,2,1,0:T(8,128)S(1)}, u32[]{:S(2)}, u32[]{:S(2)}) collective-permute-start(f32[3,1,28,111]{3,2,1,0:T(8,128)S(1)} %slice.1228), channel_id=1, source_target_pairs={{0,240},{16,0},{32,16},{48,32},{64,48},{80,64},{96,80},{112,96},{1... | collective-permute-start | bytes 111896 | tf_op jit(solution)/shard_map/ppermute | solution.py:17
  346.2 9.6 %collective-permute-start.28 = (f32[3,29,1,111]{3,2,1,0:T(1,128)S(1)}, f32[3,29,1,111]{3,2,1,0:T(1,128)S(1)}, u32[]{:S(2)}, u32[]{:S(2)}) collective-permute-start(f32[3,29,1,111]{3,2,1,0:T(1,128)S(1)} %slice.1244), channel_id=1, source_target_pairs={{0,1},{1,2},{2,3},{3,4},{4,5},{5,6},{6,7},{7,8},{8,9},{9,10},{10,1... | collective-permute-start | bytes 115892 | tf_op jit(solution)/shard_map/ppermute | solution.py:17
  358.6 8.0 %collective-permute-start.29 = (f32[3,1,28,111]{3,2,1,0:T(8,128)S(1)}, f32[3,1,28,111]{3,2,1,0:T(8,128)S(1)}, u32[]{:S(2)}, u32[]{:S(2)}) collective-permute-start(f32[3,1,28,111]{3,2,1,0:T(8,128)S(1)} %slice.1247), channel_id=1, source_target_pairs={{0,16},{16,32},{32,48},{48,64},{64,80},{80,96},{96,112},{112,128},... | collective-permute-start | bytes 111896 | tf_op jit(solution)/shard_map/ppermute | solution.py:17
  (57 other events, 343.4 us)
where the time goes:
time: 380 us; the launch traced here: 373 us
  waiting for transfers between devices  129 us (34%)
  matrix products  90.9 us (24%)
  local copies, waits for them, and re-layouts  80.8 us (21%)
  other arithmetic  39.8 us (10%)
  starting transfers between devices  27.3 us (7%)
  between operations  5.14 us (1%)
    ppermute x30, waiting for transfers between devices, from_behind(): lax.ppermute(value, axis, [(i, (i + by) % size) for i in range(size)])  129 us
    ppermute x30, starting transfers between devices, from_behind(): lax.ppermute(value, axis, [(i, (i + by) % size) for i in range(size)])  27.3 us
    dot_general x14, matrix products, along_z(): return jnp.matmul(pieces, matrix, precision=highest).reshape(layout)  20.2 us
    dot_general x7, matrix products, element_forces(): jnp.einsum('pi,cxpyjz->cxiyjz', derivative, stress[0], precision=highest)  15.8 us
    scatter-add x8, local copies, waits for them, and re-layouts, return_sums(): part_y = partial_value[:, :, :width_y].at[:, :, :1].add(from_y)  15.2 us
    dot_general x7, matrix products, element_forces(): jnp.einsum('pj,cxiypz->cxiyjz', derivative, stress[1], precision=highest)  12.5 us
    slice x8, local copies, waits for them, and re-layouts, return_sums(): return part_y[:, :width_x].at[:, :1].add(from_x)  12.4 us
    dot_general x7, matrix products, element_forces(): jnp.einsum('pj,cxiyjz->cxiypz', derivative, element_vals, precision=highest)  11.1 us
  transfers between devices with their start and end apart: 30, of which 27 were waited for; matrix products, arithmetic and copies ran while one was open for 14% of the time, Pallas kernels for 0%

commit v1 on v0

v1 whole, which is shorter than its diff:
```python
import jax
import jax.numpy as jnp
import numpy as np
from jax import lax
from jax.experimental import pallas as pl
from jax.experimental.pallas import tpu as pltpu
from jax.sharding import PartitionSpec as P

DEG = 7
N = DEG + 1
SWEEPS = 2
CHEB = 3
F32 = jnp.float32
BF16 = jnp.bfloat16
highest = lax.Precision.HIGHEST


def legendre_pair(points, degree):
    prev_poly = points * 0.0 + 1.0
    this_poly = points * 1.0
    for order in range(2, degree + 1):
        next_poly = ((2 * order - 1) * points * this_poly - (order - 1) * prev_poly) / order
        prev_poly = this_poly
        this_poly = next_poly
    return (this_poly, prev_poly)


def gll_tables(degree):
    count = degree + 1
    points = -np.cos(np.pi * np.arange(count) / degree)
    for newton_step in range(60):
        this_poly, prev_poly = legendre_pair(points, degree)
        points = points - (points * this_poly - prev_poly) / (count * this_poly)
    values, unused_poly = legendre_pair(points, degree)
    weights = 2.0 / (degree * (degree + 1) * values**2)
    identity_np = np.eye(count)
    spacing = points[:, None] - points[None, :] + identity_np
    derivative = values[:, None] / (values[None, :] * spacing) * (1.0 - identity_np)
    derivative[0, 0] = -degree * (degree + 1) / 4.0
    derivative[degree, degree] = degree * (degree + 1) / 4.0
    stiff_ratio = (weights[:, None] * derivative**2).sum(0) / weights
    return (weights, derivative, stiff_ratio)


WEIGHTS, DERIV, RATIO = gll_tables(DEG)


def halves(matrix):
    high = matrix.astype(BF16).astype(np.float32)
    low = matrix.astype(np.float32) - high
    return high, low


def z_matrices(blocks):
    width = blocks * N
    node = np.array([DEG * f + k for f in range(blocks) for k in range(N)])
    free = (node > 0) & (node < DEG * blocks)
    share = ((node[:, None] == node[None, :]) & free[:, None] & free[None, :]).astype(np.float64)
    grad = np.kron(np.eye(blocks), DERIV.T)
    back = np.kron(np.eye(blocks), DERIV) @ share
    zero = np.zeros((width, width))
    grad_hi, grad_lo = halves(grad)
    back_hi, back_lo = halves(back)
    w_grad = np.block([[grad_hi, grad_lo], [grad_hi, zero]])
    w_back = np.block([[back_hi, back_lo], [back_hi, zero]])
    w_share = np.concatenate([share, share], 0)
    return w_grad, w_back, w_share


def line_sums(vals, matrix):
    even = [vals[i] + vals[DEG - i] for i in range(N // 2)]
    odd = [vals[i] - vals[DEG - i] for i in range(N // 2)]
    outs = [None] * N
    for p in range(N // 2):
        from_even = None
        from_odd = None
        for i in range(N // 2):
            ce = float(np.float32((matrix[p, i] + matrix[p, DEG - i]) / 2.0))
            co = float(np.float32((matrix[p, i] - matrix[p, DEG - i]) / 2.0))
            te = ce * even[i]
            to = co * odd[i]
            from_even = te if from_even is None else from_even + te
            from_odd = to if from_odd is None else from_odd + to
        outs[p] = from_odd + from_even
        outs[DEG - p] = from_odd - from_even
    return outs


def split_pair(value):
    high = value.astype(BF16)
    low = (value - high.astype(F32)).astype(BF16)
    return jnp.concatenate([high, low], axis=-1)


def dot(a, b):
    return jnp.dot(a, b, preferred_element_type=F32)


ROWS = 8
SIDE = 4
ORDER = (0, 3, 1, 2)
UNROLL = 2


def flip(value):
    return jnp.concatenate([value[SIDE:], value[:SIDE]], 0)


def received(par_ref, axis, even_ref, odd_ref, *at):
    is_even = par_ref[axis] == 0
    even = even_ref[at]
    odd = odd_ref[at]
    return jnp.where(is_even, even, odd), jnp.where(is_even, odd, even)


def sum_x(par_ref, xe_ref, xo_ref, parts, c, face_at, i, j, tile):
    total = parts[tile][c, i, j]
    if 0 < i < DEG:
        return total
    row = lax.broadcasted_iota(jnp.int32, (ROWS, 128), 0)
    across = DEG - i
    if tile == 0:
        right, left = received(par_ref, 0, xe_ref, xo_ref, face_at, j)
        face = right if i else left
        face = jnp.concatenate([face, face], 0)
        inner = parts[1][c, across, j]
        low, high = (inner, face) if i else (face, inner)
    else:
        middle = flip(parts[1][c, across, j])
        outer = parts[0][c, across, j]
        low, high = (middle, outer) if i else (outer, middle)
    return total + jnp.where(row < SIDE, low, high)


def sum_all(par_ref, faces, parts, c, face_at, i, j, tile, edge):
    xe, xo, ye, yo = faces
    total = sum_x(par_ref, xe, xo, parts, c, face_at, i, j, tile)
    if edge is not None:
        row = lax.broadcasted_iota(jnp.int32, (ROWS, 128), 0)
        top, bottom = received(par_ref, 1, ye, yo, face_at, i)
        face = top if edge else bottom
        at = SIDE - 1 if edge else 0
        first = jnp.broadcast_to(face[2 * tile : 2 * tile + 1], (ROWS, 128))
        second = jnp.broadcast_to(face[2 * tile + 1 : 2 * tile + 2], (ROWS, 128))
        total = total + jnp.where(row == at, first, jnp.where(row == SIDE + at, second, 0.0))
    return total


def over_planes(body):
    body(0, 0)

    def inner(j, carry):
        body(j, None)
        return carry

    lax.fori_loop(1, DEG, inner, 0, unroll=UNROLL)
    body(DEG, 1)


def loop(count, body, unroll=UNROLL):
    def inner(i, carry):
        body(i)
        return carry

    lax.fori_loop(0, count, inner, 0, unroll=unroll)


def gradients(planes, j, wg_ref, gx_ref, gz_ref):
    flat = jnp.concatenate([planes[c][i] for c in range(3) for i in range(N)], 0)
    both = dot(split_pair(flat), wg_ref[...])
    for c in range(3):
        outs = line_sums(planes[c], DERIV)
        for i in range(N):
            gx_ref[c, i, j] = outs[i]
    both = (both[:, :128] + both[:, 128:]).reshape(3, N, ROWS, 128)
    for c in range(3):
        for i in range(N):
            gz_ref[c, i, j] = both[c, i]


def finish(par_ref, u_ref, lam_ref, mu_ref, wb_ref, ws_ref, au_ref, gx_ref, gz_ref, fy_ref):
    def stress(i):
        gy = [line_sums([u_ref[c, i, j] for j in range(N)], DERIV) for c in range(3)]
        sy = [[None] * N for c in range(3)]
        sz = [[None] * N for c in range(3)]
        for j in range(N):
            gx = [gx_ref[c, i, j] for c in range(3)]
            gz = [gz_ref[c, i, j] for c in range(3)]
            mu = mu_ref[i, j]
            mu2 = mu + mu
            trace = lam_ref[i, j] * (gx[0] + gy[1][j] + gz[2])
            sxy = mu * (gx[1] + gy[0][j])
            sxz = mu * (gx[2] + gz[0])
            syz = mu * (gy[2][j] + gz[1])
            gx_ref[0, i, j] = mu2 * gx[0] + trace
            gx_ref[1, i, j] = sxy
            gx_ref[2, i, j] = sxz
            sz[0][j] = sxz
            sz[1][j] = syz
            sz[2][j] = mu2 * gz[2] + trace
            sy[0][j] = sxy
            sy[1][j] = mu2 * gy[1][j] + trace
            sy[2][j] = syz
        flat = jnp.concatenate([sz[c][j] for c in range(3) for j in range(N)], 0)
        both = dot(split_pair(flat), wb_ref[...])
        for c in range(3):
            outs = line_sums(sy[c], DERIV.T)
            for j in range(N):
                fy_ref[c, i, j] = outs[j]
        both = (both[:, :128] + both[:, 128:]).reshape(3, N, ROWS, 128)
        for c in range(3):
            gz_ref[c, i] = both[c]

    loop(N, stress)

    def back(j):
        flat = []
        for c in range(3):
            outs = line_sums([gx_ref[c, i, j] for i in range(N)], DERIV.T)
            flat += [outs[i] + fy_ref[c, i, j] for i in range(N)]
        both = dot(split_pair(jnp.concatenate(flat, 0)), ws_ref[...]).reshape(3, N, ROWS, 128)
        for c in range(3):
            for i in range(N):
                au_ref[c, i, j] = both[c, i] + gz_ref[c, i, j]

    loop(N, back)


def assemble(par_ref, part_ref, first, face_refs):
    row = lax.broadcasted_iota(jnp.int32, (ROWS, 128), 0)
    near = row % SIDE

    def along_y(i):
        for c in range(3):
            last = part_ref[c, i, DEG]
            start = part_ref[c, i, 0]
            last = last + jnp.where(near < SIDE - 1, jnp.concatenate([start[1:], start[:1]], 0), 0.0)
            start = jnp.where(near > 0, jnp.concatenate([last[-1:], last[:-1]], 0), start)
            part_ref[c, i, DEG] = last
            part_ref[c, i, 0] = start

    loop(N, along_y)
    if not face_refs:
        return
    xe_ref, xo_ref = face_refs
    is_even = par_ref[0] == 0

    def x_faces(j):
        for c in range(3):
            right = part_ref[c, DEG, j][SIDE:]
            left = part_ref[c, 0, j][:SIDE]
            xe_ref[first + c, j] = jnp.where(is_even, right, left)
            xo_ref[first + c, j] = jnp.where(is_even, left, right)

    loop(N, x_faces)


def first_kernel(tile, par_ref, ratio_ref, u_ref, lam_ref, mu_ref, rk_ref, wg_ref, wb_ref, ws_ref, au_ref, dg_ref, *refs):
    face_refs, work = refs[:-3], refs[-3:]
    gx_ref, gz_ref, fy_ref = work

    def diagonal(i):
        rows = [[None] * N for c in range(3)]
        for j in range(N):
            lam = lam_ref[i, j]
            mu = mu_ref[i, j]
            rk = rk_ref[...]
            total = rk + (ratio_ref[i] + float(RATIO[j]))
            for c in range(3):
                own = (ratio_ref[i], float(RATIO[j]), rk)[c]
                rows[c][j] = lam * own + mu * (total + own)
        flat = jnp.concatenate([rows[c][j] for c in range(3) for j in range(N)], 0)
        both = dot(split_pair(flat), ws_ref[...]).reshape(3, N, ROWS, 128)
        for c in range(3):
            dg_ref[c, i] = both[c]

    loop(N, diagonal)

    def start(j):
        planes = [[u_ref[c, i, j] for i in range(N)] for c in range(3)]
        gradients(planes, j, wg_ref, gx_ref, gz_ref)

    loop(N, start)
    finish(par_ref, u_ref, lam_ref, mu_ref, wb_ref, ws_ref, au_ref, gx_ref, gz_ref, fy_ref)
    assemble(par_ref, au_ref, 0, face_refs)
    assemble(par_ref, dg_ref, 3, face_refs)


def corner_kernel(par_ref, xe_ref, xo_ref, *refs):
    fields = [refs[k : k + 2] for k in range(0, len(refs) - 2, 2)]
    ye_ref, yo_ref = refs[-2:]
    is_even = par_ref[1] == 0
    for n, parts in enumerate(fields):
        for c in range(3):
            at = 3 * n + c
            for i in range(N):
                rows_t = []
                rows_b = []
                for tile in range(2):
                    top = sum_x(par_ref, xe_ref, xo_ref, parts, c, at, i, DEG, tile)
                    bottom = sum_x(par_ref, xe_ref, xo_ref, parts, c, at, i, 0, tile)
                    rows_t += [top[SIDE - 1 : SIDE], top[-1:]]
                    rows_b += [bottom[:1], bottom[SIDE : SIDE + 1]]
                top = jnp.concatenate(rows_t, 0)
                bottom = jnp.concatenate(rows_b, 0)
                ye_ref[at, i] = jnp.where(is_even, top, bottom)
                yo_ref[at, i] = jnp.where(is_even, bottom, top)


def step_kernel(tile, stage, with_diag, *refs):
    restart = stage == 0
    refs = list(refs)
    take = lambda count: [refs.pop(0) for _ in range(count)]
    par_ref, coef_ref, u_ref, b_ref = take(4)
    parts = take(2)
    faces = take(4)
    inv_refs = take(2 if with_diag else 1)
    change_ref = None if restart else refs.pop(0)
    lam_ref, mu_ref, wg_ref, wb_ref, ws_ref = take(5)
    u_out, change_out, au_ref = take(3)
    inv_out = refs.pop(0) if with_diag else None
    face_refs = take(2) if tile == 0 else []
    gx_ref, gz_ref, fy_ref = refs
    lane = lax.broadcasted_iota(jnp.int32, (ROWS, 128), 1)
    clamped = (lane == 0) | (lane == 127)

    def update(j, edge):
        keep = coef_ref[2 * stage]
        gain = coef_ref[2 * stage + 1]
        planes = [[None] * N for c in range(3)]
        for c in range(3):
            for i in range(N):
                if with_diag:
                    diag = sum_all(par_ref, faces, inv_refs, c, 3 + c, i, j, tile, edge)
                    inv = jnp.where(clamped, 0.0, 1.0 / jnp.where(clamped, 1.0, diag))
                    inv_out[c, i, j] = inv
                else:
                    inv = inv_refs[0][c, i, j]
                residual = b_ref[c, i, j] - sum_all(par_ref, faces, parts, c, c, i, j, tile, edge)
                change = gain * (inv * residual)
                if not restart:
                    change = keep * change_ref[c, i, j] + change
                change_out[c, i, j] = change
                planes[c][i] = u_ref[c, i, j] + change
                u_out[c, i, j] = planes[c][i]
        gradients(planes, j, wg_ref, gx_ref, gz_ref)

    over_planes(update)
    finish(par_ref, u_out, lam_ref, mu_ref, wb_ref, ws_ref, au_ref, gx_ref, gz_ref, fy_ref)
    assemble(par_ref, au_ref, 0, face_refs)


def last_kernel(par_ref, *refs):
    b_refs, parts, faces, res_refs = refs[:2], refs[2:4], refs[4:8], refs[8:]

    def update(j, edge):
        for tile in range(2):
            for c in range(3):
                for i in range(N):
                    total = sum_all(par_ref, faces, parts, c, c, i, j, tile, edge)
                    res_refs[tile][c, i, j] = b_refs[tile][c, i, j] - total

    over_planes(update)


def lane_pick(value, index):
    return jnp.take_along_axis(value, index, axis=1, mode="promise_in_bounds")


TILES = ((0, 8), (8, 16), (16, 24), (20, 28))


def load_kernel(par_ref, coef_ref, in_ref, t0_ref, t1_ref, xl_ref, yb_ref, work_ref):
    nodes_x, width = in_ref.shape[1], in_ref.shape[2]
    nodes_z = width // nodes_x
    outs = (t0_ref, t1_ref)
    lane = lax.broadcasted_iota(jnp.int32, (ROWS, 128), 1)
    node = DEG * (lane // N) + lane % N - 1
    free = (node >= 0) & (node < nodes_z)
    node = jnp.clip(node, 0, nodes_z - 1)
    zero = jnp.zeros((ROWS, 128), F32)
    for r in range(4):
        work_ref[nodes_x, pl.ds(8 * r, 8)] = zero

    def component(c, carry):
        for y in range(nodes_x):
            tile, shift = divmod(nodes_z * y, 128)
            at = node + shift
            begin = 128 * tile
            work_ref[y, pl.ds(24, 8)] = zero
            for low, high in TILES:
                here = in_ref[c, low:high, begin : begin + 128]
                got = lane_pick(here, at & 127)
                if shift + nodes_z > 128:
                    stop = min(begin + 256, width)
                    there = in_ref[c, low:high, begin + 128 : stop]
                    if stop < begin + 256:
                        there = jnp.concatenate([there, jnp.zeros((ROWS, begin + 256 - stop), F32)], 1)
                    got = jnp.where(at < 128, got, lane_pick(there, at & 127))
                work_ref[y, low:high] = jnp.where(free, got, 0.0)
        out_c = jnp.where(c == 2, 2, 1 - c)
        for i in range(N):
            for j in range(N):
                for which in range(2):
                    rows = [work_ref[DEG * ORDER[2 * which + k] + i, pl.ds(j, SIDE, stride=DEG)] for k in range(2)]
                    value = jnp.concatenate(rows, 0)
                    outs[which][out_c, i, j] = value
                    if j == 0:
                        yb_ref[out_c, i, pl.ds(2 * which, 1)] = value[:1]
                        yb_ref[out_c, i, pl.ds(2 * which + 1, 1)] = value[SIDE : SIDE + 1]
                    if i == 0 and which == 0:
                        xl_ref[out_c, j] = value[:SIDE]
        return carry

    lax.fori_loop(0, 3, component, 0)


def coeff_kernel(par_ref, coef_ref, lame_ref, material_ref, wz_ref, *outs):
    lane = lax.broadcasted_iota(jnp.int32, (ROWS, 128), 1)
    weight_z = wz_ref[...]
    for which in range(2):
        rows = [material_ref[b, ORDER[2 * which + k]][None] for k in range(2) for b in range(SIDE)]
        kind = jnp.concatenate(rows, 0).astype(F32)
        kind = jnp.concatenate([kind, jnp.zeros((ROWS, 128 - kind.shape[1]), F32)], 1)
        kind = lane_pick(kind, lane // N)
        for part in range(2):
            value = jnp.zeros((ROWS, 128), F32)
            for label in range(lame_ref.shape[1]):
                value = jnp.where(kind == float(label), lame_ref[part, label], value)
            value = value * weight_z
            for i in range(N):
                for j in range(N):
                    outs[2 * which + part][i, j] = value * float(WEIGHTS[i] * WEIGHTS[j])


def halo_corner_kernel(xr_ref, yb_ref, out_ref):
    row = lax.broadcasted_iota(jnp.int32, (SIDE, 128), 0)
    for n in range(6):
        for i in range(N):
            value = yb_ref[n, i]
            if i == DEG:
                value = jnp.where(row == 1, jnp.broadcast_to(xr_ref[n, 0][:1], (SIDE, 128)), value)
            out_ref[n, i] = value


def halo_kernel(xr_ref, yr_ref, *refs):
    fields, outs = refs[:4], refs[4:]
    row = lax.broadcasted_iota(jnp.int32, (ROWS, 128), 0)
    for n in range(2):
        for tile in range(2):
            src, dst = fields[2 * n + tile], outs[2 * n + tile]

            def plane(j, edge):
                for c in range(3):
                    for i in range(N):
                        value = src[c, i, j]
                        if tile == 0 and i == DEG:
                            face = xr_ref[3 * n + c, j]
                            value = jnp.where(row < SIDE, value, jnp.concatenate([face, face], 0))
                        if edge == 1:
                            face = yr_ref[3 * n + c, i]
                            first = jnp.broadcast_to(face[2 * tile : 2 * tile + 1], (ROWS, 128))
                            second = jnp.broadcast_to(face[2 * tile + 1 : 2 * tile + 2], (ROWS, 128))
                            value = jnp.where(row == SIDE - 1, first, jnp.where(row == ROWS - 1, second, value))
                        dst[c, i, j] = value

            over_planes(plane)


def store_kernel(t0_ref, t1_ref, out_ref, work_ref):
    nodes_x, width = out_ref.shape[1], out_ref.shape[2]
    nodes_z = width // nodes_x
    parts = (t0_ref, t1_ref)
    lane = lax.broadcasted_iota(jnp.int32, (ROWS, 128), 1)

    def component(c, carry):
        in_c = jnp.where(c == 2, 2, 1 - c)
        for i in range(DEG):
            for j in range(DEG):
                for which in range(2):
                    value = parts[which][in_c, i, j]
                    for k in range(2):
                        at = DEG * ORDER[2 * which + k] + i
                        work_ref[at, pl.ds(j, SIDE, stride=DEG)] = value[SIDE * k : SIDE * k + SIDE]
        for begin in range(0, width, 128):
            stop = min(begin + 128, width)
            for low, high in TILES:
                result = None
                for y in range(begin // nodes_z, (stop - 1) // nodes_z + 1):
                    node = jnp.clip(lane + (begin - nodes_z * y), 0, nodes_z - 1) + 1
                    got = lane_pick(work_ref[y, low:high], N * (node // DEG) + node % DEG)
                    result = got if result is None else jnp.where(lane + begin >= nodes_z * y, got, result)
                out_ref[c, low:high, begin:stop] = result[:, : stop - begin]
        return carry

    lax.fori_loop(0, 3, component, 0)


VM = pl.BlockSpec(memory_space=pltpu.VMEM)
SM = pl.BlockSpec(memory_space=pltpu.SMEM)
FIELD = (3, N, N, ROWS, 128)


def shape(dims):
    return jax.ShapeDtypeStruct(dims, F32)


def call(kernel, smem, inputs, outs, work=0, rows=FIELD):
    return pl.pallas_call(
        kernel,
        in_specs=[SM] * smem + [VM] * (len(inputs) - smem),
        out_specs=[VM] * len(outs),
        out_shape=[shape(dims) for dims in outs],
        scratch_shapes=[pltpu.VMEM(rows, F32)] * work,
        compiler_params=pltpu.CompilerParams(vmem_limit_bytes=6 << 20),
    )(*inputs)


def swaps(even, odd, axis):
    size = lax.axis_size(axis)
    got_odd = lax.ppermute(odd, axis, [(i, (((i + 1) ^ 1) - 1) % size) for i in range(size)])
    got_even = lax.ppermute(even, axis, [(i, i ^ 1) for i in range(size)])
    return got_even, got_odd


def exchange(par, x_faces, fields):
    xe, xo = swaps(*x_faces, "gy")
    ye, yo = call(corner_kernel, 1, (par, xe, xo, *fields), (xe.shape, xe.shape))
    ye, yo = swaps(ye, yo, "gx")
    return xe, xo, ye, yo


def from_next(value, axis):
    size = lax.axis_size(axis)
    return lax.ppermute(value, axis, [(i, (i - 1) % size) for i in range(size)])


def local(right_side, guess, material, lame, upper, lower_ratio):
    elems_x, elems_y, elems_z = material.shape
    nodes_y = DEG * elems_y
    w_grad, w_back, w_share = z_matrices(elems_z)
    w_grad = jnp.asarray(w_grad, BF16)
    w_back = jnp.asarray(w_back, BF16)
    w_share = jnp.asarray(w_share, BF16)
    par = jnp.stack([lax.axis_index("gy") % 2, lax.axis_index("gx") % 2]).astype(jnp.int32)

    upper_edge = upper[0]
    lower_edge = lower_ratio[0] * upper_edge
    center = (upper_edge + lower_edge) / 2.0
    radius = (upper_edge - lower_edge) / 2.0
    sigma_ratio = center / radius
    pairs = [(jnp.zeros((), F32), 1.0 / center)]
    factor = 1.0 / sigma_ratio
    for step_index in range(CHEB - 1):
        factor_next = 1.0 / (2.0 * sigma_ratio - factor)
        pairs.append((factor_next * factor, 2.0 * factor_next / radius))
        factor = factor_next
    coef = jnp.stack([value for pair in pairs for value in pair]).astype(F32)
    grid = (N, N, ROWS, 128)
    weight_z = jnp.asarray(np.tile(WEIGHTS, (ROWS, elems_z)), F32)
    coeffs = call(coeff_kernel, 3, (par, coef, lame, material, weight_z), (grid,) * 4)
    coeffs = [coeffs[:2], coeffs[2:]]

    plane = (3, N, SIDE, 128)
    staged = (nodes_y + 1, nodes_y + SIDE, 128)
    loads = [call(load_kernel, 2, (par, coef, value), (FIELD, FIELD, plane, plane), 1, staged) for value in (guess, right_side)]
    x_halo = from_next(jnp.concatenate([load[2] for load in loads], 0), "gy")
    y_halo = jnp.concatenate([load[3] for load in loads], 0)
    (y_halo,) = call(halo_corner_kernel, 0, (x_halo, y_halo), (y_halo.shape,))
    y_halo = from_next(y_halo, "gx")
    u0, u1, b0, b1 = call(halo_kernel, 0, (x_halo, y_halo, *loads[0][:2], *loads[1][:2]), (FIELD,) * 4)
    u, b = [u0, u1], [b0, b1]

    ratio_z = jnp.asarray(np.tile(RATIO, (ROWS, elems_z)), F32)

    weights = (w_grad, w_back, w_share)
    au = [None, None]
    diag = [None, None]
    for tile in range(2):
        lam_w, mu_w = coeffs[tile][0], coeffs[tile][1]
        faces = ((6, N, SIDE, 128),) * (0 if tile else 2)
        au[tile], diag[tile], *got_faces = call(
            lambda *refs, tile=tile: first_kernel(tile, *refs), 2,
            (par, jnp.asarray(RATIO, F32), u[tile], lam_w, mu_w, ratio_z, *weights), (FIELD, FIELD) + faces, 3,
        )
        x_faces = x_faces if tile else got_faces
    fields = (*au, *diag)
    change = [None, None]
    inv = [None, None]
    for count in range(SWEEPS * CHEB):
        got = exchange(par, x_faces, fields)
        stage = count % CHEB
        with_diag = count == 0
        old_au, au = au, [None, None]
        for tile in range(2):
            lam_w, mu_w = coeffs[tile][0], coeffs[tile][1]
            inputs = (par, coef, u[tile], b[tile], *old_au, *got)
            inputs += tuple(diag) if with_diag else (inv[tile],)
            inputs += () if stage == 0 else (change[tile],)
            inputs += (lam_w, mu_w, *weights)
            outs = (FIELD, FIELD, FIELD) + ((FIELD,) if with_diag else ())
            outs += () if tile else ((3, N, SIDE, 128),) * 2

            def kernel(*refs, flags=(tile, stage, with_diag)):
                step_kernel(*flags, *refs)

            results = list(call(kernel, 2, inputs, outs, 3))
            u[tile], change[tile], au[tile] = results[:3]
            if with_diag:
                inv[tile] = results[3]
            if tile == 0:
                x_faces = results[-2:]
        fields = au
    got = exchange(par, x_faces, fields)
    residual = call(last_kernel, 1, (par, *b, *au, *got), (FIELD, FIELD))

    def to_nodes(field):
        return call(store_kernel, 0, tuple(field), (guess.shape,), 1, staged)[0]

    return (to_nodes(u), to_nodes(residual))


def solution(mesh):
    placed = (P(None, "gx", "gy"), P(None, "gx", "gy"), P("gx", "gy", None), P(), P(), P())
    return jax.shard_map(
        local,
        mesh=mesh,
        in_specs=placed,
        out_specs=(P(None, "gx", "gy"), P(None, "gx", "gy")),
        check_vma=False,
    )
```

time: 380 us -> 193 us (0.51); the launches traced: 373 us -> 193 us
  matrix products: 90.9 us -> 0 us
  waiting for transfers between devices: 129 us -> 39.2 us
  local copies, waits for them, and re-layouts: 80.8 us -> 2 us
  Pallas kernels: 0 us -> 76.4 us
  starting transfers between devices: 27.3 us -> 72.5 us
  other arithmetic: 39.8 us -> 0.13 us
    dot_general x58 -> x0, matrix products: 90.9 us -> none  [the longest x14 20.2 us: along_z(): return jnp.matmul(pieces, matrix, precision=highest).reshape(layout)]
    ppermute x30, waiting for transfers between devices: 129 us -> 39.2 us  [the longest x14 34.8 us: swaps(): lax.ppermute(odd, axis, [(i, ((i + 1 ^ 1) - 1) % size) for i in range(siz...]
    pallas_call x0 -> x29, Pallas kernels: none -> 76.4 us  [call(): pl.pallas_call(kernel, in_specs=[SM] * smem + [VM] * (len(inputs) - smem)...]
    ppermute x30, starting transfers between devices: 27.3 us -> 72.5 us  [the longest x14 60.3 us: swaps(): lax.ppermute(odd, axis, [(i, ((i + 1 ^ 1) - 1) % size) for i in range(siz...]
    slice x63 -> x0, local copies, waits for them, and re-layouts: 27.1 us -> none  [the longest x8 12.4 us: return_sums(): return part_y[:, :width_x].at[:, :1].add(from_x)]
    add x40 -> x0, other arithmetic: 22.5 us -> none  [the longest x7 8.4 us: element_forces(): mu_w * (gradients + jnp.swapaxes(gradients, 0, 1))]
    reshape x11 -> x0, local copies, waits for them, and re-layouts: 17.7 us -> none  [the longest x7 6.01 us: split_open(): leading.reshape(layout[:dim_index] + (blocks, DEG) + layout[dim_index + 1:])]
    scatter-add x8 -> x0, local copies, waits for them, and re-layouts: 15.2 us -> none  [return_sums(): part_y = partial_value[:, :, :width_y].at[:, :, :1].add(from_y)]
  transfers between devices with their start and end apart: 30 -> 30, of which waited for: 27 -> 15; matrix products, arithmetic and copies ran while one was open for 14% -> 0% of each run, Pallas kernels for 0% -> 17%
where the time goes in v1:
time: 193 us
  Pallas kernels  76.4 us (40%)
  starting transfers between devices  72.5 us (38%)
  waiting for transfers between devices  39.2 us (20%)
  between operations  2.61 us (1%)
  local copies, waits for them, and re-layouts  2 us (1%)
    pallas_call x29, Pallas kernels, call(): pl.pallas_call(kernel, in_specs=[SM] * smem + [VM] * (len(inputs) - smem)...  76.4 us
    ppermute x14, starting transfers between devices, swaps(): lax.ppermute(odd, axis, [(i, ((i + 1 ^ 1) - 1) % size) for i in range(siz...  60.3 us
    ppermute x14, waiting for transfers between devices, swaps(): lax.ppermute(odd, axis, [(i, ((i + 1 ^ 1) - 1) % size) for i in range(siz...  34.8 us
    ppermute x2, starting transfers between devices, from_next(): return lax.ppermute(value, axis, [(i, (i - 1) % size) for i in range(size)])  11 us
    ppermute x2, waiting for transfers between devices, from_next(): return lax.ppermute(value, axis, [(i, (i - 1) % size) for i in range(size)])  4.37 us
  transfers between devices with their start and end apart: 30, of which 15 were waited for; matrix products, arithmetic and copies ran while one was open for 0% of the time, Pallas kernels for 17%

profile of v1, /device:TPU:0, one launch (start us, length us, event | category | flops | bytes accessed | tf_op | source)
XLA Modules:
  0.0 192.9 jit_solution(4123387854021338)
XLA Ops:
  7.4 7.4 %collective-permute-start = (f32[6,8,4,128]{3,2,1,0:T(4,128)S(1)}, f32[6,8,4,128]{3,2,1,0:T(4,128)S(1)}, u32[]{:S(2)}, u32[]{:S(2)}) collective-permute-start(f32[6,8,4,128]{3,2,1,0:T(4,128)S(1)} %pad_maximum_fusion), channel_id=1, source_target_pairs={{0,15},{1,0},{2,1},{3,2},{4,3},{5,4},{6,5},{7,6},{8,7},{9,8},{10,9... | collective-permute-start | bytes 294920 | tf_op jit(solution)/shard_map/ppermute | solution.py:535
  24.5 4.5 %shard_map.145 = (f32[3,8,8,8,128]{4,3,2,1,0:T(8,128)S(1)}, f32[3,8,8,8,128]{4,3,2,1,0:T(8,128)S(1)}, f32[6,8,4,128]{3,2,1,0:T(4,128)S(1)}, f32[6,8,4,128]{3,2,1,0:T(4,128)S(1)}) custom-call(s32[2]{0:T(128)S(1)} %pad_add_fusion.par_ref.refs_0_, f32[8]{0:T(128)S(1)} %copy-done.8, f32[3,8,8,8,128]{4,3,2,1,0:T(8,128)S(1)} %get-tuple-element.94.refs_2_, ...), custom_call_target="tpu_custom_call" | custom-call | tf_op jit(solution)/shard_map/pallas_call | solution.py:509
  29.1 7.2 %collective-permute-start.3 = (f32[6,8,4,128]{3,2,1,0:T(4,128)S(1)}, f32[6,8,4,128]{3,2,1,0:T(4,128)S(1)}, u32[]{:S(2)}, u32[]{:S(2)}) collective-permute-start(f32[6,8,4,128]{3,2,1,0:T(4,128)S(1)} %get-tuple-element.104), channel_id=1, source_target_pairs={{0,15},{1,2},{2,1},{3,4},{4,3},{5,6},{6,5},{7,8},{8,7},{9,10},{10,... | collective-permute-start | bytes 294920 | tf_op jit(solution)/shard_map/ppermute | solution.py:521
  36.3 4.5 %shard_map.146 = (f32[3,8,8,8,128]{4,3,2,1,0:T(8,128)S(1)}, f32[3,8,8,8,128]{4,3,2,1,0:T(8,128)S(1)}) custom-call(s32[2]{0:T(128)S(1)} %pad_add_fusion.par_ref.refs_0_, f32[8]{0:T(128)S(1)} %copy-done.8, f32[3,8,8,8,128]{4,3,2,1,0:T(8,128)S(1)} %get-tuple-element.99.refs_2_, f32[8,8,8,128]{3,2,1,0:T(8,128)S(1)} %get-tuple-element.100.refs_3_.refs_12_.refs_11_, ...), custom_call_target="tpu_custom_call" | custom-call | tf_op jit(solution)/shard_map/pallas_call | solution.py:509
  41.5 6.1 %collective-permute-start.5 = (f32[6,8,4,128]{3,2,1,0:T(4,128)S(1)}, f32[6,8,4,128]{3,2,1,0:T(4,128)S(1)}, u32[]{:S(2)}, u32[]{:S(2)}) collective-permute-start(f32[6,8,4,128]{3,2,1,0:T(4,128)S(1)} %get-tuple-element.108), channel_id=1, source_target_pairs={{0,240},{16,32},{32,16},{48,64},{64,48},{80,96},{96,80},{112,128},... | collective-permute-start | bytes 294920 | tf_op jit(solution)/shard_map/ppermute | solution.py:521
  51.3 4.2 %shard_map.148 = (f32[3,8,8,8,128]{4,3,2,1,0:T(8,128)S(1)}, f32[3,8,8,8,128]{4,3,2,1,0:T(8,128)S(1)}, f32[3,8,8,8,128]{4,3,2,1,0:T(8,128)S(1)}, f32[3,8,8,8,128]...) custom-call(s32[2]{0:T(128)S(1)} %pad_add_fusion.par_ref.refs_0_, ...), custom_call_target="tpu_custom_call" | custom-call | tf_op jit(solution)/shard_map/pallas_call | solution.py:509
  55.5 5.2 %collective-permute-start.7 = (f32[3,8,4,128]{3,2,1,0:T(4,128)S(1)}, f32[3,8,4,128]{3,2,1,0:T(4,128)S(1)}, u32[]{:S(2)}, u32[]{:S(2)}) collective-permute-start(f32[3,8,4,128]{3,2,1,0:T(4,128)S(1)} %get-tuple-element.114), channel_id=1, source_target_pairs={{0,15},{1,2},{2,1},{3,4},{4,3},{5,6},{6,5},{7,8},{8,7},{9,10},{10,... | collective-permute-start | bytes 147464 | tf_op jit(solution)/shard_map/ppermute | solution.py:521
  60.7 4.1 %shard_map.149 = (f32[3,8,8,8,128]{4,3,2,1,0:T(8,128)S(1)}, f32[3,8,8,8,128]{4,3,2,1,0:T(8,128)S(1)}, f32[3,8,8,8,128]{4,3,2,1,0:T(8,128)S(1)}, f32[3,8,8,8,128]{4,3,2,1,0:T(8,128)S(1)}) custom-call(s32[2]{0:T(128)S(1)} %pad_add_fusion.par_ref.refs_0_, f32[6]{0:T(128)S(1)} %stack.35.coef_ref.refs_1_, f32[3,8,8,8,128]{4,3,2,1,0:T(8,128)S(1)} %get-tuple-element.99.refs_2_, ...), custom_call_target="tpu_custom_call" | custom-call | tf_op jit(solution)/shard_map/pallas_call | solution.py:509
  65.9 5.0 %collective-permute-start.9 = (f32[3,8,4,128]{3,2,1,0:T(4,128)S(1)}, f32[3,8,4,128]{3,2,1,0:T(4,128)S(1)}, u32[]{:S(2)}, u32[]{:S(2)}) collective-permute-start(f32[3,8,4,128]{3,2,1,0:T(4,128)S(1)} %get-tuple-element.116), channel_id=1, source_target_pairs={{0,240},{16,32},{32,16},{48,64},{64,48},{80,96},{96,80},{112,128},... | collective-permute-start | bytes 147464 | tf_op jit(solution)/shard_map/ppermute | solution.py:521
  74.0 4.0 %shard_map.151 = (f32[3,8,8,8,128]{4,3,2,1,0:T(8,128)S(1)}, f32[3,8,8,8,128]{4,3,2,1,0:T(8,128)S(1)}, f32[3,8,8,8,128]{4,3,2,1,0:T(8,128)S(1)}, f32[3,8,4,128]{3,2,1,0:T(4,128)S(1)}, f32[3,8,4,128]{3,2,1,0:T(4,128)S(1)}) custom-call(s32[2]{0:T(128)S(1)} %pad_add_fusion.par_ref.refs_0_, f32[6]{0:T(128)S(1)} %stack.35.coef_ref.refs_1_, ...), custom_call_target="tpu_custom_call" | custom-call | tf_op jit(solution)/shard_map/pallas_call | solution.py:509
  78.3 4.2 %collective-permute-start.11 = (f32[3,8,4,128]{3,2,1,0:T(4,128)S(1)}, f32[3,8,4,128]{3,2,1,0:T(4,128)S(1)}, u32[]{:S(2)}, u32[]{:S(2)}) collective-permute-start(f32[3,8,4,128]{3,2,1,0:T(4,128)S(1)} %get-tuple-element.126), channel_id=1, source_target_pairs={{0,15},{1,2},{2,1},{3,4},{4,3},{5,6},{6,5},{7,8},{8,7},{9,10},{10,... | collective-permute-start | bytes 147464 | tf_op jit(solution)/shard_map/ppermute | solution.py:521
  88.6 5.0 %collective-permute-start.13 = (f32[3,8,4,128]{3,2,1,0:T(4,128)S(1)}, f32[3,8,4,128]{3,2,1,0:T(4,128)S(1)}, u32[]{:S(2)}, u32[]{:S(2)}) collective-permute-start(f32[3,8,4,128]{3,2,1,0:T(4,128)S(1)} %get-tuple-element.128), channel_id=1, source_target_pairs={{0,240},{16,32},{32,16},{48,64},{64,48},{80,96},{96,80},{112,128},... | collective-permute-start | bytes 147464 | tf_op jit(solution)/shard_map/ppermute | solution.py:521
  96.7 4.9 %shard_map.154 = (f32[3,8,8,8,128]{4,3,2,1,0:T(8,128)S(1)}, f32[3,8,8,8,128]{4,3,2,1,0:T(8,128)}, f32[3,8,8,8,128]{4,3,2,1,0:T(8,128)S(1)}, f32[3,8,4,128]{3,2,1,0:T(4,128)S(1)}, f32[3,8,4,128]{3,2,1,0:T(4,128)S(1)}) custom-call(s32[2]{0:T(128)S(1)} %pad_add_fusion.par_ref.refs_0_, f32[6]{0:T(128)S(1)} %stack.35.coef_ref.refs_1_, ...), custom_call_target="tpu_custom_call" | custom-call | tf_op jit(solution)/shard_map/pallas_call | solution.py:509
  104.9 4.9 %shard_map.155 = (f32[3,8,8,8,128]{4,3,2,1,0:T(8,128)S(1)}, f32[3,8,8,8,128]{4,3,2,1,0:T(8,128)}, f32[3,8,8,8,128]{4,3,2,1,0:T(8,128)S(1)}) custom-call(s32[2]{0:T(128)S(1)} %pad_add_fusion.par_ref.refs_0_, f32[6]{0:T(128)S(1)} %stack.35.coef_ref.refs_1_, f32[3,8,8,8,128]{4,3,2,1,0:T(8,128)S(1)} %get-tuple-element.132.refs_2_, ...), custom_call_target="tpu_custom_call" | custom-call | tf_op jit(solution)/shard_map/pallas_call | solution.py:509
  111.9 5.0 %collective-permute-start.17 = (f32[3,8,4,128]{3,2,1,0:T(4,128)S(1)}, f32[3,8,4,128]{3,2,1,0:T(4,128)S(1)}, u32[]{:S(2)}, u32[]{:S(2)}) collective-permute-start(f32[3,8,4,128]{3,2,1,0:T(4,128)S(1)} %get-tuple-element.138), channel_id=1, source_target_pairs={{0,240},{16,32},{32,16},{48,64},{64,48},{80,96},{96,80},{112,128},... | collective-permute-start | bytes 147464 | tf_op jit(solution)/shard_map/ppermute | solution.py:521
  120.0 4.0 %shard_map.157 = (f32[3,8,8,8,128]{4,3,2,1,0:T(8,128)S(1)}, f32[3,8,8,8,128]{4,3,2,1,0:T(8,128)S(1)}, f32[3,8,8,8,128]{4,3,2,1,0:T(8,128)S(1)}, f32[3,8,4,128]{3,2,1,0:T(4,128)S(1)}, f32[3,8,4,128]{3,2,1,0:T(4,128)S(1)}) custom-call(s32[2]{0:T(128)S(1)} %pad_add_fusion.par_ref.refs_0_, f32[6]{0:T(128)S(1)} %stack.35.coef_ref.refs_1_, ...), custom_call_target="tpu_custom_call" | custom-call | tf_op jit(solution)/shard_map/pallas_call | solution.py:509
  134.7 5.2 %collective-permute-start.21 = (f32[3,8,4,128]{3,2,1,0:T(4,128)S(1)}, f32[3,8,4,128]{3,2,1,0:T(4,128)S(1)}, u32[]{:S(2)}, u32[]{:S(2)}) collective-permute-start(f32[3,8,4,128]{3,2,1,0:T(4,128)S(1)} %get-tuple-element.146), channel_id=1, source_target_pairs={{0,240},{16,32},{32,16},{48,64},{64,48},{80,96},{96,80},{112,128},... | collective-permute-start | bytes 147464 | tf_op jit(solution)/shard_map/ppermute | solution.py:521
  143.0 4.1 %shard_map.160 = (f32[3,8,8,8,128]{4,3,2,1,0:T(8,128)S(1)}, f32[3,8,8,8,128]{4,3,2,1,0:T(8,128)S(1)}, f32[3,8,8,8,128]{4,3,2,1,0:T(8,128)S(1)}, f32[3,8,4,128]{3,2,1,0:T(4,128)S(1)}, f32[3,8,4,128]{3,2,1,0:T(4,128)S(1)}) custom-call(s32[2]{0:T(128)S(1)} %pad_add_fusion.par_ref.refs_0_, f32[6]{0:T(128)S(1)} %stack.35.coef_ref.refs_1_, ...), custom_call_target="tpu_custom_call" | custom-call | tf_op jit(solution)/shard_map/pallas_call | solution.py:509
  148.1 4.0 %shard_map.161 = (f32[3,8,8,8,128]{4,3,2,1,0:T(8,128)S(1)}, f32[3,8,8,8,128]{4,3,2,1,0:T(8,128)S(1)}, f32[3,8,8,8,128]{4,3,2,1,0:T(8,128)S(1)}) custom-call(s32[2]{0:T(128)S(1)} %pad_add_fusion.par_ref.refs_0_, f32[6]{0:T(128)S(1)} %stack.35.coef_ref.refs_1_, f32[3,8,8,8,128]{4,3,2,1,0:T(8,128)S(1)} %get-tuple-element.150.refs_2_, ...), custom_call_target="tpu_custom_call" | custom-call | tf_op jit(solution)/shard_map/pallas_call | solution.py:509
  152.1 4.7 %collective-permute-done.23.xo_ref.refs_7_ = f32[3,8,4,128]{3,2,1,0:T(4,128)S(1)} collective-permute-done((f32[3,8,4,128]{3,2,1,0:T(4,128)S(1)}, f32[3,8,4,128]{3,2,1,0:T(4,128)S(1)}, u32[]{:S(2)}, u32[]{:S(2)}) %collective-permute-start.23) | collective-permute-done | bytes 49184 | tf_op jit(solution)/shard_map/ppermute | solution.py:521
  157.5 5.0 %collective-permute-start.25 = (f32[3,8,4,128]{3,2,1,0:T(4,128)S(1)}, f32[3,8,4,128]{3,2,1,0:T(4,128)S(1)}, u32[]{:S(2)}, u32[]{:S(2)}) collective-permute-start(f32[3,8,4,128]{3,2,1,0:T(4,128)S(1)} %get-tuple-element.156), channel_id=1, source_target_pairs={{0,240},{16,32},{32,16},{48,64},{64,48},{80,96},{96,80},{112,128},... | collective-permute-start | bytes 147464 | tf_op jit(solution)/shard_map/ppermute | solution.py:521
  165.6 4.9 %shard_map.163 = (f32[3,8,8,8,128]{4,3,2,1,0:T(8,128)S(1)}, f32[3,8,8,8,128]{4,3,2,1,0:T(8,128)}, f32[3,8,8,8,128]{4,3,2,1,0:T(8,128)S(1)}, f32[3,8,4,128]{3,2,1,0:T(4,128)S(1)}, f32[3,8,4,128]{3,2,1,0:T(4,128)S(1)}) custom-call(s32[2]{0:T(128)S(1)} %pad_add_fusion.par_ref.refs_0_, f32[6]{0:T(128)S(1)} %stack.35.coef_ref.refs_1_, ...), custom_call_target="tpu_custom_call" | custom-call | tf_op jit(solution)/shard_map/pallas_call | solution.py:509
  171.6 4.9 %shard_map.164 = (f32[3,8,8,8,128]{4,3,2,1,0:T(8,128)S(1)}, f32[3,8,8,8,128]{4,3,2,1,0:T(8,128)}, f32[3,8,8,8,128]{4,3,2,1,0:T(8,128)S(1)}) custom-call(s32[2]{0:T(128)S(1)} %pad_add_fusion.par_ref.refs_0_, f32[6]{0:T(128)S(1)} %stack.35.coef_ref.refs_1_, f32[3,8,8,8,128]{4,3,2,1,0:T(8,128)S(1)} %get-tuple-element.159.refs_2_, ...), custom_call_target="tpu_custom_call" | custom-call | tf_op jit(solution)/shard_map/pallas_call | solution.py:509
  181.0 5.0 %collective-permute-start.29 = (f32[3,8,4,128]{3,2,1,0:T(4,128)S(1)}, f32[3,8,4,128]{3,2,1,0:T(4,128)S(1)}, u32[]{:S(2)}, u32[]{:S(2)}) collective-permute-start(f32[3,8,4,128]{3,2,1,0:T(4,128)S(1)} %get-tuple-element.167), channel_id=1, source_target_pairs={{0,240},{16,32},{32,16},{48,64},{64,48},{80,96},{96,80},{112,128},... | collective-permute-start | bytes 147464 | tf_op jit(solution)/shard_map/ppermute | solution.py:521
  (89 shorter events, 72.3 us)
Async XLA Ops:
  7.4 10.4 %collective-permute-start = (f32[6,8,4,128]{3,2,1,0:T(4,128)S(1)}, f32[6,8,4,128]{3,2,1,0:T(4,128)S(1)}, u32[]{:S(2)}, u32[]{:S(2)}) collective-permute-start(f32[6,8,4,128]{3,2,1,0:T(4,128)S(1)} %pad_maximum_fusion), channel_id=1, source_target_pairs={{0,15},{1,0},{2,1},{3,2},{4,3},{5,4},{6,5},{7,6},{8,7},{9,8},{10,9... | collective-permute-start | bytes 294920 | tf_op jit(solution)/shard_map/ppermute | solution.py:535
  17.8 5.7 %collective-permute-start.1 = (f32[6,8,4,128]{3,2,1,0:T(4,128)S(1)}, f32[6,8,4,128]{3,2,1,0:T(4,128)S(1)}, u32[]{:S(2)}, u32[]{:S(2)}) collective-permute-start(f32[6,8,4,128]{3,2,1,0:T(4,128)S(1)} %shard_map.142), channel_id=1, source_target_pairs={{0,240},{16,0},{32,16},{48,32},{64,48},{80,64},{96,80},{112,96},{1... | collective-permute-start | bytes 294920 | tf_op jit(solution)/shard_map/ppermute | solution.py:535
  29.0 11.7 %collective-permute-start.2 = (f32[6,8,4,128]{3,2,1,0:T(4,128)S(1)}, f32[6,8,4,128]{3,2,1,0:T(4,128)S(1)}, u32[]{:S(2)}, u32[]{:S(2)}) collective-permute-start(f32[6,8,4,128]{3,2,1,0:T(4,128)S(1)} %get-tuple-element.103), channel_id=1, source_target_pairs={{0,1},{1,0},{2,3},{3,2},{4,5},{5,4},{6,7},{7,6},{8,9},{9,8},{10,11... | collective-permute-start | bytes 294920 | tf_op jit(solution)/shard_map/ppermute | solution.py:522
  29.1 11.7 %collective-permute-start.3 = (f32[6,8,4,128]{3,2,1,0:T(4,128)S(1)}, f32[6,8,4,128]{3,2,1,0:T(4,128)S(1)}, u32[]{:S(2)}, u32[]{:S(2)}) collective-permute-start(f32[6,8,4,128]{3,2,1,0:T(4,128)S(1)} %get-tuple-element.104), channel_id=1, source_target_pairs={{0,15},{1,2},{2,1},{3,4},{4,3},{5,6},{6,5},{7,8},{8,7},{9,10},{10,... | collective-permute-start | bytes 294920 | tf_op jit(solution)/shard_map/ppermute | solution.py:521
  41.4 6.2 %collective-permute-start.4 = (f32[6,8,4,128]{3,2,1,0:T(4,128)S(1)}, f32[6,8,4,128]{3,2,1,0:T(4,128)S(1)}, u32[]{:S(2)}, u32[]{:S(2)}) collective-permute-start(f32[6,8,4,128]{3,2,1,0:T(4,128)S(1)} %get-tuple-element.107), channel_id=1, source_target_pairs={{0,16},{16,0},{32,48},{48,32},{64,80},{80,64},{96,112},{112,96},{1... | collective-permute-start | bytes 294920 | tf_op jit(solution)/shard_map/ppermute | solution.py:522
  41.5 9.7 %collective-permute-start.5 = (f32[6,8,4,128]{3,2,1,0:T(4,128)S(1)}, f32[6,8,4,128]{3,2,1,0:T(4,128)S(1)}, u32[]{:S(2)}, u32[]{:S(2)}) collective-permute-start(f32[6,8,4,128]{3,2,1,0:T(4,128)S(1)} %get-tuple-element.108), channel_id=1, source_target_pairs={{0,240},{16,32},{32,16},{48,64},{64,48},{80,96},{96,80},{112,128},... | collective-permute-start | bytes 294920 | tf_op jit(solution)/shard_map/ppermute | solution.py:521
  55.4 9.4 %collective-permute-start.6 = (f32[3,8,4,128]{3,2,1,0:T(4,128)S(1)}, f32[3,8,4,128]{3,2,1,0:T(4,128)S(1)}, u32[]{:S(2)}, u32[]{:S(2)}) collective-permute-start(f32[3,8,4,128]{3,2,1,0:T(4,128)S(1)} %get-tuple-element.113), channel_id=1, source_target_pairs={{0,1},{1,0},{2,3},{3,2},{4,5},{5,4},{6,7},{7,6},{8,9},{9,8},{10,11... | collective-permute-start | bytes 147464 | tf_op jit(solution)/shard_map/ppermute | solution.py:522
  55.5 9.6 %collective-permute-start.7 = (f32[3,8,4,128]{3,2,1,0:T(4,128)S(1)}, f32[3,8,4,128]{3,2,1,0:T(4,128)S(1)}, u32[]{:S(2)}, u32[]{:S(2)}) collective-permute-start(f32[3,8,4,128]{3,2,1,0:T(4,128)S(1)} %get-tuple-element.114), channel_id=1, source_target_pairs={{0,15},{1,2},{2,1},{3,4},{4,3},{5,6},{6,5},{7,8},{8,7},{9,10},{10,... | collective-permute-start | bytes 147464 | tf_op jit(solution)/shard_map/ppermute | solution.py:521
  65.9 8.1 %collective-permute-start.9 = (f32[3,8,4,128]{3,2,1,0:T(4,128)S(1)}, f32[3,8,4,128]{3,2,1,0:T(4,128)S(1)}, u32[]{:S(2)}, u32[]{:S(2)}) collective-permute-start(f32[3,8,4,128]{3,2,1,0:T(4,128)S(1)} %get-tuple-element.116), channel_id=1, source_target_pairs={{0,240},{16,32},{32,16},{48,64},{64,48},{80,96},{96,80},{112,128},... | collective-permute-start | bytes 147464 | tf_op jit(solution)/shard_map/ppermute | solution.py:521
  78.0 8.5 %collective-permute-start.10 = (f32[3,8,4,128]{3,2,1,0:T(4,128)S(1)}, f32[3,8,4,128]{3,2,1,0:T(4,128)S(1)}, u32[]{:S(2)}, u32[]{:S(2)}) collective-permute-start(f32[3,8,4,128]{3,2,1,0:T(4,128)S(1)} %get-tuple-element.125), channel_id=1, source_target_pairs={{0,1},{1,0},{2,3},{3,2},{4,5},{5,4},{6,7},{7,6},{8,9},{9,8},{10,11... | collective-permute-start | bytes 147464 | tf_op jit(solution)/shard_map/ppermute | solution.py:522
  78.3 9.6 %collective-permute-start.11 = (f32[3,8,4,128]{3,2,1,0:T(4,128)S(1)}, f32[3,8,4,128]{3,2,1,0:T(4,128)S(1)}, u32[]{:S(2)}, u32[]{:S(2)}) collective-permute-start(f32[3,8,4,128]{3,2,1,0:T(4,128)S(1)} %get-tuple-element.126), channel_id=1, source_target_pairs={{0,15},{1,2},{2,1},{3,4},{4,3},{5,6},{6,5},{7,8},{8,7},{9,10},{10,... | collective-permute-start | bytes 147464 | tf_op jit(solution)/shard_map/ppermute | solution.py:521
  88.6 8.1 %collective-permute-start.13 = (f32[3,8,4,128]{3,2,1,0:T(4,128)S(1)}, f32[3,8,4,128]{3,2,1,0:T(4,128)S(1)}, u32[]{:S(2)}, u32[]{:S(2)}) collective-permute-start(f32[3,8,4,128]{3,2,1,0:T(4,128)S(1)} %get-tuple-element.128), channel_id=1, source_target_pairs={{0,240},{16,32},{32,16},{48,64},{64,48},{80,96},{96,80},{112,128},... | collective-permute-start | bytes 147464 | tf_op jit(solution)/shard_map/ppermute | solution.py:521
  101.7 8.1 %collective-permute-start.14 = (f32[3,8,4,128]{3,2,1,0:T(4,128)S(1)}, f32[3,8,4,128]{3,2,1,0:T(4,128)S(1)}, u32[]{:S(2)}, u32[]{:S(2)}) collective-permute-start(f32[3,8,4,128]{3,2,1,0:T(4,128)S(1)} %get-tuple-element.135), channel_id=1, source_target_pairs={{0,1},{1,0},{2,3},{3,2},{4,5},{5,4},{6,7},{7,6},{8,9},{9,8},{10,11... | collective-permute-start | bytes 147464 | tf_op jit(solution)/shard_map/ppermute | solution.py:522
  101.7 9.5 %collective-permute-start.15 = (f32[3,8,4,128]{3,2,1,0:T(4,128)S(1)}, f32[3,8,4,128]{3,2,1,0:T(4,128)S(1)}, u32[]{:S(2)}, u32[]{:S(2)}) collective-permute-start(f32[3,8,4,128]{3,2,1,0:T(4,128)S(1)} %get-tuple-element.136), channel_id=1, source_target_pairs={{0,15},{1,2},{2,1},{3,4},{4,3},{5,6},{6,5},{7,8},{8,7},{9,10},{10,... | collective-permute-start | bytes 147464 | tf_op jit(solution)/shard_map/ppermute | solution.py:521
  111.9 8.1 %collective-permute-start.17 = (f32[3,8,4,128]{3,2,1,0:T(4,128)S(1)}, f32[3,8,4,128]{3,2,1,0:T(4,128)S(1)}, u32[]{:S(2)}, u32[]{:S(2)}) collective-permute-start(f32[3,8,4,128]{3,2,1,0:T(4,128)S(1)} %get-tuple-element.138), channel_id=1, source_target_pairs={{0,240},{16,32},{32,16},{48,64},{64,48},{80,96},{96,80},{112,128},... | collective-permute-start | bytes 147464 | tf_op jit(solution)/shard_map/ppermute | solution.py:521
  124.0 6.2 %collective-permute-start.18 = (f32[3,8,4,128]{3,2,1,0:T(4,128)S(1)}, f32[3,8,4,128]{3,2,1,0:T(4,128)S(1)}, u32[]{:S(2)}, u32[]{:S(2)}) collective-permute-start(f32[3,8,4,128]{3,2,1,0:T(4,128)S(1)} %get-tuple-element.143), channel_id=1, source_target_pairs={{0,1},{1,0},{2,3},{3,2},{4,5},{5,4},{6,7},{7,6},{8,9},{9,8},{10,11... | collective-permute-start | bytes 147464 | tf_op jit(solution)/shard_map/ppermute | solution.py:522
  124.1 9.9 %collective-permute-start.19 = (f32[3,8,4,128]{3,2,1,0:T(4,128)S(1)}, f32[3,8,4,128]{3,2,1,0:T(4,128)S(1)}, u32[]{:S(2)}, u32[]{:S(2)}) collective-permute-start(f32[3,8,4,128]{3,2,1,0:T(4,128)S(1)} %get-tuple-element.144), channel_id=1, source_target_pairs={{0,15},{1,2},{2,1},{3,4},{4,3},{5,6},{6,5},{7,8},{8,7},{9,10},{10,... | collective-permute-start | bytes 147464 | tf_op jit(solution)/shard_map/ppermute | solution.py:521
  134.7 8.3 %collective-permute-start.21 = (f32[3,8,4,128]{3,2,1,0:T(4,128)S(1)}, f32[3,8,4,128]{3,2,1,0:T(4,128)S(1)}, u32[]{:S(2)}, u32[]{:S(2)}) collective-permute-start(f32[3,8,4,128]{3,2,1,0:T(4,128)S(1)} %get-tuple-element.146), channel_id=1, source_target_pairs={{0,240},{16,32},{32,16},{48,64},{64,48},{80,96},{96,80},{112,128},... | collective-permute-start | bytes 147464 | tf_op jit(solution)/shard_map/ppermute | solution.py:521
  147.2 9.6 %collective-permute-start.23 = (f32[3,8,4,128]{3,2,1,0:T(4,128)S(1)}, f32[3,8,4,128]{3,2,1,0:T(4,128)S(1)}, u32[]{:S(2)}, u32[]{:S(2)}) collective-permute-start(f32[3,8,4,128]{3,2,1,0:T(4,128)S(1)} %get-tuple-element.154), channel_id=1, source_target_pairs={{0,15},{1,2},{2,1},{3,4},{4,3},{5,6},{6,5},{7,8},{8,7},{9,10},{10,... | collective-permute-start | bytes 147464 | tf_op jit(solution)/shard_map/ppermute | solution.py:521
  157.5 8.1 %collective-permute-start.25 = (f32[3,8,4,128]{3,2,1,0:T(4,128)S(1)}, f32[3,8,4,128]{3,2,1,0:T(4,128)S(1)}, u32[]{:S(2)}, u32[]{:S(2)}) collective-permute-start(f32[3,8,4,128]{3,2,1,0:T(4,128)S(1)} %get-tuple-element.156), channel_id=1, source_target_pairs={{0,240},{16,32},{32,16},{48,64},{64,48},{80,96},{96,80},{112,128},... | collective-permute-start | bytes 147464 | tf_op jit(solution)/shard_map/ppermute | solution.py:521
  170.5 5.9 %collective-permute-start.26 = (f32[3,8,4,128]{3,2,1,0:T(4,128)S(1)}, f32[3,8,4,128]{3,2,1,0:T(4,128)S(1)}, u32[]{:S(2)}, u32[]{:S(2)}) collective-permute-start(f32[3,8,4,128]{3,2,1,0:T(4,128)S(1)} %get-tuple-element.164), channel_id=1, source_target_pairs={{0,1},{1,0},{2,3},{3,2},{4,5},{5,4},{6,7},{7,6},{8,9},{9,8},{10,11... | collective-permute-start | bytes 147464 | tf_op jit(solution)/shard_map/ppermute | solution.py:522
  170.5 9.7 %collective-permute-start.27 = (f32[3,8,4,128]{3,2,1,0:T(4,128)S(1)}, f32[3,8,4,128]{3,2,1,0:T(4,128)S(1)}, u32[]{:S(2)}, u32[]{:S(2)}) collective-permute-start(f32[3,8,4,128]{3,2,1,0:T(4,128)S(1)} %get-tuple-element.165), channel_id=1, source_target_pairs={{0,15},{1,2},{2,1},{3,4},{4,3},{5,6},{6,5},{7,8},{8,7},{9,10},{10,... | collective-permute-start | bytes 147464 | tf_op jit(solution)/shard_map/ppermute | solution.py:521
  180.9 7.9 %collective-permute-start.28 = (f32[3,8,4,128]{3,2,1,0:T(4,128)S(1)}, f32[3,8,4,128]{3,2,1,0:T(4,128)S(1)}, u32[]{:S(2)}, u32[]{:S(2)}) collective-permute-start(f32[3,8,4,128]{3,2,1,0:T(4,128)S(1)} %get-tuple-element.166), channel_id=1, source_target_pairs={{0,16},{16,0},{32,48},{48,32},{64,80},{80,64},{96,112},{112,96},{1... | collective-permute-start | bytes 147464 | tf_op jit(solution)/shard_map/ppermute | solution.py:522
  181.0 8.1 %collective-permute-start.29 = (f32[3,8,4,128]{3,2,1,0:T(4,128)S(1)}, f32[3,8,4,128]{3,2,1,0:T(4,128)S(1)}, u32[]{:S(2)}, u32[]{:S(2)}) collective-permute-start(f32[3,8,4,128]{3,2,1,0:T(4,128)S(1)} %get-tuple-element.167), channel_id=1, source_target_pairs={{0,240},{16,32},{32,16},{48,64},{64,48},{80,96},{96,80},{112,128},... | collective-permute-start | bytes 147464 | tf_op jit(solution)/shard_map/ppermute | solution.py:521
  (16 other events, 85.8 us)

commit v2 on v1

v2 whole, which is shorter than its diff:
```python
import jax
import jax.numpy as jnp
import numpy as np
from jax import lax
from jax.experimental import pallas as pl
from jax.experimental.pallas import tpu as pltpu
from jax.sharding import PartitionSpec as P

DEG = 7
N = DEG + 1
SWEEPS = 2
CHEB = 3
F32 = jnp.float32
BF16 = jnp.bfloat16
highest = lax.Precision.HIGHEST


def legendre_pair(points, degree):
    prev_poly = points * 0.0 + 1.0
    this_poly = points * 1.0
    for order in range(2, degree + 1):
        next_poly = ((2 * order - 1) * points * this_poly - (order - 1) * prev_poly) / order
        prev_poly = this_poly
        this_poly = next_poly
    return (this_poly, prev_poly)


def gll_tables(degree):
    count = degree + 1
    points = -np.cos(np.pi * np.arange(count) / degree)
    for newton_step in range(60):
        this_poly, prev_poly = legendre_pair(points, degree)
        points = points - (points * this_poly - prev_poly) / (count * this_poly)
    values, unused_poly = legendre_pair(points, degree)
    weights = 2.0 / (degree * (degree + 1) * values**2)
    identity_np = np.eye(count)
    spacing = points[:, None] - points[None, :] + identity_np
    derivative = values[:, None] / (values[None, :] * spacing) * (1.0 - identity_np)
    derivative[0, 0] = -degree * (degree + 1) / 4.0
    derivative[degree, degree] = degree * (degree + 1) / 4.0
    stiff_ratio = (weights[:, None] * derivative**2).sum(0) / weights
    return (weights, derivative, stiff_ratio)


WEIGHTS, DERIV, RATIO = gll_tables(DEG)


def halves(matrix):
    high = matrix.astype(BF16).astype(np.float32)
    low = matrix.astype(np.float32) - high
    return high, low


def z_matrices(blocks):
    width = blocks * N
    node = np.array([DEG * f + k for f in range(blocks) for k in range(N)])
    free = (node > 0) & (node < DEG * blocks)
    share = ((node[:, None] == node[None, :]) & free[:, None] & free[None, :]).astype(np.float64)
    grad = np.kron(np.eye(blocks), DERIV.T)
    back = np.kron(np.eye(blocks), DERIV) @ share
    zero = np.zeros((width, width))
    grad_hi, grad_lo = halves(grad)
    back_hi, back_lo = halves(back)
    w_grad = np.block([[grad_hi, grad_lo], [grad_hi, zero]])
    w_back = np.block([[back_hi, back_lo], [back_hi, zero]])
    w_share = np.concatenate([share, share], 0)
    return w_grad, w_back, w_share


def line_sums(vals, matrix, pairs=range(N // 2)):
    even = [vals[i] + vals[DEG - i] for i in range(N // 2)]
    odd = [vals[i] - vals[DEG - i] for i in range(N // 2)]
    outs = [None] * N
    for p in pairs:
        from_even = None
        from_odd = None
        for i in range(N // 2):
            te = float(np.float32((matrix[p, i] + matrix[p, DEG - i]) / 2.0)) * even[i]
            to = float(np.float32((matrix[p, i] - matrix[p, DEG - i]) / 2.0)) * odd[i]
            from_even = te if from_even is None else from_even + te
            from_odd = to if from_odd is None else from_odd + to
        outs[p] = from_odd + from_even
        outs[DEG - p] = from_odd - from_even
    return outs


def split_pair(value):
    high = value.astype(BF16)
    low = (value - high.astype(F32)).astype(BF16)
    return jnp.concatenate([high, low], axis=-1)


def dot(a, b):
    return jnp.dot(a, b, preferred_element_type=F32)


ROWS = 8
SIDE = 4
ORDER = (0, 3, 1, 2)
UNROLL = 2


def flip(value):
    return jnp.concatenate([value[SIDE:], value[:SIDE]], 0)


def whole(ref):
    return lambda c, i, j: ref[c, i, j]


def by_i(face_ref, inner_ref):
    return lambda c, i, j: face_ref[c, i // DEG, j] if i in (0, DEG) else inner_ref[c, i - 1, j]


def by_j(mid_ref, edge_ref):
    return lambda c, i, j: edge_ref[c, i, j // DEG] if j in (0, DEG) else mid_ref[c, i, j - 1]


def received(ctl_ref, axis, even_ref, odd_ref, *at):
    is_even = ctl_ref[axis][:SIDE] < 0.5
    even = even_ref[at]
    odd = odd_ref[at]
    return jnp.where(is_even, even, odd), jnp.where(is_even, odd, even)


def sum_x(ctl_ref, xe_ref, xo_ref, parts, c, face_at, i, j, tile):
    total = parts[tile](c, i, j)
    if 0 < i < DEG:
        return total
    row = lax.broadcasted_iota(jnp.int32, (ROWS, 128), 0)
    across = DEG - i
    if tile == 0:
        right, left = received(ctl_ref, 0, xe_ref, xo_ref, face_at, j)
        face = right if i else left
        face = jnp.concatenate([face, face], 0)
        inner = parts[1](c, across, j)
        low, high = (inner, face) if i else (face, inner)
    else:
        middle = flip(parts[1](c, across, j))
        outer = parts[0](c, across, j)
        low, high = (middle, outer) if i else (outer, middle)
    return total + jnp.where(row < SIDE, low, high)


def sum_all(ctl_ref, faces, parts, c, face_at, i, j, tile):
    xe, xo, ye, yo = faces
    total = sum_x(ctl_ref, xe, xo, parts, c, face_at, i, j, tile)
    if j in (0, DEG):
        row = lax.broadcasted_iota(jnp.int32, (ROWS, 128), 0)
        top, bottom = received(ctl_ref, 1, ye, yo, face_at, i)
        face = top if j else bottom
        at = SIDE - 1 if j else 0
        first = jnp.broadcast_to(face[2 * tile : 2 * tile + 1], (ROWS, 128))
        second = jnp.broadcast_to(face[2 * tile + 1 : 2 * tile + 2], (ROWS, 128))
        total = total + jnp.where(row == at, first, jnp.where(row == SIDE + at, second, 0.0))
    return total


def loop(count, body, unroll=UNROLL):
    def inner(i, carry):
        body(i)
        return carry

    lax.fori_loop(0, count, inner, 0, unroll=unroll)


def gradients(planes, at, wg_ref, gx_ref, gz_ref):
    flat = jnp.concatenate([planes[c][i] for c in range(3) for i in range(N)], 0)
    both = dot(split_pair(flat), wg_ref[...])
    for c in range(3):
        outs = line_sums(planes[c], DERIV)
        for i in range(N):
            gx_ref[c, i, at] = outs[i]
    both = (both[:, :128] + both[:, 128:]).reshape(3, N, ROWS, 128)
    for c in range(3):
        for i in range(N):
            gz_ref[c, i, at] = both[c, i]


def stress(u_at, gx_at, gz_at, lam_ref, mu_ref, wb_ref, sx_ref, fz_ref, fy_ref):
    def plane(i):
        gy = [line_sums([u_at(c, i, j) for j in range(N)], DERIV) for c in range(3)]
        sy = [[None] * N for c in range(3)]
        sz = [[None] * N for c in range(3)]
        for j in range(N):
            gx = [gx_at(c, i, j) for c in range(3)]
            gz = [gz_at(c, i, j) for c in range(3)]
            mu = mu_ref[i, j]
            mu2 = mu + mu
            trace = lam_ref[i, j] * (gx[0] + gy[1][j] + gz[2])
            sxy = mu * (gx[1] + gy[0][j])
            sxz = mu * (gx[2] + gz[0])
            syz = mu * (gy[2][j] + gz[1])
            sx_ref[0, i, j] = mu2 * gx[0] + trace
            sx_ref[1, i, j] = sxy
            sx_ref[2, i, j] = sxz
            sz[0][j] = sxz
            sz[1][j] = syz
            sz[2][j] = mu2 * gz[2] + trace
            sy[0][j] = sxy
            sy[1][j] = mu2 * gy[1][j] + trace
            sy[2][j] = syz
        flat = jnp.concatenate([sz[c][j] for c in range(3) for j in range(N)], 0)
        both = dot(split_pair(flat), wb_ref[...])
        for c in range(3):
            outs = line_sums(sy[c], DERIV.T)
            for j in range(N):
                fy_ref[c, i, j] = outs[j]
        both = (both[:, :128] + both[:, 128:]).reshape(3, N, ROWS, 128)
        for c in range(3):
            fz_ref[c, i] = both[c]

    loop(N, plane)


def back(ws_ref, work, out_ref, nodes, planes):
    sx_ref, fz_ref, fy_ref = work
    pairs = sorted({min(i, DEG - i) for i in nodes})
    flat = []
    for j in planes:
        for c in range(3):
            outs = line_sums([sx_ref[c, i, j] for i in range(N)], DERIV.T, pairs)
            flat += [outs[i] + fy_ref[c, i, j] for i in nodes]
    both = dot(split_pair(jnp.concatenate(flat, 0)), ws_ref[...]).reshape(len(planes), 3, len(nodes), ROWS, 128)
    for at, j in enumerate(planes):
        for c in range(3):
            for k, i in enumerate(nodes):
                out_ref[c, k, j] = both[at, c, k] + fz_ref[c, i, j]


def back_loop(ws_ref, work, out_ref, nodes):
    loop(N, lambda j: back(ws_ref, work, out_ref, nodes, (j,)))


def join_y(part_ref):
    row = lax.broadcasted_iota(jnp.int32, (ROWS, 128), 0)
    near = row % SIDE

    def along(i):
        for c in range(3):
            last = part_ref[c, i, DEG]
            start = part_ref[c, i, 0]
            last = last + jnp.where(near < SIDE - 1, jnp.concatenate([start[1:], start[:1]], 0), 0.0)
            start = jnp.where(near > 0, jnp.concatenate([last[-1:], last[:-1]], 0), start)
            part_ref[c, i, DEG] = last
            part_ref[c, i, 0] = start

    loop(part_ref.shape[1], along)


def give_faces(ctl_ref, part_ref, first, xe_ref, xo_ref):
    is_even = ctl_ref[0][:SIDE] < 0.5
    end = part_ref.shape[1] - 1

    def plane(j):
        for c in range(3):
            right = part_ref[c, end, j][SIDE:]
            left = part_ref[c, 0, j][:SIDE]
            xe_ref[first + c, j] = jnp.where(is_even, right, left)
            xo_ref[first + c, j] = jnp.where(is_even, left, right)

    loop(N, plane)


ENDS = (0, DEG)
INSIDE = tuple(range(1, DEG))
ALL = tuple(range(N))


def send_first(ctl_ref, ws_ref, work, face_ref, xe_ref, xo_ref):
    back(ws_ref, work, face_ref, ENDS, ALL)
    join_y(face_ref)
    give_faces(ctl_ref, face_ref, 0, xe_ref, xo_ref)


def finish_second(ws_ref, work, work_0, inner_ref, au_ref):
    back_loop(ws_ref, work, au_ref, ALL)
    join_y(au_ref)
    back_loop(ws_ref, work_0, inner_ref, INSIDE)
    join_y(inner_ref)


def first_kernel(tile, *refs):
    refs = list(refs)
    take = lambda count: [refs.pop(0) for _ in range(count)]
    ctl_ref, mid_ref, edge_ref, lam_ref, mu_ref, ratio_ref, rk_ref, wg_ref, wb_ref, ws_ref = take(10)
    if tile == 0:
        dg_ref, face_ref, xe_ref, xo_ref = take(4)
    else:
        work_0 = take(3)
        dg_ref, inner_ref, au_ref = take(3)
    sx_ref, fz_ref, fy_ref = take(3)

    def diagonal(i):
        rows = [[None] * N for c in range(3)]
        for j in range(N):
            lam = lam_ref[i, j]
            mu = mu_ref[i, j]
            ri = ratio_ref[i]
            rk = rk_ref[...]
            total = rk + (ri + float(RATIO[j]))
            for c in range(3):
                own = (ri, float(RATIO[j]), rk)[c]
                rows[c][j] = lam * own + mu * (total + own)
        flat = jnp.concatenate([rows[c][j] for c in range(3) for j in range(N)], 0)
        both = dot(split_pair(flat), ws_ref[...]).reshape(3, N, ROWS, 128)
        for c in range(3):
            dg_ref[c, i] = both[c]

    loop(N, diagonal, 1)

    def start(at):
        gradients([[mid_ref[c, i, at] for i in range(N)] for c in range(3)], at + 1, wg_ref, sx_ref, fz_ref)

    loop(N - 2, start)
    for k in range(2):
        gradients([[edge_ref[c, i, k] for i in range(N)] for c in range(3)], DEG * k, wg_ref, sx_ref, fz_ref)
    work = (sx_ref, fz_ref, fy_ref)
    stress(by_j(mid_ref, edge_ref), whole(sx_ref), whole(fz_ref), lam_ref, mu_ref, wb_ref, *work)
    join_y(dg_ref)
    if tile == 0:
        send_first(ctl_ref, ws_ref, work, face_ref, xe_ref, xo_ref)
        give_faces(ctl_ref, dg_ref, 3, xe_ref, xo_ref)
    else:
        finish_second(ws_ref, work, work_0, inner_ref, au_ref)


def corner_kernel(ctl_ref, xe_ref, xo_ref, face_ref, inner_ref, au_ref, *refs):
    ye_ref, yo_ref = refs[-2:]
    fields = [(by_i(face_ref, inner_ref), whole(au_ref))]
    if len(refs) > 2:
        fields.append((whole(refs[0]), whole(refs[1])))
    is_even = ctl_ref[1][:SIDE] < 0.5
    for n, parts in enumerate(fields):
        for c in range(3):
            at = 3 * n + c
            for i in range(N):
                rows_t = []
                rows_b = []
                for tile in range(2):
                    top = sum_x(ctl_ref, xe_ref, xo_ref, parts, c, at, i, DEG, tile)
                    bottom = sum_x(ctl_ref, xe_ref, xo_ref, parts, c, at, i, 0, tile)
                    rows_t += [top[SIDE - 1 : SIDE], top[-1:]]
                    rows_b += [bottom[:1], bottom[SIDE : SIDE + 1]]
                top = jnp.concatenate(rows_t, 0)
                bottom = jnp.concatenate(rows_b, 0)
                ye_ref[at, i] = jnp.where(is_even, top, bottom)
                yo_ref[at, i] = jnp.where(is_even, bottom, top)


def invert(diag):
    lane = lax.broadcasted_iota(jnp.int32, (ROWS, 128), 1)
    clamped = (lane == 0) | (lane == 127)
    return jnp.where(clamped, 0.0, 1.0 / jnp.where(clamped, 1.0, diag))


def advance(ctl_ref, stage, u, load, total, inv, change):
    change_new = ctl_ref[3 + 2 * stage] * (inv * (load - total))
    if stage:
        change_new = ctl_ref[2 + 2 * stage] * change + change_new
    return u + change_new, change_new


def mid_kernel(stage, with_diag, *refs):
    refs = list(refs)
    take = lambda count: [refs.pop(0) for _ in range(count)]
    ctl_ref, wg_ref, face_ref, inner_ref, au_ref, xe_ref, xo_ref = take(7)
    parts = (by_i(face_ref, inner_ref), whole(au_ref))
    diag_parts = [whole(ref) for ref in take(2)] if with_diag else None
    ins = []
    for tile in range(2):
        u_ref, b_ref = take(2)
        ins.append((u_ref, b_ref, None if with_diag else take(1)[0], take(1)[0] if stage else None))
    for tile in range(2):
        u_ref, b_ref, inv_ref, change_ref = ins[tile]
        u_out, change_out, gx_ref, gz_ref = take(4)
        inv_out = take(1)[0] if with_diag else None

        def plane(at):
            j = at + 1
            planes = [[None] * N for c in range(3)]
            for c in range(3):
                for i in range(N):
                    if with_diag:
                        inv = invert(sum_x(ctl_ref, xe_ref, xo_ref, diag_parts, c, 3 + c, i, j, tile))
                        inv_out[c, i, at] = inv
                    else:
                        inv = inv_ref[c, i, at]
                    total = sum_x(ctl_ref, xe_ref, xo_ref, parts, c, c, i, j, tile)
                    change = change_ref[c, i, at] if stage else None
                    planes[c][i], change = advance(ctl_ref, stage, u_ref[c, i, at], b_ref[c, i, j], total, inv, change)
                    change_out[c, i, at] = change
                    u_out[c, i, at] = planes[c][i]
            gradients(planes, at, wg_ref, gx_ref, gz_ref)

        loop(N - 2, plane)


def edge_kernel(tile, stage, with_diag, *refs):
    refs = list(refs)
    take = lambda count: [refs.pop(0) for _ in range(count)]
    ctl_ref, wg_ref, wb_ref, ws_ref, lam_ref, mu_ref, face_in, inner_in, au_in = take(9)
    faces = take(4)
    parts = (by_i(face_in, inner_in), whole(au_in))
    diag_parts = [whole(ref) for ref in take(2)] if with_diag else None
    mid_ref, gx_ref, gz_ref, u_ref, b_ref = take(5)
    inv_ref = None if with_diag else take(1)[0]
    change_ref = take(1)[0] if stage else None
    work_0 = take(3) if tile else None
    u_out, change_out = take(2)
    inv_out = take(1)[0] if with_diag else None
    outs = take(2 if tile else 3)
    work = take(3)
    sx_ref, fz_ref, fy_ref = work
    for k in range(2):
        j = DEG * k
        planes = [[None] * N for c in range(3)]
        for c in range(3):
            for i in range(N):
                if with_diag:
                    inv = invert(sum_all(ctl_ref, faces, diag_parts, c, 3 + c, i, j, tile))
                    inv_out[c, i, k] = inv
                else:
                    inv = inv_ref[c, i, k]
                total = sum_all(ctl_ref, faces, parts, c, c, i, j, tile)
                change = change_ref[c, i, k] if stage else None
                planes[c][i], change = advance(ctl_ref, stage, u_ref[c, i, k], b_ref[c, i, j], total, inv, change)
                change_out[c, i, k] = change
                u_out[c, i, k] = planes[c][i]
        gradients(planes, j, wg_ref, sx_ref, fz_ref)

    def mixed(mid, full):
        return lambda c, i, j: full[c, i, j] if j in ENDS else mid[c, i, j - 1]

    stress(by_j(mid_ref, u_out), mixed(gx_ref, sx_ref), mixed(gz_ref, fz_ref), lam_ref, mu_ref, wb_ref, *work)
    if tile == 0:
        send_first(ctl_ref, ws_ref, work, *outs)
    else:
        finish_second(ws_ref, work, work_0, *outs)


def lane_pick(value, index):
    return jnp.take_along_axis(value, index, axis=1, mode="promise_in_bounds")


TILES = ((0, 8), (8, 16), (16, 24), (20, 28))


def load_kernel(ctl_ref, in_ref, t0_ref, t1_ref, xl_ref, yb_ref, work_ref):
    nodes_x, width = in_ref.shape[1], in_ref.shape[2]
    nodes_z = width // nodes_x
    outs = (t0_ref, t1_ref)
    lane = lax.broadcasted_iota(jnp.int32, (ROWS, 128), 1)
    node = DEG * (lane // N) + lane % N - 1
    free = (node >= 0) & (node < nodes_z)
    node = jnp.clip(node, 0, nodes_z - 1)
    zero = jnp.zeros((ROWS, 128), F32)
    for r in range(4):
        work_ref[nodes_x, pl.ds(8 * r, 8)] = zero

    def component(c, carry):
        for y in range(nodes_x):
            tile, shift = divmod(nodes_z * y, 128)
            at = node + shift
            begin = 128 * tile
            work_ref[y, pl.ds(24, 8)] = zero
            for low, high in TILES:
                here = in_ref[c, low:high, begin : begin + 128]
                got = lane_pick(here, at & 127)
                if shift + nodes_z > 128:
                    stop = min(begin + 256, width)
                    there = in_ref[c, low:high, begin + 128 : stop]
                    if stop < begin + 256:
                        there = jnp.concatenate([there, jnp.zeros((ROWS, begin + 256 - stop), F32)], 1)
                    got = jnp.where(at < 128, got, lane_pick(there, at & 127))
                work_ref[y, low:high] = jnp.where(free, got, 0.0)
        out_c = jnp.where(c == 2, 2, 1 - c)
        for i in range(N):
            for j in range(N):
                for which in range(2):
                    rows = [work_ref[DEG * ORDER[2 * which + k] + i, pl.ds(j, SIDE, stride=DEG)] for k in range(2)]
                    value = jnp.concatenate(rows, 0)
                    outs[which][out_c, i, j] = value
                    if j == 0:
                        yb_ref[out_c, i, pl.ds(2 * which, 1)] = value[:1]
                        yb_ref[out_c, i, pl.ds(2 * which + 1, 1)] = value[SIDE : SIDE + 1]
                    if i == 0 and which == 0:
                        xl_ref[out_c, j] = value[:SIDE]
        return carry

    lax.fori_loop(0, 3, component, 0)


def coeff_kernel(lame_ref, ctl_ref, material_ref, wz_ref, *outs):
    lane = lax.broadcasted_iota(jnp.int32, (ROWS, 128), 1)
    weight_z = wz_ref[...]
    for which in range(2):
        rows = [material_ref[b, ORDER[2 * which + k]][None] for k in range(2) for b in range(SIDE)]
        kind = jnp.concatenate(rows, 0).astype(F32)
        kind = jnp.concatenate([kind, jnp.zeros((ROWS, 128 - kind.shape[1]), F32)], 1)
        kind = lane_pick(kind, lane // N)
        for part in range(2):
            value = jnp.zeros((ROWS, 128), F32)
            for label in range(lame_ref.shape[1]):
                value = jnp.where(kind == float(label), lame_ref[part, label], value)
            value = value * weight_z
            for i in range(N):
                for j in range(N):
                    outs[2 * which + part][i, j] = value * float(WEIGHTS[i] * WEIGHTS[j])


def halo_corner_kernel(xr_ref, yb_ref, out_ref):
    row = lax.broadcasted_iota(jnp.int32, (SIDE, 128), 0)
    for n in range(6):
        for i in range(N):
            value = yb_ref[n, i]
            if i == DEG:
                value = jnp.where(row == 1, jnp.broadcast_to(xr_ref[n, 0][:1], (SIDE, 128)), value)
            out_ref[n, i] = value


def halo_kernel(xr_ref, yr_ref, *refs):
    fields, outs = refs[:4], refs[4:]
    row = lax.broadcasted_iota(jnp.int32, (ROWS, 128), 0)
    for n in range(2):
        for tile in range(2):
            src = fields[2 * n + tile]
            mid_ref, edge_ref = outs[2 * tile : 2 * tile + 2]
            dst = outs[4 + tile]

            def plane(j):
                for c in range(3):
                    for i in range(N):
                        value = src[c, i, j]
                        if tile == 0 and i == DEG:
                            face = xr_ref[3 * n + c, j]
                            value = jnp.where(row < SIDE, value, jnp.concatenate([face, face], 0))
                        if j is DEG:
                            face = yr_ref[3 * n + c, i]
                            first = jnp.broadcast_to(face[2 * tile : 2 * tile + 1], (ROWS, 128))
                            second = jnp.broadcast_to(face[2 * tile + 1 : 2 * tile + 2], (ROWS, 128))
                            value = jnp.where(row == SIDE - 1, first, jnp.where(row == ROWS - 1, second, value))
                        if n == 1:
                            dst[c, i, j] = value
                        elif isinstance(j, int):
                            edge_ref[c, i, j // DEG] = value
                        else:
                            mid_ref[c, i, j - 1] = value

            plane(0)
            loop(N - 2, lambda at: plane(at + 1), 1)
            plane(DEG)


def store_kernel(with_residual, *refs):
    refs = list(refs)
    take = lambda count: [refs.pop(0) for _ in range(count)]
    if with_residual:
        ctl_ref, b0_ref, b1_ref, face_ref, inner_ref, au_ref = take(6)
        faces = take(4)
        sums = (by_i(face_ref, inner_ref), whole(au_ref))
        loads = (whole(b0_ref), whole(b1_ref))
        parts = [
            lambda c, i, j, tile=tile: loads[tile](c, i, j) - sum_all(ctl_ref, faces, sums, c, c, i, j, tile)
            for tile in range(2)
        ]
    else:
        parts = [by_j(*take(2)) for tile in range(2)]
    out_ref, work_ref = refs
    nodes_x, width = out_ref.shape[1], out_ref.shape[2]
    nodes_z = width // nodes_x
    lane = lax.broadcasted_iota(jnp.int32, (ROWS, 128), 1)

    def component(c, carry):
        in_c = jnp.where(c == 2, 2, 1 - c)
        for i in range(DEG):
            for j in range(DEG):
                for which in range(2):
                    value = parts[which](in_c, i, j)
                    for k in range(2):
                        at = DEG * ORDER[2 * which + k] + i
                        work_ref[at, pl.ds(j, SIDE, stride=DEG)] = value[SIDE * k : SIDE * k + SIDE]
        for begin in range(0, width, 128):
            stop = min(begin + 128, width)
            for low, high in TILES:
                result = None
                for y in range(begin // nodes_z, (stop - 1) // nodes_z + 1):
                    node = jnp.clip(lane + (begin - nodes_z * y), 0, nodes_z - 1) + 1
                    got = lane_pick(work_ref[y, low:high], N * (node // DEG) + node % DEG)
                    result = got if result is None else jnp.where(lane + begin >= nodes_z * y, got, result)
                out_ref[c, low:high, begin:stop] = result[:, : stop - begin]
        return carry

    lax.fori_loop(0, 3, component, 0)


VM = pl.BlockSpec(memory_space=pltpu.VMEM)
SM = pl.BlockSpec(memory_space=pltpu.SMEM)
FIELD = (3, N, N, ROWS, 128)
MID = (3, N, N - 2, ROWS, 128)
EDGE = (3, N, 2, ROWS, 128)
FACE = (3, 2, N, ROWS, 128)
INNER = (3, N - 2, N, ROWS, 128)


def shape(dims):
    return jax.ShapeDtypeStruct(dims, F32)


def call(kernel, smem, inputs, outs, work=0, rows=FIELD):
    return pl.pallas_call(
        kernel,
        in_specs=[SM] * smem + [VM] * (len(inputs) - smem),
        out_specs=[VM] * len(outs),
        out_shape=[shape(dims) for dims in outs],
        scratch_shapes=[pltpu.VMEM(rows, F32)] * work,
        compiler_params=pltpu.CompilerParams(vmem_limit_bytes=6 << 20),
    )(*inputs)


def swaps(even, odd, axis):
    size = lax.axis_size(axis)
    got_odd = lax.ppermute(odd, axis, [(i, (((i + 1) ^ 1) - 1) % size) for i in range(size)])
    got_even = lax.ppermute(even, axis, [(i, i ^ 1) for i in range(size)])
    return got_even, got_odd


def exchange(ctl, x_faces, fields):
    xe, xo = swaps(*x_faces, "gy")
    ye, yo = call(corner_kernel, 0, (ctl, xe, xo, *fields), (xe.shape, xe.shape))
    ye, yo = swaps(ye, yo, "gx")
    return (xe, xo), (ye, yo)


def from_next(value, axis):
    size = lax.axis_size(axis)
    return lax.ppermute(value, axis, [(i, (i - 1) % size) for i in range(size)])


def local(right_side, guess, material, lame, upper, lower_ratio):
    elems_x, elems_y, elems_z = material.shape
    nodes_y = DEG * elems_y
    w_grad, w_back, w_share = z_matrices(elems_z)
    w_grad = jnp.asarray(w_grad, BF16)
    w_back = jnp.asarray(w_back, BF16)
    w_share = jnp.asarray(w_share, BF16)
    upper_edge = upper[0]
    lower_edge = lower_ratio[0] * upper_edge
    center = (upper_edge + lower_edge) / 2.0
    radius = (upper_edge - lower_edge) / 2.0
    sigma_ratio = center / radius
    pairs = [(jnp.zeros((), F32), 1.0 / center)]
    factor = 1.0 / sigma_ratio
    for step_index in range(CHEB - 1):
        factor_next = 1.0 / (2.0 * sigma_ratio - factor)
        pairs.append((factor_next * factor, 2.0 * factor_next / radius))
        factor = factor_next
    flags = [(lax.axis_index(axis) % 2).astype(F32) for axis in ("gy", "gx")]
    ctl = jnp.stack(flags + [value for pair in pairs for value in pair])
    ctl = jnp.broadcast_to(ctl[:, None, None], (2 + 2 * CHEB, ROWS, 128))
    grid = (N, N, ROWS, 128)
    weight_z = jnp.asarray(np.tile(WEIGHTS, (ROWS, elems_z)), F32)
    coeffs = call(coeff_kernel, 1, (lame, ctl, material, weight_z), (grid,) * 4)
    coeffs = [coeffs[:2], coeffs[2:]]

    plane = (3, N, SIDE, 128)
    staged = (nodes_y + 1, nodes_y + SIDE, 128)
    loads = [call(load_kernel, 0, (ctl, value), (FIELD, FIELD, plane, plane), 1, staged) for value in (guess, right_side)]
    x_halo = from_next(jnp.concatenate([load[2] for load in loads], 0), "gy")
    y_halo = jnp.concatenate([load[3] for load in loads], 0)
    (y_halo,) = call(halo_corner_kernel, 0, (x_halo, y_halo), (y_halo.shape,))
    y_halo = from_next(y_halo, "gx")
    *nodes, b0, b1 = call(
        halo_kernel, 0, (x_halo, y_halo, *loads[0][:2], *loads[1][:2]), (MID, EDGE, MID, EDGE, FIELD, FIELD)
    )
    u_mid = [nodes[0], nodes[2]]
    u_edge = [nodes[1], nodes[3]]
    b = [b0, b1]

    ratio_z = jnp.asarray(np.tile(RATIO, (ROWS, elems_z)), F32)
    ratio_i = jnp.asarray(np.broadcast_to(RATIO[:, None, None], (N, ROWS, 128)), F32)
    weights = (w_grad, w_back, w_share)
    work = (FIELD,) * 3
    both_faces = ((6, N, SIDE, 128),) * 2

    def first(tile, extra, outs, scratch):
        inputs = (ctl, u_mid[tile], u_edge[tile], *coeffs[tile], ratio_i, ratio_z, *weights, *extra)
        return call(lambda *refs: first_kernel(tile, *refs), 0, inputs, (FIELD,) + outs, scratch)

    diag_0, face, *rest = first(0, (), (FACE, *both_faces, *work), 0)
    x_faces, work_0 = rest[:2], rest[2:]
    diag_1, inner, au = first(1, work_0, (INNER, FIELD), 3)
    diag = (diag_0, diag_1)
    change_mid = [None, None]
    change_edge = [None, None]
    inv_mid = [None, None]
    inv_edge = [None, None]
    for count in range(SWEEPS * CHEB):
        stage = count % CHEB
        with_diag = count == 0
        sums = (face, inner, au)
        x_got, y_got = exchange(ctl, x_faces, sums + (diag if with_diag else ()))
        keep_inv = 1 if with_diag else 0

        inputs = (ctl, w_grad, *sums, *x_got) + (diag if with_diag else ())
        for tile in range(2):
            inputs += (u_mid[tile], b[tile]) + (() if with_diag else (inv_mid[tile],))
            inputs += (change_mid[tile],) if stage else ()
        outs = (MID,) * (4 + keep_inv) * 2
        results = call(lambda *refs: mid_kernel(stage, with_diag, *refs), 0, inputs, outs)
        slopes = [None, None]
        for tile in range(2):
            got = results[(4 + keep_inv) * tile : (4 + keep_inv) * (tile + 1)]
            u_mid[tile], change_mid[tile] = got[:2]
            slopes[tile] = got[2:4]
            if with_diag:
                inv_mid[tile] = got[4]

        for tile in range(2):
            inputs = (ctl, *weights, *coeffs[tile], *sums, *x_got, *y_got) + (diag if with_diag else ())
            inputs += (u_mid[tile], *slopes[tile], u_edge[tile], b[tile])
            inputs += () if with_diag else (inv_edge[tile],)
            inputs += (change_edge[tile],) if stage else ()
            inputs += tuple(work_0) if tile else ()
            outs = (EDGE,) * (2 + keep_inv)
            outs += (INNER, FIELD) if tile else (FACE, *((3, N, SIDE, 128),) * 2, *work)
            results = list(
                call(lambda *refs: edge_kernel(tile, stage, with_diag, *refs), 0, inputs, outs, 3 if tile else 0)
            )
            u_edge[tile], change_edge[tile] = results[:2]
            if with_diag:
                inv_edge[tile] = results[2]
            results = results[2 + keep_inv :]
            if tile:
                inner, au = results
            else:
                face, x_faces, work_0 = results[0], results[1:3], results[3:]
    sums = (face, inner, au)
    x_got, y_got = exchange(ctl, x_faces, sums)

    def store(with_residual, inputs):
        return call(lambda *refs: store_kernel(with_residual, *refs), 0, inputs, (guess.shape,), 1, staged)[0]

    smoothed = store(False, (u_mid[0], u_edge[0], u_mid[1], u_edge[1]))
    return (smoothed, store(True, (ctl, *b, *sums, *x_got, *y_got)))


def solution(mesh):
    placed = (P(None, "gx", "gy"), P(None, "gx", "gy"), P("gx", "gy", None), P(), P(), P())
    return jax.shard_map(
        local,
        mesh=mesh,
        in_specs=placed,
        out_specs=(P(None, "gx", "gy"), P(None, "gx", "gy")),
        check_vma=False,
    )
```

time: 193 us -> 174 us (0.902)
  Pallas kernels: 76.4 us -> 64.6 us
  starting transfers between devices: 72.5 us -> 66.8 us
    pallas_call x29 -> x34, Pallas kernels: 76.4 us -> 64.6 us  [call(): pl.pallas_call(kernel, in_specs=[SM] * smem + [VM] * (len(inputs) - smem)...]
    ppermute x14, starting transfers between devices: 60.3 us -> 54.5 us  [swaps(): lax.ppermute(odd, axis, [(i, ((i + 1 ^ 1) - 1) % size) for i in range(siz...]
  transfers between devices with their start and end apart: 30 -> 30, of which waited for: 15 -> 15; matrix products, arithmetic and copies ran while one was open for 0% -> 0% of each run, Pallas kernels for 17% -> 24%
where the time goes in v2:
time: 174 us
  starting transfers between devices  66.8 us (38%)
  Pallas kernels  64.6 us (37%)
  waiting for transfers between devices  38 us (22%)
  between operations  2.61 us (2%)
  local copies, waits for them, and re-layouts  1.92 us (1%)
    pallas_call x34, Pallas kernels, call(): pl.pallas_call(kernel, in_specs=[SM] * smem + [VM] * (len(inputs) - smem)...  64.6 us
    ppermute x14, starting transfers between devices, swaps(): lax.ppermute(odd, axis, [(i, ((i + 1 ^ 1) - 1) % size) for i in range(siz...  54.5 us
    ppermute x14, waiting for transfers between devices, swaps(): lax.ppermute(odd, axis, [(i, ((i + 1 ^ 1) - 1) % size) for i in range(siz...  33.5 us
    ppermute x2, starting transfers between devices, from_next(): return lax.ppermute(value, axis, [(i, (i - 1) % size) for i in range(size)])  11 us
    ppermute x2, waiting for transfers between devices, from_next(): return lax.ppermute(value, axis, [(i, (i - 1) % size) for i in range(size)])  4.38 us
  transfers between devices with their start and end apart: 30, of which 15 were waited for; matrix products, arithmetic and copies ran while one was open for 0% of the time, Pallas kernels for 24%

profile of v2, /device:TPU:0, one launch (start us, length us, event | category | flops | bytes accessed | tf_op | source)
XLA Modules:
  0.0 173.9 jit_solution(5449214720192428800)
XLA Ops:
  6.3 7.4 %collective-permute-start = (f32[6,8,4,128]{3,2,1,0:T(4,128)S(1)}, f32[6,8,4,128]{3,2,1,0:T(4,128)S(1)}, u32[]{:S(2)}, u32[]{:S(2)}) collective-permute-start(f32[6,8,4,128]{3,2,1,0:T(4,128)S(1)} %pad_maximum_fusion), channel_id=1, source_target_pairs={{0,15},{1,0},{2,1},{3,2},{4,3},{5,4},{6,5},{7,6},{8,7},{9,8},{10,9... | collective-permute-start | bytes 294920 | tf_op jit(solution)/shard_map/ppermute | solution.py:637
  16.7 3.5 %collective-permute-start.1 = (f32[6,8,4,128]{3,2,1,0:T(4,128)S(1)}, f32[6,8,4,128]{3,2,1,0:T(4,128)S(1)}, u32[]{:S(2)}, u32[]{:S(2)}) collective-permute-start(f32[6,8,4,128]{3,2,1,0:T(4,128)S(1)} %shard_map.134), channel_id=1, source_target_pairs={{0,240},{16,0},{32,16},{48,32},{64,48},{80,64},{96,80},{112,96},{1... | collective-permute-start | bytes 294920 | tf_op jit(solution)/shard_map/ppermute | solution.py:637
  23.4 3.8 %shard_map.136 = (f32[3,8,8,8,128]{4,3,2,1,0:T(8,128)S(1)}, f32[3,2,8,8,128]{4,3,2,1,0:T(8,128)S(1)}, f32[6,8,4,128]{3,2,1,0:T(4,128)S(1)}, f32[6,8,4,128]{3,2,1...) custom-call(f32[8,8,128]{2,1,0:T(8,128)S(1)} %broadcast_in_dim.2.ctl, ...), custom_call_target="tpu_custom_call" | custom-call | tf_op jit(solution)/shard_map/pallas_call | solution.py:611
  27.3 7.2 %collective-permute-start.3 = (f32[6,8,4,128]{3,2,1,0:T(4,128)S(1)}, f32[6,8,4,128]{3,2,1,0:T(4,128)S(1)}, u32[]{:S(2)}, u32[]{:S(2)}) collective-permute-start(f32[6,8,4,128]{3,2,1,0:T(4,128)S(1)} %get-tuple-element.183), channel_id=1, source_target_pairs={{0,15},{1,2},{2,1},{3,4},{4,3},{5,6},{6,5},{7,8},{8,7},{9,10},{10,... | collective-permute-start | bytes 294920 | tf_op jit(solution)/shard_map/ppermute | solution.py:623
  34.4 5.3 %shard_map.137 = (f32[3,8,8,8,128]{4,3,2,1,0:T(8,128)S(1)}, f32[3,6,8,8,128]{4,3,2,1,0:T(8,128)S(1)}, f32[3,8,8,8,128]{4,3,2,1,0:T(8,128)S(1)}) custom-call(f32[8,8,128]{2,1,0:T(8,128)S(1)} %broadcast_in_dim.2.ctl_ref.refs_0_, f32[3,8,6,8,128]{4,3,2,1,0:T(8,128)S(1)} %get-tuple-element.173.refs_1_.refs_11_, ...), custom_call_target="tpu_custom_call" | custom-call | tf_op jit(solution)/shard_map/pallas_call | solution.py:611
  40.0 6.1 %collective-permute-start.5 = (f32[6,8,4,128]{3,2,1,0:T(4,128)S(1)}, f32[6,8,4,128]{3,2,1,0:T(4,128)S(1)}, u32[]{:S(2)}, u32[]{:S(2)}) collective-permute-start(f32[6,8,4,128]{3,2,1,0:T(4,128)S(1)} %get-tuple-element.187), channel_id=1, source_target_pairs={{0,240},{16,32},{32,16},{48,64},{64,48},{80,96},{96,80},{112,128},... | collective-permute-start | bytes 294920 | tf_op jit(solution)/shard_map/ppermute | solution.py:623
  51.7 4.6 %collective-permute-start.7 = (f32[3,8,4,128]{3,2,1,0:T(4,128)S(1)}, f32[3,8,4,128]{3,2,1,0:T(4,128)S(1)}, u32[]{:S(2)}, u32[]{:S(2)}) collective-permute-start(f32[3,8,4,128]{3,2,1,0:T(4,128)S(1)} %get-tuple-element.203), channel_id=1, source_target_pairs={{0,15},{1,2},{2,1},{3,4},{4,3},{5,6},{6,5},{7,8},{8,7},{9,10},{10,... | collective-permute-start | bytes 147464 | tf_op jit(solution)/shard_map/ppermute | solution.py:623
  56.3 3.4 %shard_map.141 = (f32[3,8,2,8,128]{4,3,2,1,0:T(8,128)S(1)}, f32[3,8,2,8,128]{4,3,2,1,0:T(8,128)S(1)}, f32[3,8,2,8,128]{4,3,2,1,0:T(8,128)S(1)}, f32[3,6,8,8,128]{4,3,2,1,0:T(8,128)S(1)}, f32[3,8,8,8,128]{4,3,2,1,0:T(8,128)S(1)}) custom-call(f32[8,8,128]{2,1,0:T(8,128)S(1)} %broadcast_in_dim.2.ctl_ref.refs_0_, bf16[256,256]{1,0:T(8,128)(2,1)S(1)} %copy-done, ...), custom_call_target="tpu_custom_call" | custom-call | tf_op jit(solution)/shard_map/pallas_call | solution.py:611
  61.5 5.1 %collective-permute-start.9 = (f32[3,8,4,128]{3,2,1,0:T(4,128)S(1)}, f32[3,8,4,128]{3,2,1,0:T(4,128)S(1)}, u32[]{:S(2)}, u32[]{:S(2)}) collective-permute-start(f32[3,8,4,128]{3,2,1,0:T(4,128)S(1)} %get-tuple-element.205), channel_id=1, source_target_pairs={{0,240},{16,32},{32,16},{48,64},{64,48},{80,96},{96,80},{112,128},... | collective-permute-start | bytes 147464 | tf_op jit(solution)/shard_map/ppermute | solution.py:623
  71.7 3.5 %collective-permute-start.11 = (f32[3,8,4,128]{3,2,1,0:T(4,128)S(1)}, f32[3,8,4,128]{3,2,1,0:T(4,128)S(1)}, u32[]{:S(2)}, u32[]{:S(2)}) collective-permute-start(f32[3,8,4,128]{3,2,1,0:T(4,128)S(1)} %get-tuple-element.229), channel_id=1, source_target_pairs={{0,15},{1,2},{2,1},{3,4},{4,3},{5,6},{6,5},{7,8},{8,7},{9,10},{10,... | collective-permute-start | bytes 147464 | tf_op jit(solution)/shard_map/ppermute | solution.py:623
  75.2 3.4 %shard_map.145 = (f32[3,8,2,8,128]{4,3,2,1,0:T(8,128)S(1)}, f32[3,8,2,8,128]{4,3,2,1,0:T(8,128)S(1)}, f32[3,6,8,8,128]{4,3,2,1,0:T(8,128)S(1)}, f32[3,8,8,8,128]{4,3,2,1,0:T(8,128)S(1)}) custom-call(f32[8,8,128]{2,1,0:T(8,128)S(1)} %broadcast_in_dim.2.ctl_ref.refs_0_, bf16[256,256]{1,0:T(8,128)(2,1)S(1)} %copy-done, bf16[256,256]{1,0:T(8,128)(2,1)S(1)} %copy-done.1, ...), custom_call_target="tpu_custom_call" | custom-call | tf_op jit(solution)/shard_map/pallas_call | solution.py:611
  78.5 3.3 %collective-permute-done.11.xo_ref.refs_6_.refs_10_ = f32[3,8,4,128]{3,2,1,0:T(4,128)S(1)} collective-permute-done((f32[3,8,4,128]{3,2,1,0:T(4,128)S(1)}, f32[3,8,4,128]{3,2,1,0:T(4,128)S(1)}, u32[]{:S(2)}, u32[]{:S(2)}) %collective-permute-start.11) | collective-permute-done | bytes 49184 | tf_op jit(solution)/shard_map/ppermute | solution.py:623
  82.0 5.0 %collective-permute-start.13 = (f32[3,8,4,128]{3,2,1,0:T(4,128)S(1)}, f32[3,8,4,128]{3,2,1,0:T(4,128)S(1)}, u32[]{:S(2)}, u32[]{:S(2)}) collective-permute-start(f32[3,8,4,128]{3,2,1,0:T(4,128)S(1)} %get-tuple-element.231), channel_id=1, source_target_pairs={{0,240},{16,32},{32,16},{48,64},{64,48},{80,96},{96,80},{112,128},... | collective-permute-start | bytes 147464 | tf_op jit(solution)/shard_map/ppermute | solution.py:623
  95.3 4.0 %shard_map.149 = (f32[3,8,2,8,128]{4,3,2,1,0:T(8,128)S(1)}, f32[3,8,2,8,128]{4,3,2,1,0:T(8,128)}, f32[3,6,8,8,128]{4,3,2,1,0:T(8,128)S(1)}, f32[3,8,8,8,128]{4,3,2,1,0:T(8,128)S(1)}) custom-call(f32[8,8,128]{2,1,0:T(8,128)S(1)} %broadcast_in_dim.2.ctl_ref.refs_0_, bf16[256,256]{1,0:T(8,128)(2,1)S(1)} %copy-done, bf16[256,256]{1,0:T(8,128)(2,1)S(1)} %copy-done.1, ...), custom_call_target="tpu_custom_call" | custom-call | tf_op jit(solution)/shard_map/pallas_call | solution.py:611
  102.7 4.6 %collective-permute-start.17 = (f32[3,8,4,128]{3,2,1,0:T(4,128)S(1)}, f32[3,8,4,128]{3,2,1,0:T(4,128)S(1)}, u32[]{:S(2)}, u32[]{:S(2)}) collective-permute-start(f32[3,8,4,128]{3,2,1,0:T(4,128)S(1)} %get-tuple-element.253), channel_id=1, source_target_pairs={{0,240},{16,32},{32,16},{48,64},{64,48},{80,96},{96,80},{112,128},... | collective-permute-start | bytes 147464 | tf_op jit(solution)/shard_map/ppermute | solution.py:623
  113.9 3.4 %shard_map.153 = (f32[3,8,2,8,128]{4,3,2,1,0:T(8,128)S(1)}, f32[3,8,2,8,128]{4,3,2,1,0:T(8,128)S(1)}, f32[3,6,8,8,128]{4,3,2,1,0:T(8,128)S(1)}, f32[3,8,8,8,128]{4,3,2,1,0:T(8,128)S(1)}) custom-call(f32[8,8,128]{2,1,0:T(8,128)S(1)} %broadcast_in_dim.2.ctl_ref.refs_0_, bf16[256,256]{1,0:T(8,128)(2,1)S(1)} %copy-done, bf16[256,256]{1,0:T(8,128)(2,1)S(1)} %copy-done.1, ...), custom_call_target="tpu_custom_call" | custom-call | tf_op jit(solution)/shard_map/pallas_call | solution.py:611
  117.3 5.2 %collective-permute-done.19.xo_ref.refs_6_.refs_10_ = f32[3,8,4,128]{3,2,1,0:T(4,128)S(1)} collective-permute-done((f32[3,8,4,128]{3,2,1,0:T(4,128)S(1)}, f32[3,8,4,128]{3,2,1,0:T(4,128)S(1)}, u32[]{:S(2)}, u32[]{:S(2)}) %collective-permute-start.19) | collective-permute-done | bytes 49184 | tf_op jit(solution)/shard_map/ppermute | solution.py:623
  122.9 4.5 %collective-permute-start.21 = (f32[3,8,4,128]{3,2,1,0:T(4,128)S(1)}, f32[3,8,4,128]{3,2,1,0:T(4,128)S(1)}, u32[]{:S(2)}, u32[]{:S(2)}) collective-permute-start(f32[3,8,4,128]{3,2,1,0:T(4,128)S(1)} %get-tuple-element.271), channel_id=1, source_target_pairs={{0,240},{16,32},{32,16},{48,64},{64,48},{80,96},{96,80},{112,128},... | collective-permute-start | bytes 147464 | tf_op jit(solution)/shard_map/ppermute | solution.py:623
  133.3 3.4 %shard_map.157 = (f32[3,8,2,8,128]{4,3,2,1,0:T(8,128)S(1)}, f32[3,8,2,8,128]{4,3,2,1,0:T(8,128)S(1)}, f32[3,6,8,8,128]{4,3,2,1,0:T(8,128)S(1)}, f32[3,8,8,8,128]{4,3,2,1,0:T(8,128)S(1)}) custom-call(f32[8,8,128]{2,1,0:T(8,128)S(1)} %broadcast_in_dim.2.ctl_ref.refs_0_, bf16[256,256]{1,0:T(8,128)(2,1)S(1)} %copy-done, bf16[256,256]{1,0:T(8,128)(2,1)S(1)} %copy-done.1, ...), custom_call_target="tpu_custom_call" | custom-call | tf_op jit(solution)/shard_map/pallas_call | solution.py:611
  136.7 5.8 %collective-permute-done.23.refs_6_.xo_ref.refs_10_ = f32[3,8,4,128]{3,2,1,0:T(4,128)S(1)} collective-permute-done((f32[3,8,4,128]{3,2,1,0:T(4,128)S(1)}, f32[3,8,4,128]{3,2,1,0:T(4,128)S(1)}, u32[]{:S(2)}, u32[]{:S(2)}) %collective-permute-start.23) | collective-permute-done | bytes 49184 | tf_op jit(solution)/shard_map/ppermute | solution.py:623
  142.6 4.5 %collective-permute-start.25 = (f32[3,8,4,128]{3,2,1,0:T(4,128)S(1)}, f32[3,8,4,128]{3,2,1,0:T(4,128)S(1)}, u32[]{:S(2)}, u32[]{:S(2)}) collective-permute-start(f32[3,8,4,128]{3,2,1,0:T(4,128)S(1)} %get-tuple-element.296), channel_id=1, source_target_pairs={{0,240},{16,32},{32,16},{48,64},{64,48},{80,96},{96,80},{112,128},... | collective-permute-start | bytes 147464 | tf_op jit(solution)/shard_map/ppermute | solution.py:623
  153.7 4.0 %shard_map.161 = (f32[3,8,2,8,128]{4,3,2,1,0:T(8,128)S(1)}, f32[3,8,2,8,128]{4,3,2,1,0:T(8,128)}, f32[3,6,8,8,128]{4,3,2,1,0:T(8,128)S(1)}, f32[3,8,8,8,128]{4,3,2,1,0:T(8,128)S(1)}) custom-call(f32[8,8,128]{2,1,0:T(8,128)S(1)} %broadcast_in_dim.2.ctl_ref.refs_0_, bf16[256,256]{1,0:T(8,128)(2,1)S(1)} %copy-done, bf16[256,256]{1,0:T(8,128)(2,1)S(1)} %copy-done.1, ...), custom_call_target="tpu_custom_call" | custom-call | tf_op jit(solution)/shard_map/pallas_call | solution.py:611
  157.7 5.1 %collective-permute-done.27.xo_ref.refs_7_ = f32[3,8,4,128]{3,2,1,0:T(4,128)S(1)} collective-permute-done((f32[3,8,4,128]{3,2,1,0:T(4,128)S(1)}, f32[3,8,4,128]{3,2,1,0:T(4,128)S(1)}, u32[]{:S(2)}, u32[]{:S(2)}) %collective-permute-start.27) | collective-permute-done | bytes 49184 | tf_op jit(solution)/shard_map/ppermute | solution.py:623
  163.0 4.5 %collective-permute-start.29 = (f32[3,8,4,128]{3,2,1,0:T(4,128)S(1)}, f32[3,8,4,128]{3,2,1,0:T(4,128)S(1)}, u32[]{:S(2)}, u32[]{:S(2)}) collective-permute-start(f32[3,8,4,128]{3,2,1,0:T(4,128)S(1)} %get-tuple-element.317), channel_id=1, source_target_pairs={{0,240},{16,32},{32,16},{48,64},{64,48},{80,96},{96,80},{112,128},... | collective-permute-start | bytes 147464 | tf_op jit(solution)/shard_map/ppermute | solution.py:623
  (94 shorter events, 60.7 us)
Async XLA Ops:
  6.3 10.4 %collective-permute-start = (f32[6,8,4,128]{3,2,1,0:T(4,128)S(1)}, f32[6,8,4,128]{3,2,1,0:T(4,128)S(1)}, u32[]{:S(2)}, u32[]{:S(2)}) collective-permute-start(f32[6,8,4,128]{3,2,1,0:T(4,128)S(1)} %pad_maximum_fusion), channel_id=1, source_target_pairs={{0,15},{1,0},{2,1},{3,2},{4,3},{5,4},{6,5},{7,6},{8,7},{9,8},{10,9... | collective-permute-start | bytes 294920 | tf_op jit(solution)/shard_map/ppermute | solution.py:637
  27.2 12.6 %collective-permute-start.2 = (f32[6,8,4,128]{3,2,1,0:T(4,128)S(1)}, f32[6,8,4,128]{3,2,1,0:T(4,128)S(1)}, u32[]{:S(2)}, u32[]{:S(2)}) collective-permute-start(f32[6,8,4,128]{3,2,1,0:T(4,128)S(1)} %get-tuple-element.182), channel_id=1, source_target_pairs={{0,1},{1,0},{2,3},{3,2},{4,5},{5,4},{6,7},{7,6},{8,9},{9,8},{10,11... | collective-permute-start | bytes 294920 | tf_op jit(solution)/shard_map/ppermute | solution.py:624
  27.3 12.5 %collective-permute-start.3 = (f32[6,8,4,128]{3,2,1,0:T(4,128)S(1)}, f32[6,8,4,128]{3,2,1,0:T(4,128)S(1)}, u32[]{:S(2)}, u32[]{:S(2)}) collective-permute-start(f32[6,8,4,128]{3,2,1,0:T(4,128)S(1)} %get-tuple-element.183), channel_id=1, source_target_pairs={{0,15},{1,2},{2,1},{3,4},{4,3},{5,6},{6,5},{7,8},{8,7},{9,10},{10,... | collective-permute-start | bytes 294920 | tf_op jit(solution)/shard_map/ppermute | solution.py:623
  39.9 8.0 %collective-permute-start.4 = (f32[6,8,4,128]{3,2,1,0:T(4,128)S(1)}, f32[6,8,4,128]{3,2,1,0:T(4,128)S(1)}, u32[]{:S(2)}, u32[]{:S(2)}) collective-permute-start(f32[6,8,4,128]{3,2,1,0:T(4,128)S(1)} %get-tuple-element.186), channel_id=1, source_target_pairs={{0,16},{16,0},{32,48},{48,32},{64,80},{80,64},{96,112},{112,96},{1... | collective-permute-start | bytes 294920 | tf_op jit(solution)/shard_map/ppermute | solution.py:624
  40.0 9.7 %collective-permute-start.5 = (f32[6,8,4,128]{3,2,1,0:T(4,128)S(1)}, f32[6,8,4,128]{3,2,1,0:T(4,128)S(1)}, u32[]{:S(2)}, u32[]{:S(2)}) collective-permute-start(f32[6,8,4,128]{3,2,1,0:T(4,128)S(1)} %get-tuple-element.187), channel_id=1, source_target_pairs={{0,240},{16,32},{32,16},{48,64},{64,48},{80,96},{96,80},{112,128},... | collective-permute-start | bytes 294920 | tf_op jit(solution)/shard_map/ppermute | solution.py:623
  51.6 8.2 %collective-permute-start.6 = (f32[3,8,4,128]{3,2,1,0:T(4,128)S(1)}, f32[3,8,4,128]{3,2,1,0:T(4,128)S(1)}, u32[]{:S(2)}, u32[]{:S(2)}) collective-permute-start(f32[3,8,4,128]{3,2,1,0:T(4,128)S(1)} %get-tuple-element.202), channel_id=1, source_target_pairs={{0,1},{1,0},{2,3},{3,2},{4,5},{5,4},{6,7},{7,6},{8,9},{9,8},{10,11... | collective-permute-start | bytes 147464 | tf_op jit(solution)/shard_map/ppermute | solution.py:624
  51.7 9.6 %collective-permute-start.7 = (f32[3,8,4,128]{3,2,1,0:T(4,128)S(1)}, f32[3,8,4,128]{3,2,1,0:T(4,128)S(1)}, u32[]{:S(2)}, u32[]{:S(2)}) collective-permute-start(f32[3,8,4,128]{3,2,1,0:T(4,128)S(1)} %get-tuple-element.203), channel_id=1, source_target_pairs={{0,15},{1,2},{2,1},{3,4},{4,3},{5,6},{6,5},{7,8},{8,7},{9,10},{10,... | collective-permute-start | bytes 147464 | tf_op jit(solution)/shard_map/ppermute | solution.py:623
  61.4 6.9 %collective-permute-start.8 = (f32[3,8,4,128]{3,2,1,0:T(4,128)S(1)}, f32[3,8,4,128]{3,2,1,0:T(4,128)S(1)}, u32[]{:S(2)}, u32[]{:S(2)}) collective-permute-start(f32[3,8,4,128]{3,2,1,0:T(4,128)S(1)} %get-tuple-element.204), channel_id=1, source_target_pairs={{0,16},{16,0},{32,48},{48,32},{64,80},{80,64},{96,112},{112,96},{1... | collective-permute-start | bytes 147464 | tf_op jit(solution)/shard_map/ppermute | solution.py:624
  61.5 8.3 %collective-permute-start.9 = (f32[3,8,4,128]{3,2,1,0:T(4,128)S(1)}, f32[3,8,4,128]{3,2,1,0:T(4,128)S(1)}, u32[]{:S(2)}, u32[]{:S(2)}) collective-permute-start(f32[3,8,4,128]{3,2,1,0:T(4,128)S(1)} %get-tuple-element.205), channel_id=1, source_target_pairs={{0,240},{16,32},{32,16},{48,64},{64,48},{80,96},{96,80},{112,128},... | collective-permute-start | bytes 147464 | tf_op jit(solution)/shard_map/ppermute | solution.py:623
  71.6 7.0 %collective-permute-start.10 = (f32[3,8,4,128]{3,2,1,0:T(4,128)S(1)}, f32[3,8,4,128]{3,2,1,0:T(4,128)S(1)}, u32[]{:S(2)}, u32[]{:S(2)}) collective-permute-start(f32[3,8,4,128]{3,2,1,0:T(4,128)S(1)} %get-tuple-element.228), channel_id=1, source_target_pairs={{0,1},{1,0},{2,3},{3,2},{4,5},{5,4},{6,7},{7,6},{8,9},{9,8},{10,11... | collective-permute-start | bytes 147464 | tf_op jit(solution)/shard_map/ppermute | solution.py:624
  71.7 10.2 %collective-permute-start.11 = (f32[3,8,4,128]{3,2,1,0:T(4,128)S(1)}, f32[3,8,4,128]{3,2,1,0:T(4,128)S(1)}, u32[]{:S(2)}, u32[]{:S(2)}) collective-permute-start(f32[3,8,4,128]{3,2,1,0:T(4,128)S(1)} %get-tuple-element.229), channel_id=1, source_target_pairs={{0,15},{1,2},{2,1},{3,4},{4,3},{5,6},{6,5},{7,8},{8,7},{9,10},{10,... | collective-permute-start | bytes 147464 | tf_op jit(solution)/shard_map/ppermute | solution.py:623
  81.9 7.7 %collective-permute-start.12 = (f32[3,8,4,128]{3,2,1,0:T(4,128)S(1)}, f32[3,8,4,128]{3,2,1,0:T(4,128)S(1)}, u32[]{:S(2)}, u32[]{:S(2)}) collective-permute-start(f32[3,8,4,128]{3,2,1,0:T(4,128)S(1)} %get-tuple-element.230), channel_id=1, source_target_pairs={{0,16},{16,0},{32,48},{48,32},{64,80},{80,64},{96,112},{112,96},{1... | collective-permute-start | bytes 147464 | tf_op jit(solution)/shard_map/ppermute | solution.py:624
  82.0 8.1 %collective-permute-start.13 = (f32[3,8,4,128]{3,2,1,0:T(4,128)S(1)}, f32[3,8,4,128]{3,2,1,0:T(4,128)S(1)}, u32[]{:S(2)}, u32[]{:S(2)}) collective-permute-start(f32[3,8,4,128]{3,2,1,0:T(4,128)S(1)} %get-tuple-element.231), channel_id=1, source_target_pairs={{0,240},{16,32},{32,16},{48,64},{64,48},{80,96},{96,80},{112,128},... | collective-permute-start | bytes 147464 | tf_op jit(solution)/shard_map/ppermute | solution.py:623
  92.6 6.8 %collective-permute-start.14 = (f32[3,8,4,128]{3,2,1,0:T(4,128)S(1)}, f32[3,8,4,128]{3,2,1,0:T(4,128)S(1)}, u32[]{:S(2)}, u32[]{:S(2)}) collective-permute-start(f32[3,8,4,128]{3,2,1,0:T(4,128)S(1)} %get-tuple-element.250), channel_id=1, source_target_pairs={{0,1},{1,0},{2,3},{3,2},{4,5},{5,4},{6,7},{7,6},{8,9},{9,8},{10,11... | collective-permute-start | bytes 147464 | tf_op jit(solution)/shard_map/ppermute | solution.py:624
  92.6 10.0 %collective-permute-start.15 = (f32[3,8,4,128]{3,2,1,0:T(4,128)S(1)}, f32[3,8,4,128]{3,2,1,0:T(4,128)S(1)}, u32[]{:S(2)}, u32[]{:S(2)}) collective-permute-start(f32[3,8,4,128]{3,2,1,0:T(4,128)S(1)} %get-tuple-element.251), channel_id=1, source_target_pairs={{0,15},{1,2},{2,1},{3,4},{4,3},{5,6},{6,5},{7,8},{8,7},{9,10},{10,... | collective-permute-start | bytes 147464 | tf_op jit(solution)/shard_map/ppermute | solution.py:623
  102.7 8.1 %collective-permute-start.17 = (f32[3,8,4,128]{3,2,1,0:T(4,128)S(1)}, f32[3,8,4,128]{3,2,1,0:T(4,128)S(1)}, u32[]{:S(2)}, u32[]{:S(2)}) collective-permute-start(f32[3,8,4,128]{3,2,1,0:T(4,128)S(1)} %get-tuple-element.253), channel_id=1, source_target_pairs={{0,240},{16,32},{32,16},{48,64},{64,48},{80,96},{96,80},{112,128},... | collective-permute-start | bytes 147464 | tf_op jit(solution)/shard_map/ppermute | solution.py:623
  112.7 9.7 %collective-permute-start.19 = (f32[3,8,4,128]{3,2,1,0:T(4,128)S(1)}, f32[3,8,4,128]{3,2,1,0:T(4,128)S(1)}, u32[]{:S(2)}, u32[]{:S(2)}) collective-permute-start(f32[3,8,4,128]{3,2,1,0:T(4,128)S(1)} %get-tuple-element.269), channel_id=1, source_target_pairs={{0,15},{1,2},{2,1},{3,4},{4,3},{5,6},{6,5},{7,8},{8,7},{9,10},{10,... | collective-permute-start | bytes 147464 | tf_op jit(solution)/shard_map/ppermute | solution.py:623
  122.9 8.1 %collective-permute-start.21 = (f32[3,8,4,128]{3,2,1,0:T(4,128)S(1)}, f32[3,8,4,128]{3,2,1,0:T(4,128)S(1)}, u32[]{:S(2)}, u32[]{:S(2)}) collective-permute-start(f32[3,8,4,128]{3,2,1,0:T(4,128)S(1)} %get-tuple-element.271), channel_id=1, source_target_pairs={{0,240},{16,32},{32,16},{48,64},{64,48},{80,96},{96,80},{112,128},... | collective-permute-start | bytes 147464 | tf_op jit(solution)/shard_map/ppermute | solution.py:623
  132.9 9.6 %collective-permute-start.23 = (f32[3,8,4,128]{3,2,1,0:T(4,128)S(1)}, f32[3,8,4,128]{3,2,1,0:T(4,128)S(1)}, u32[]{:S(2)}, u32[]{:S(2)}) collective-permute-start(f32[3,8,4,128]{3,2,1,0:T(4,128)S(1)} %get-tuple-element.291), channel_id=1, source_target_pairs={{0,15},{1,2},{2,1},{3,4},{4,3},{5,6},{6,5},{7,8},{8,7},{9,10},{10,... | collective-permute-start | bytes 147464 | tf_op jit(solution)/shard_map/ppermute | solution.py:623
  142.5 7.2 %collective-permute-start.24 = (f32[3,8,4,128]{3,2,1,0:T(4,128)S(1)}, f32[3,8,4,128]{3,2,1,0:T(4,128)S(1)}, u32[]{:S(2)}, u32[]{:S(2)}) collective-permute-start(f32[3,8,4,128]{3,2,1,0:T(4,128)S(1)} %get-tuple-element.295), channel_id=1, source_target_pairs={{0,16},{16,0},{32,48},{48,32},{64,80},{80,64},{96,112},{112,96},{1... | collective-permute-start | bytes 147464 | tf_op jit(solution)/shard_map/ppermute | solution.py:624
  142.6 8.1 %collective-permute-start.25 = (f32[3,8,4,128]{3,2,1,0:T(4,128)S(1)}, f32[3,8,4,128]{3,2,1,0:T(4,128)S(1)}, u32[]{:S(2)}, u32[]{:S(2)}) collective-permute-start(f32[3,8,4,128]{3,2,1,0:T(4,128)S(1)} %get-tuple-element.296), channel_id=1, source_target_pairs={{0,240},{16,32},{32,16},{48,64},{64,48},{80,96},{96,80},{112,128},... | collective-permute-start | bytes 147464 | tf_op jit(solution)/shard_map/ppermute | solution.py:623
  153.2 9.6 %collective-permute-start.27 = (f32[3,8,4,128]{3,2,1,0:T(4,128)S(1)}, f32[3,8,4,128]{3,2,1,0:T(4,128)S(1)}, u32[]{:S(2)}, u32[]{:S(2)}) collective-permute-start(f32[3,8,4,128]{3,2,1,0:T(4,128)S(1)} %get-tuple-element.315), channel_id=1, source_target_pairs={{0,15},{1,2},{2,1},{3,4},{4,3},{5,6},{6,5},{7,8},{8,7},{9,10},{10,... | collective-permute-start | bytes 147464 | tf_op jit(solution)/shard_map/ppermute | solution.py:623
  162.9 7.4 %collective-permute-start.28 = (f32[3,8,4,128]{3,2,1,0:T(4,128)S(1)}, f32[3,8,4,128]{3,2,1,0:T(4,128)S(1)}, u32[]{:S(2)}, u32[]{:S(2)}) collective-permute-start(f32[3,8,4,128]{3,2,1,0:T(4,128)S(1)} %get-tuple-element.316), channel_id=1, source_target_pairs={{0,16},{16,0},{32,48},{48,32},{64,80},{80,64},{96,112},{112,96},{1... | collective-permute-start | bytes 147464 | tf_op jit(solution)/shard_map/ppermute | solution.py:624
  163.0 8.1 %collective-permute-start.29 = (f32[3,8,4,128]{3,2,1,0:T(4,128)S(1)}, f32[3,8,4,128]{3,2,1,0:T(4,128)S(1)}, u32[]{:S(2)}, u32[]{:S(2)}) collective-permute-start(f32[3,8,4,128]{3,2,1,0:T(4,128)S(1)} %get-tuple-element.317), channel_id=1, source_target_pairs={{0,240},{16,32},{32,16},{48,64},{64,48},{80,96},{96,80},{112,128},... | collective-permute-start | bytes 147464 | tf_op jit(solution)/shard_map/ppermute | solution.py:623
  (16 other events, 84.6 us)

commit v3 on v2

--- a/solution.py
+++ b/solution.py
@@ -114,6 +114,24 @@
 
 def by_j(mid_ref, edge_ref):
     return lambda c, i, j: edge_ref[c, i, j // DEG] if j in (0, DEG) else mid_ref[c, i, j - 1]
+
+
+def mixed(mid, full):
+    return lambda c, i, j: full[c, i, j] if j in (0, DEG) else mid[c, i, j - 1]
+
+
+def with_halo(src, xr_ref, yr_ref, face_at, c, i, j, tile):
+    value = src[c, i, j]
+    row = lax.broadcasted_iota(jnp.int32, (ROWS, 128), 0)
+    if tile == 0 and i == DEG:
+        face = xr_ref[face_at, j]
+        value = jnp.where(row < SIDE, value, jnp.concatenate([face, face], 0))
+    if isinstance(j, int) and j == DEG:
+        face = yr_ref[face_at, i]
+        first = jnp.broadcast_to(face[2 * tile : 2 * tile + 1], (ROWS, 128))
+        second = jnp.broadcast_to(face[2 * tile + 1 : 2 * tile + 2], (ROWS, 128))
+        value = jnp.where(row == SIDE - 1, first, jnp.where(row == ROWS - 1, second, value))
+    return value
 
 
 def received(ctl_ref, axis, even_ref, odd_ref, *at):
@@ -145,7 +163,7 @@
 def sum_all(ctl_ref, faces, parts, c, face_at, i, j, tile):
     xe, xo, ye, yo = faces
     total = sum_x(ctl_ref, xe, xo, parts, c, face_at, i, j, tile)
-    if j in (0, DEG):
+    if isinstance(j, int) and j in (0, DEG):
         row = lax.broadcasted_iota(jnp.int32, (ROWS, 128), 0)
         top, bottom = received(ctl_ref, 1, ye, yo, face_at, i)
         face = top if j else bottom
@@ -280,17 +298,7 @@
     join_y(inner_ref)
 
 
-def first_kernel(tile, *refs):
-    refs = list(refs)
-    take = lambda count: [refs.pop(0) for _ in range(count)]
-    ctl_ref, mid_ref, edge_ref, lam_ref, mu_ref, ratio_ref, rk_ref, wg_ref, wb_ref, ws_ref = take(10)
-    if tile == 0:
-        dg_ref, face_ref, xe_ref, xo_ref = take(4)
-    else:
-        work_0 = take(3)
-        dg_ref, inner_ref, au_ref = take(3)
-    sx_ref, fz_ref, fy_ref = take(3)
-
+def diag_kernel(lam_ref, mu_ref, ratio_ref, rk_ref, ws_ref, dg_ref):
     def diagonal(i):
         rows = [[None] * N for c in range(3)]
         for j in range(N):
@@ -308,16 +316,42 @@
             dg_ref[c, i] = both[c]
 
     loop(N, diagonal, 1)
-
-    def start(at):
-        gradients([[mid_ref[c, i, at] for i in range(N)] for c in range(3)], at + 1, wg_ref, sx_ref, fz_ref)
-
-    loop(N - 2, start)
+    join_y(dg_ref)
+
+
+def first_mid_kernel(wg_ref, xr_ref, t0_ref, t1_ref, *outs):
+    for tile, src in enumerate((t0_ref, t1_ref)):
+        u_out, gx_ref, gz_ref = outs[3 * tile : 3 * tile + 3]
+
+        def plane(at):
+            planes = [[with_halo(src, xr_ref, None, c, c, i, at + 1, tile) for i in range(N)] for c in range(3)]
+            for c in range(3):
+                for i in range(N):
+                    u_out[c, i, at] = planes[c][i]
+            gradients(planes, at, wg_ref, gx_ref, gz_ref)
+
+        loop(N - 2, plane)
+
+
+def first_kernel(tile, *refs):
+    refs = list(refs)
+    take = lambda count: [refs.pop(0) for _ in range(count)]
+    ctl_ref, wg_ref, wb_ref, ws_ref, lam_ref, mu_ref, src, xr_ref, yr_ref, mid_ref, gx_ref, gz_ref = take(12)
+    if tile == 0:
+        (dg_ref,) = take(1)
+        u_out, face_ref, xe_ref, xo_ref = take(4)
+    else:
+        work_0 = take(3)
+        u_out, inner_ref, au_ref = take(3)
+    work = take(3)
+    sx_ref, fz_ref, fy_ref = work
     for k in range(2):
-        gradients([[edge_ref[c, i, k] for i in range(N)] for c in range(3)], DEG * k, wg_ref, sx_ref, fz_ref)
-    work = (sx_ref, fz_ref, fy_ref)
-    stress(by_j(mid_ref, edge_ref), whole(sx_ref), whole(fz_ref), lam_ref, mu_ref, wb_ref, *work)
-    join_y(dg_ref)
+        planes = [[with_halo(src, xr_ref, yr_ref, c, c, i, DEG * k, tile) for i in range(N)] for c in range(3)]
+        for c in range(3):
+            for i in range(N):
+                u_out[c, i, k] = planes[c][i]
+        gradients(planes, DEG * k, wg_ref, sx_ref, fz_ref)
+    stress(by_j(mid_ref, u_out), mixed(gx_ref, sx_ref), mixed(gz_ref, fz_ref), lam_ref, mu_ref, wb_ref, *work)
     if tile == 0:
         send_first(ctl_ref, ws_ref, work, face_ref, xe_ref, xo_ref)
         give_faces(ctl_ref, dg_ref, 3, xe_ref, xo_ref)
@@ -373,7 +407,8 @@
         ins.append((u_ref, b_ref, None if with_diag else take(1)[0], take(1)[0] if stage else None))
     for tile in range(2):
         u_ref, b_ref, inv_ref, change_ref = ins[tile]
-        u_out, change_out, gx_ref, gz_ref = take(4)
+        u_out, gx_ref, gz_ref = take(3)
+        change_out = take(1 if stage < CHEB - 1 else 0)
         inv_out = take(1)[0] if with_diag else None
 
         def plane(at):
@@ -389,7 +424,8 @@
                     total = sum_x(ctl_ref, xe_ref, xo_ref, parts, c, c, i, j, tile)
                     change = change_ref[c, i, at] if stage else None
                     planes[c][i], change = advance(ctl_ref, stage, u_ref[c, i, at], b_ref[c, i, j], total, inv, change)
-                    change_out[c, i, at] = change
+                    if change_out:
+                        change_out[0][c, i, at] = change
                     u_out[c, i, at] = planes[c][i]
             gradients(planes, at, wg_ref, gx_ref, gz_ref)
 
@@ -407,7 +443,8 @@
     inv_ref = None if with_diag else take(1)[0]
     change_ref = take(1)[0] if stage else None
     work_0 = take(3) if tile else None
-    u_out, change_out = take(2)
+    (u_out,) = take(1)
+    change_out = take(1 if stage < CHEB - 1 else 0)
     inv_out = take(1)[0] if with_diag else None
     outs = take(2 if tile else 3)
     work = take(3)
@@ -425,12 +462,10 @@
                 total = sum_all(ctl_ref, faces, parts, c, c, i, j, tile)
                 change = change_ref[c, i, k] if stage else None
                 planes[c][i], change = advance(ctl_ref, stage, u_ref[c, i, k], b_ref[c, i, j], total, inv, change)
-                change_out[c, i, k] = change
+                if change_out:
+                    change_out[0][c, i, k] = change
                 u_out[c, i, k] = planes[c][i]
         gradients(planes, j, wg_ref, sx_ref, fz_ref)
-
-    def mixed(mid, full):
-        return lambda c, i, j: full[c, i, j] if j in ENDS else mid[c, i, j - 1]
 
     stress(by_j(mid_ref, u_out), mixed(gx_ref, sx_ref), mixed(gz_ref, fz_ref), lam_ref, mu_ref, wb_ref, *work)
     if tile == 0:
@@ -519,37 +554,17 @@
             out_ref[n, i] = value
 
 
-def halo_kernel(xr_ref, yr_ref, *refs):
-    fields, outs = refs[:4], refs[4:]
-    row = lax.broadcasted_iota(jnp.int32, (ROWS, 128), 0)
-    for n in range(2):
-        for tile in range(2):
-            src = fields[2 * n + tile]
-            mid_ref, edge_ref = outs[2 * tile : 2 * tile + 2]
-            dst = outs[4 + tile]
-
-            def plane(j):
-                for c in range(3):
-                    for i in range(N):
-                        value = src[c, i, j]
-                        if tile == 0 and i == DEG:
-                            face = xr_ref[3 * n + c, j]
-                            value = jnp.where(row < SIDE, value, jnp.concatenate([face, face], 0))
-                        if j is DEG:
-                            face = yr_ref[3 * n + c, i]
-                            first = jnp.broadcast_to(face[2 * tile : 2 * tile + 1], (ROWS, 128))
-                            second = jnp.broadcast_to(face[2 * tile + 1 : 2 * tile + 2], (ROWS, 128))
-                            value = jnp.where(row == SIDE - 1, first, jnp.where(row == ROWS - 1, second, value))
-                        if n == 1:
-                            dst[c, i, j] = value
-                        elif isinstance(j, int):
-                            edge_ref[c, i, j // DEG] = value
-                        else:
-                            mid_ref[c, i, j - 1] = value
-
-            plane(0)
-            loop(N - 2, lambda at: plane(at + 1), 1)
-            plane(DEG)
+def halo_kernel(xr_ref, yr_ref, t0_ref, t1_ref, o0_ref, o1_ref):
+    for tile, (src, dst) in enumerate(((t0_ref, o0_ref), (t1_ref, o1_ref))):
+
+        def plane(j):
+            for c in range(3):
+                for i in range(N):
+                    dst[c, i, j] = with_halo(src, xr_ref, yr_ref, 3 + c, c, i, j, tile)
+
+        plane(0)
+        loop(N - 2, lambda at: plane(at + 1), 1)
+        plane(DEG)
 
 
 def store_kernel(with_residual, *refs):
@@ -586,7 +601,8 @@
                 result = None
                 for y in range(begin // nodes_z, (stop - 1) // nodes_z + 1):
                     node = jnp.clip(lane + (begin - nodes_z * y), 0, nodes_z - 1) + 1
-                    got = lane_pick(work_ref[y, low:high], N * (node // DEG) + node % DEG)
+                    sevens = ((node.astype(F32) + 0.5) * (1.0 / DEG)).astype(jnp.int32)
+                    got = lane_pick(work_ref[y, low:high], node + sevens)
                     result = got if result is None else jnp.where(lane + begin >= nodes_z * y, got, result)
                 out_ref[c, low:high, begin:stop] = result[:, : stop - begin]
         return carry
@@ -670,27 +686,24 @@
     y_halo = jnp.concatenate([load[3] for load in loads], 0)
     (y_halo,) = call(halo_corner_kernel, 0, (x_halo, y_halo), (y_halo.shape,))
     y_halo = from_next(y_halo, "gx")
-    *nodes, b0, b1 = call(
-        halo_kernel, 0, (x_halo, y_halo, *loads[0][:2], *loads[1][:2]), (MID, EDGE, MID, EDGE, FIELD, FIELD)
-    )
-    u_mid = [nodes[0], nodes[2]]
-    u_edge = [nodes[1], nodes[3]]
-    b = [b0, b1]
-
     ratio_z = jnp.asarray(np.tile(RATIO, (ROWS, elems_z)), F32)
     ratio_i = jnp.asarray(np.broadcast_to(RATIO[:, None, None], (N, ROWS, 128)), F32)
     weights = (w_grad, w_back, w_share)
     work = (FIELD,) * 3
     both_faces = ((6, N, SIDE, 128),) * 2
+    diag = tuple(call(diag_kernel, 0, (*coeffs[tile], ratio_i, ratio_z, w_share), (FIELD,))[0] for tile in range(2))
+    got = call(first_mid_kernel, 0, (w_grad, x_halo, *loads[0][:2]), (MID,) * 6)
+    u_mid = [got[0], got[3]]
 
     def first(tile, extra, outs, scratch):
-        inputs = (ctl, u_mid[tile], u_edge[tile], *coeffs[tile], ratio_i, ratio_z, *weights, *extra)
-        return call(lambda *refs: first_kernel(tile, *refs), 0, inputs, (FIELD,) + outs, scratch)
-
-    diag_0, face, *rest = first(0, (), (FACE, *both_faces, *work), 0)
+        inputs = (ctl, *weights, *coeffs[tile], loads[0][tile], x_halo, y_halo, *got[3 * tile : 3 * tile + 3], *extra)
+        return call(lambda *refs: first_kernel(tile, *refs), 0, inputs, (EDGE,) + outs, scratch)
+
+    edge_0, face, *rest = first(0, diag[:1], (FACE, *both_faces, *work), 0)
     x_faces, work_0 = rest[:2], rest[2:]
-    diag_1, inner, au = first(1, work_0, (INNER, FIELD), 3)
-    diag = (diag_0, diag_1)
+    edge_1, inner, au = first(1, work_0, (INNER, FIELD), 3)
+    u_edge = [edge_0, edge_1]
+    b = call(halo_kernel, 0, (x_halo, y_halo, *loads[1][:2]), (FIELD, FIELD))
     change_mid = [None, None]
     change_edge = [None, None]
     inv_mid = [None, None]
@@ -706,15 +719,19 @@
         for tile in range(2):
             inputs += (u_mid[tile], b[tile]) + (() if with_diag else (inv_mid[tile],))
             inputs += (change_mid[tile],) if stage else ()
-        outs = (MID,) * (4 + keep_inv) * 2
+        keep_change = 1 if stage < CHEB - 1 else 0
+        each = 3 + keep_change + keep_inv
+        outs = (MID,) * each * 2
         results = call(lambda *refs: mid_kernel(stage, with_diag, *refs), 0, inputs, outs)
         slopes = [None, None]
         for tile in range(2):
-            got = results[(4 + keep_inv) * tile : (4 + keep_inv) * (tile + 1)]
-            u_mid[tile], change_mid[tile] = got[:2]
-            slopes[tile] = got[2:4]
+            got = results[each * tile : each * (tile + 1)]
+            u_mid[tile] = got[0]
+            slopes[tile] = got[1:3]
+            if keep_change:
+                change_mid[tile] = got[3]
             if with_diag:
-                inv_mid[tile] = got[4]
+                inv_mid[tile] = got[-1]
 
         for tile in range(2):
             inputs = (ctl, *weights, *coeffs[tile], *sums, *x_got, *y_got) + (diag if with_diag else ())
@@ -722,15 +739,16 @@
             inputs += () if with_diag else (inv_edge[tile],)
             inputs += (change_edge[tile],) if stage else ()
             inputs += tuple(work_0) if tile else ()
-            outs = (EDGE,) * (2 + keep_inv)
+            outs = (EDGE,) * (1 + keep_change + keep_inv)
             outs += (INNER, FIELD) if tile else (FACE, *((3, N, SIDE, 128),) * 2, *work)
             results = list(
                 call(lambda *refs: edge_kernel(tile, stage, with_diag, *refs), 0, inputs, outs, 3 if tile else 0)
             )
-            u_edge[tile], change_edge[tile] = results[:2]
+            u_edge[tile] = results.pop(0)
+            if keep_change:
+                change_edge[tile] = results.pop(0)
             if with_diag:
-                inv_edge[tile] = results[2]
-            results = results[2 + keep_inv :]
+                inv_edge[tile] = results.pop(0)
             if tile:
                 inner, au = results
             else:

time: 174 us -> 169 us (0.971)
  Pallas kernels: 64.6 us -> 60 us
    pallas_call x34 -> x37, Pallas kernels: 64.6 us -> 60 us  [call(): pl.pallas_call(kernel, in_specs=[SM] * smem + [VM] * (len(inputs) - smem)...]
  transfers between devices with their start and end apart: 30 -> 30, of which waited for: 15 -> 14; matrix products, arithmetic and copies ran while one was open for 0% -> 0% of each run, Pallas kernels for 24% -> 25%
where the time goes in v3:
time: 169 us
  starting transfers between devices  66.8 us (40%)
  Pallas kernels  60 us (36%)
  waiting for transfers between devices  38 us (22%)
  between operations  2.79 us (2%)
    pallas_call x37, Pallas kernels, call(): pl.pallas_call(kernel, in_specs=[SM] * smem + [VM] * (len(inputs) - smem)...  60 us
    ppermute x14, starting transfers between devices, swaps(): lax.ppermute(odd, axis, [(i, ((i + 1 ^ 1) - 1) % size) for i in range(siz...  54.6 us
    ppermute x14, waiting for transfers between devices, swaps(): lax.ppermute(odd, axis, [(i, ((i + 1 ^ 1) - 1) % size) for i in range(siz...  35.1 us
    ppermute x2, starting transfers between devices, from_next(): return lax.ppermute(value, axis, [(i, (i - 1) % size) for i in range(size)])  11 us
  transfers between devices with their start and end apart: 30, of which 14 were waited for; matrix products, arithmetic and copies ran while one was open for 0% of the time, Pallas kernels for 25%

profile of v3, /device:TPU:0, one launch (start us, length us, event | category | flops | bytes accessed | tf_op | source)
XLA Modules:
  0.0 169.2 jit_solution(792761559114780823)
XLA Ops:
  6.4 7.4 %collective-permute-start = (f32[6,8,4,128]{3,2,1,0:T(4,128)S(1)}, f32[6,8,4,128]{3,2,1,0:T(4,128)S(1)}, u32[]{:S(2)}, u32[]{:S(2)}) collective-permute-start(f32[6,8,4,128]{3,2,1,0:T(4,128)S(1)} %pad_maximum_fusion), channel_id=1, source_target_pairs={{0,15},{1,0},{2,1},{3,2},{4,3},{5,4},{6,5},{7,6},{8,7},{9,8},{10,9... | collective-permute-start | bytes 294920 | tf_op jit(solution)/shard_map/ppermute | solution.py:653
  16.7 3.5 %collective-permute-start.1 = (f32[6,8,4,128]{3,2,1,0:T(4,128)S(1)}, f32[6,8,4,128]{3,2,1,0:T(4,128)S(1)}, u32[]{:S(2)}, u32[]{:S(2)}) collective-permute-start(f32[6,8,4,128]{3,2,1,0:T(4,128)S(1)} %shard_map.134), channel_id=1, source_target_pairs={{0,240},{16,0},{32,16},{48,32},{64,48},{80,64},{96,80},{112,96},{1... | collective-permute-start | bytes 294920 | tf_op jit(solution)/shard_map/ppermute | solution.py:653
  25.6 7.8 %collective-permute-start.3 = (f32[6,8,4,128]{3,2,1,0:T(4,128)S(1)}, f32[6,8,4,128]{3,2,1,0:T(4,128)S(1)}, u32[]{:S(2)}, u32[]{:S(2)}) collective-permute-start(f32[6,8,4,128]{3,2,1,0:T(4,128)S(1)} %get-tuple-element.185), channel_id=1, source_target_pairs={{0,15},{1,2},{2,1},{3,4},{4,3},{5,6},{6,5},{7,8},{8,7},{9,10},{10,... | collective-permute-start | bytes 294920 | tf_op jit(solution)/shard_map/ppermute | solution.py:639
  34.8 3.3 %shard_map.138 = (f32[3,8,2,8,128]{4,3,2,1,0:T(8,128)S(1)}, f32[3,6,8,8,128]{4,3,2,1,0:T(8,128)S(1)}, f32[3,8,8,8,128]{4,3,2,1,0:T(8,128)S(1)}) custom-call(f32[8,8,128]{2,1,0:T(8,128)S(1)} %broadcast_in_dim.2.ctl_ref.refs_0_, bf16[256,256]{1,0:T(8,128)(2,1)S(1)} %copy-done, bf16[256,256]{1,0:T(8,128)(2,1)S(1)} %copy-done.1, bf16[256,128]{1,0:T(8,128)(2,1)S(1)} %copy-done.2, ...), custom_call_target="tpu_custom_call" | custom-call | tf_op jit(solution)/shard_map/pallas_call | solution.py:627
  38.3 4.2 %collective-permute-start.5 = (f32[6,8,4,128]{3,2,1,0:T(4,128)S(1)}, f32[6,8,4,128]{3,2,1,0:T(4,128)S(1)}, u32[]{:S(2)}, u32[]{:S(2)}) collective-permute-start(f32[6,8,4,128]{3,2,1,0:T(4,128)S(1)} %get-tuple-element.187), channel_id=1, source_target_pairs={{0,240},{16,32},{32,16},{48,64},{64,48},{80,96},{96,80},{112,128},... | collective-permute-start | bytes 294920 | tf_op jit(solution)/shard_map/ppermute | solution.py:639
  48.9 5.5 %collective-permute-start.7 = (f32[3,8,4,128]{3,2,1,0:T(4,128)S(1)}, f32[3,8,4,128]{3,2,1,0:T(4,128)S(1)}, u32[]{:S(2)}, u32[]{:S(2)}) collective-permute-start(f32[3,8,4,128]{3,2,1,0:T(4,128)S(1)} %get-tuple-element.207), channel_id=1, source_target_pairs={{0,15},{1,2},{2,1},{3,4},{4,3},{5,6},{6,5},{7,8},{8,7},{9,10},{10,... | collective-permute-start | bytes 147464 | tf_op jit(solution)/shard_map/ppermute | solution.py:639
  54.4 3.4 %shard_map.144 = (f32[3,8,2,8,128]{4,3,2,1,0:T(8,128)S(1)}, f32[3,8,2,8,128]{4,3,2,1,0:T(8,128)S(1)}, f32[3,8,2,8,128]{4,3,2,1,0:T(8,128)S(1)}, f32[3,6,8,8,128]{4,3,2,1,0:T(8,128)S(1)}, f32[3,8,8,8,128]{4,3,2,1,0:T(8,128)S(1)}) custom-call(f32[8,8,128]{2,1,0:T(8,128)S(1)} %broadcast_in_dim.2.ctl_ref.refs_0_, bf16[256,256]{1,0:T(8,128)(2,1)S(1)} %copy-done, ...), custom_call_target="tpu_custom_call" | custom-call | tf_op jit(solution)/shard_map/pallas_call | solution.py:627
  58.7 4.5 %collective-permute-start.9 = (f32[3,8,4,128]{3,2,1,0:T(4,128)S(1)}, f32[3,8,4,128]{3,2,1,0:T(4,128)S(1)}, u32[]{:S(2)}, u32[]{:S(2)}) collective-permute-start(f32[3,8,4,128]{3,2,1,0:T(4,128)S(1)} %get-tuple-element.209), channel_id=1, source_target_pairs={{0,240},{16,32},{32,16},{48,64},{64,48},{80,96},{96,80},{112,128},... | collective-permute-start | bytes 147464 | tf_op jit(solution)/shard_map/ppermute | solution.py:639
  68.9 4.3 %collective-permute-start.11 = (f32[3,8,4,128]{3,2,1,0:T(4,128)S(1)}, f32[3,8,4,128]{3,2,1,0:T(4,128)S(1)}, u32[]{:S(2)}, u32[]{:S(2)}) collective-permute-start(f32[3,8,4,128]{3,2,1,0:T(4,128)S(1)} %get-tuple-element.233), channel_id=1, source_target_pairs={{0,15},{1,2},{2,1},{3,4},{4,3},{5,6},{6,5},{7,8},{8,7},{9,10},{10,... | collective-permute-start | bytes 147464 | tf_op jit(solution)/shard_map/ppermute | solution.py:639
  73.2 3.4 %shard_map.148 = (f32[3,8,2,8,128]{4,3,2,1,0:T(8,128)S(1)}, f32[3,8,2,8,128]{4,3,2,1,0:T(8,128)S(1)}, f32[3,6,8,8,128]{4,3,2,1,0:T(8,128)S(1)}, f32[3,8,8,8,128]{4,3,2,1,0:T(8,128)S(1)}) custom-call(f32[8,8,128]{2,1,0:T(8,128)S(1)} %broadcast_in_dim.2.ctl_ref.refs_0_, bf16[256,256]{1,0:T(8,128)(2,1)S(1)} %copy-done, bf16[256,256]{1,0:T(8,128)(2,1)S(1)} %copy-done.1, ...), custom_call_target="tpu_custom_call" | custom-call | tf_op jit(solution)/shard_map/pallas_call | solution.py:627
  78.7 4.3 %collective-permute-start.13 = (f32[3,8,4,128]{3,2,1,0:T(4,128)S(1)}, f32[3,8,4,128]{3,2,1,0:T(4,128)S(1)}, u32[]{:S(2)}, u32[]{:S(2)}) collective-permute-start(f32[3,8,4,128]{3,2,1,0:T(4,128)S(1)} %get-tuple-element.235), channel_id=1, source_target_pairs={{0,240},{16,32},{32,16},{48,64},{64,48},{80,96},{96,80},{112,128},... | collective-permute-start | bytes 147464 | tf_op jit(solution)/shard_map/ppermute | solution.py:639
  88.7 3.2 %collective-permute-start.15 = (f32[3,8,4,128]{3,2,1,0:T(4,128)S(1)}, f32[3,8,4,128]{3,2,1,0:T(4,128)S(1)}, u32[]{:S(2)}, u32[]{:S(2)}) collective-permute-start(f32[3,8,4,128]{3,2,1,0:T(4,128)S(1)} %get-tuple-element.255), channel_id=1, source_target_pairs={{0,15},{1,2},{2,1},{3,4},{4,3},{5,6},{6,5},{7,8},{8,7},{9,10},{10,... | collective-permute-start | bytes 147464 | tf_op jit(solution)/shard_map/ppermute | solution.py:639
  91.9 3.4 %shard_map.152 = (f32[3,8,2,8,128]{4,3,2,1,0:T(8,128)S(1)}, f32[3,6,8,8,128]{4,3,2,1,0:T(8,128)S(1)}, f32[3,8,8,8,128]{4,3,2,1,0:T(8,128)S(1)}) custom-call(f32[8,8,128]{2,1,0:T(8,128)S(1)} %broadcast_in_dim.2.ctl_ref.refs_0_, bf16[256,256]{1,0:T(8,128)(2,1)S(1)} %copy-done, bf16[256,256]{1,0:T(8,128)(2,1)S(1)} %copy-done.1, bf16[256,128]{1,0:T(8,128)(2,1)S(1)} %copy-done.2, ...), custom_call_target="tpu_custom_call" | custom-call | tf_op jit(solution)/shard_map/pallas_call | solution.py:627
  95.2 3.3 %collective-permute-done.15.xo_ref.refs_6_.refs_10_ = f32[3,8,4,128]{3,2,1,0:T(4,128)S(1)} collective-permute-done((f32[3,8,4,128]{3,2,1,0:T(4,128)S(1)}, f32[3,8,4,128]{3,2,1,0:T(4,128)S(1)}, u32[]{:S(2)}, u32[]{:S(2)}) %collective-permute-start.15) | collective-permute-done | bytes 49184 | tf_op jit(solution)/shard_map/ppermute | solution.py:639
  98.7 4.3 %collective-permute-start.17 = (f32[3,8,4,128]{3,2,1,0:T(4,128)S(1)}, f32[3,8,4,128]{3,2,1,0:T(4,128)S(1)}, u32[]{:S(2)}, u32[]{:S(2)}) collective-permute-start(f32[3,8,4,128]{3,2,1,0:T(4,128)S(1)} %get-tuple-element.257), channel_id=1, source_target_pairs={{0,240},{16,32},{32,16},{48,64},{64,48},{80,96},{96,80},{112,128},... | collective-permute-start | bytes 147464 | tf_op jit(solution)/shard_map/ppermute | solution.py:639
  110.8 3.4 %shard_map.156 = (f32[3,8,2,8,128]{4,3,2,1,0:T(8,128)S(1)}, f32[3,8,2,8,128]{4,3,2,1,0:T(8,128)S(1)}, f32[3,6,8,8,128]{4,3,2,1,0:T(8,128)S(1)}, f32[3,8,8,8,128]{4,3,2,1,0:T(8,128)S(1)}) custom-call(f32[8,8,128]{2,1,0:T(8,128)S(1)} %broadcast_in_dim.2.ctl_ref.refs_0_, bf16[256,256]{1,0:T(8,128)(2,1)S(1)} %copy-done, bf16[256,256]{1,0:T(8,128)(2,1)S(1)} %copy-done.1, ...), custom_call_target="tpu_custom_call" | custom-call | tf_op jit(solution)/shard_map/pallas_call | solution.py:627
  114.1 4.2 %collective-permute-done.19.xo_ref.refs_6_.refs_10_ = f32[3,8,4,128]{3,2,1,0:T(4,128)S(1)} collective-permute-done((f32[3,8,4,128]{3,2,1,0:T(4,128)S(1)}, f32[3,8,4,128]{3,2,1,0:T(4,128)S(1)}, u32[]{:S(2)}, u32[]{:S(2)}) %collective-permute-start.19) | collective-permute-done | bytes 49184 | tf_op jit(solution)/shard_map/ppermute | solution.py:639
  118.5 4.5 %collective-permute-start.21 = (f32[3,8,4,128]{3,2,1,0:T(4,128)S(1)}, f32[3,8,4,128]{3,2,1,0:T(4,128)S(1)}, u32[]{:S(2)}, u32[]{:S(2)}) collective-permute-start(f32[3,8,4,128]{3,2,1,0:T(4,128)S(1)} %get-tuple-element.275), channel_id=1, source_target_pairs={{0,240},{16,32},{32,16},{48,64},{64,48},{80,96},{96,80},{112,128},... | collective-permute-start | bytes 147464 | tf_op jit(solution)/shard_map/ppermute | solution.py:639
  129.6 3.4 %shard_map.160 = (f32[3,8,2,8,128]{4,3,2,1,0:T(8,128)S(1)}, f32[3,8,2,8,128]{4,3,2,1,0:T(8,128)S(1)}, f32[3,6,8,8,128]{4,3,2,1,0:T(8,128)S(1)}, f32[3,8,8,8,128]{4,3,2,1,0:T(8,128)S(1)}) custom-call(f32[8,8,128]{2,1,0:T(8,128)S(1)} %broadcast_in_dim.2.ctl_ref.refs_0_, bf16[256,256]{1,0:T(8,128)(2,1)S(1)} %copy-done, bf16[256,256]{1,0:T(8,128)(2,1)S(1)} %copy-done.1, ...), custom_call_target="tpu_custom_call" | custom-call | tf_op jit(solution)/shard_map/pallas_call | solution.py:627
  133.0 5.3 %collective-permute-done.23.refs_6_.xo_ref.refs_10_ = f32[3,8,4,128]{3,2,1,0:T(4,128)S(1)} collective-permute-done((f32[3,8,4,128]{3,2,1,0:T(4,128)S(1)}, f32[3,8,4,128]{3,2,1,0:T(4,128)S(1)}, u32[]{:S(2)}, u32[]{:S(2)}) %collective-permute-start.23) | collective-permute-done | bytes 49184 | tf_op jit(solution)/shard_map/ppermute | solution.py:639
  138.5 4.3 %collective-permute-start.25 = (f32[3,8,4,128]{3,2,1,0:T(4,128)S(1)}, f32[3,8,4,128]{3,2,1,0:T(4,128)S(1)}, u32[]{:S(2)}, u32[]{:S(2)}) collective-permute-start(f32[3,8,4,128]{3,2,1,0:T(4,128)S(1)} %get-tuple-element.300), channel_id=1, source_target_pairs={{0,240},{16,32},{32,16},{48,64},{64,48},{80,96},{96,80},{112,128},... | collective-permute-start | bytes 147464 | tf_op jit(solution)/shard_map/ppermute | solution.py:639
  149.1 3.4 %shard_map.164 = (f32[3,8,2,8,128]{4,3,2,1,0:T(8,128)S(1)}, f32[3,6,8,8,128]{4,3,2,1,0:T(8,128)S(1)}, f32[3,8,8,8,128]{4,3,2,1,0:T(8,128)S(1)}) custom-call(f32[8,8,128]{2,1,0:T(8,128)S(1)} %broadcast_in_dim.2.ctl_ref.refs_0_, bf16[256,256]{1,0:T(8,128)(2,1)S(1)} %copy-done, bf16[256,256]{1,0:T(8,128)(2,1)S(1)} %copy-done.1, bf16[256,128]{1,0:T(8,128)(2,1)S(1)} %copy-done.2, ...), custom_call_target="tpu_custom_call" | custom-call | tf_op jit(solution)/shard_map/pallas_call | solution.py:627
  152.4 5.7 %collective-permute-done.27.xo_ref.refs_7_ = f32[3,8,4,128]{3,2,1,0:T(4,128)S(1)} collective-permute-done((f32[3,8,4,128]{3,2,1,0:T(4,128)S(1)}, f32[3,8,4,128]{3,2,1,0:T(4,128)S(1)}, u32[]{:S(2)}, u32[]{:S(2)}) %collective-permute-start.27) | collective-permute-done | bytes 49184 | tf_op jit(solution)/shard_map/ppermute | solution.py:639
  158.3 4.3 %collective-permute-start.29 = (f32[3,8,4,128]{3,2,1,0:T(4,128)S(1)}, f32[3,8,4,128]{3,2,1,0:T(4,128)S(1)}, u32[]{:S(2)}, u32[]{:S(2)}) collective-permute-start(f32[3,8,4,128]{3,2,1,0:T(4,128)S(1)} %get-tuple-element.321), channel_id=1, source_target_pairs={{0,240},{16,32},{32,16},{48,64},{64,48},{80,96},{96,80},{112,128},... | collective-permute-start | bytes 147464 | tf_op jit(solution)/shard_map/ppermute | solution.py:639
  (97 shorter events, 62.4 us)
Async XLA Ops:
  6.4 10.4 %collective-permute-start = (f32[6,8,4,128]{3,2,1,0:T(4,128)S(1)}, f32[6,8,4,128]{3,2,1,0:T(4,128)S(1)}, u32[]{:S(2)}, u32[]{:S(2)}) collective-permute-start(f32[6,8,4,128]{3,2,1,0:T(4,128)S(1)} %pad_maximum_fusion), channel_id=1, source_target_pairs={{0,15},{1,0},{2,1},{3,2},{4,3},{5,4},{6,5},{7,6},{8,7},{9,8},{10,9... | collective-permute-start | bytes 294920 | tf_op jit(solution)/shard_map/ppermute | solution.py:653
  16.7 7.0 %collective-permute-start.1 = (f32[6,8,4,128]{3,2,1,0:T(4,128)S(1)}, f32[6,8,4,128]{3,2,1,0:T(4,128)S(1)}, u32[]{:S(2)}, u32[]{:S(2)}) collective-permute-start(f32[6,8,4,128]{3,2,1,0:T(4,128)S(1)} %shard_map.134), channel_id=1, source_target_pairs={{0,240},{16,0},{32,16},{48,32},{64,48},{80,64},{96,80},{112,96},{1... | collective-permute-start | bytes 294920 | tf_op jit(solution)/shard_map/ppermute | solution.py:653
  25.5 12.5 %collective-permute-start.2 = (f32[6,8,4,128]{3,2,1,0:T(4,128)S(1)}, f32[6,8,4,128]{3,2,1,0:T(4,128)S(1)}, u32[]{:S(2)}, u32[]{:S(2)}) collective-permute-start(f32[6,8,4,128]{3,2,1,0:T(4,128)S(1)} %get-tuple-element.184), channel_id=1, source_target_pairs={{0,1},{1,0},{2,3},{3,2},{4,5},{5,4},{6,7},{7,6},{8,9},{9,8},{10,11... | collective-permute-start | bytes 294920 | tf_op jit(solution)/shard_map/ppermute | solution.py:640
  25.6 12.4 %collective-permute-start.3 = (f32[6,8,4,128]{3,2,1,0:T(4,128)S(1)}, f32[6,8,4,128]{3,2,1,0:T(4,128)S(1)}, u32[]{:S(2)}, u32[]{:S(2)}) collective-permute-start(f32[6,8,4,128]{3,2,1,0:T(4,128)S(1)} %get-tuple-element.185), channel_id=1, source_target_pairs={{0,15},{1,2},{2,1},{3,4},{4,3},{5,6},{6,5},{7,8},{8,7},{9,10},{10,... | collective-permute-start | bytes 294920 | tf_op jit(solution)/shard_map/ppermute | solution.py:639
  38.2 6.4 %collective-permute-start.4 = (f32[6,8,4,128]{3,2,1,0:T(4,128)S(1)}, f32[6,8,4,128]{3,2,1,0:T(4,128)S(1)}, u32[]{:S(2)}, u32[]{:S(2)}) collective-permute-start(f32[6,8,4,128]{3,2,1,0:T(4,128)S(1)} %get-tuple-element.186), channel_id=1, source_target_pairs={{0,16},{16,0},{32,48},{48,32},{64,80},{80,64},{96,112},{112,96},{1... | collective-permute-start | bytes 294920 | tf_op jit(solution)/shard_map/ppermute | solution.py:640
  38.3 8.6 %collective-permute-start.5 = (f32[6,8,4,128]{3,2,1,0:T(4,128)S(1)}, f32[6,8,4,128]{3,2,1,0:T(4,128)S(1)}, u32[]{:S(2)}, u32[]{:S(2)}) collective-permute-start(f32[6,8,4,128]{3,2,1,0:T(4,128)S(1)} %get-tuple-element.187), channel_id=1, source_target_pairs={{0,240},{16,32},{32,16},{48,64},{64,48},{80,96},{96,80},{112,128},... | collective-permute-start | bytes 294920 | tf_op jit(solution)/shard_map/ppermute | solution.py:639
  48.8 9.0 %collective-permute-start.6 = (f32[3,8,4,128]{3,2,1,0:T(4,128)S(1)}, f32[3,8,4,128]{3,2,1,0:T(4,128)S(1)}, u32[]{:S(2)}, u32[]{:S(2)}) collective-permute-start(f32[3,8,4,128]{3,2,1,0:T(4,128)S(1)} %get-tuple-element.206), channel_id=1, source_target_pairs={{0,1},{1,0},{2,3},{3,2},{4,5},{5,4},{6,7},{7,6},{8,9},{9,8},{10,11... | collective-permute-start | bytes 147464 | tf_op jit(solution)/shard_map/ppermute | solution.py:640
  48.9 9.6 %collective-permute-start.7 = (f32[3,8,4,128]{3,2,1,0:T(4,128)S(1)}, f32[3,8,4,128]{3,2,1,0:T(4,128)S(1)}, u32[]{:S(2)}, u32[]{:S(2)}) collective-permute-start(f32[3,8,4,128]{3,2,1,0:T(4,128)S(1)} %get-tuple-element.207), channel_id=1, source_target_pairs={{0,15},{1,2},{2,1},{3,4},{4,3},{5,6},{6,5},{7,8},{8,7},{9,10},{10,... | collective-permute-start | bytes 147464 | tf_op jit(solution)/shard_map/ppermute | solution.py:639
  58.6 6.3 %collective-permute-start.8 = (f32[3,8,4,128]{3,2,1,0:T(4,128)S(1)}, f32[3,8,4,128]{3,2,1,0:T(4,128)S(1)}, u32[]{:S(2)}, u32[]{:S(2)}) collective-permute-start(f32[3,8,4,128]{3,2,1,0:T(4,128)S(1)} %get-tuple-element.208), channel_id=1, source_target_pairs={{0,16},{16,0},{32,48},{48,32},{64,80},{80,64},{96,112},{112,96},{1... | collective-permute-start | bytes 147464 | tf_op jit(solution)/shard_map/ppermute | solution.py:640
  58.7 8.3 %collective-permute-start.9 = (f32[3,8,4,128]{3,2,1,0:T(4,128)S(1)}, f32[3,8,4,128]{3,2,1,0:T(4,128)S(1)}, u32[]{:S(2)}, u32[]{:S(2)}) collective-permute-start(f32[3,8,4,128]{3,2,1,0:T(4,128)S(1)} %get-tuple-element.209), channel_id=1, source_target_pairs={{0,240},{16,32},{32,16},{48,64},{64,48},{80,96},{96,80},{112,128},... | collective-permute-start | bytes 147464 | tf_op jit(solution)/shard_map/ppermute | solution.py:639
  68.8 7.8 %collective-permute-start.10 = (f32[3,8,4,128]{3,2,1,0:T(4,128)S(1)}, f32[3,8,4,128]{3,2,1,0:T(4,128)S(1)}, u32[]{:S(2)}, u32[]{:S(2)}) collective-permute-start(f32[3,8,4,128]{3,2,1,0:T(4,128)S(1)} %get-tuple-element.232), channel_id=1, source_target_pairs={{0,1},{1,0},{2,3},{3,2},{4,5},{5,4},{6,7},{7,6},{8,9},{9,8},{10,11... | collective-permute-start | bytes 147464 | tf_op jit(solution)/shard_map/ppermute | solution.py:640
  68.9 9.6 %collective-permute-start.11 = (f32[3,8,4,128]{3,2,1,0:T(4,128)S(1)}, f32[3,8,4,128]{3,2,1,0:T(4,128)S(1)}, u32[]{:S(2)}, u32[]{:S(2)}) collective-permute-start(f32[3,8,4,128]{3,2,1,0:T(4,128)S(1)} %get-tuple-element.233), channel_id=1, source_target_pairs={{0,15},{1,2},{2,1},{3,4},{4,3},{5,6},{6,5},{7,8},{8,7},{9,10},{10,... | collective-permute-start | bytes 147464 | tf_op jit(solution)/shard_map/ppermute | solution.py:639
  78.7 8.1 %collective-permute-start.13 = (f32[3,8,4,128]{3,2,1,0:T(4,128)S(1)}, f32[3,8,4,128]{3,2,1,0:T(4,128)S(1)}, u32[]{:S(2)}, u32[]{:S(2)}) collective-permute-start(f32[3,8,4,128]{3,2,1,0:T(4,128)S(1)} %get-tuple-element.235), channel_id=1, source_target_pairs={{0,240},{16,32},{32,16},{48,64},{64,48},{80,96},{96,80},{112,128},... | collective-permute-start | bytes 147464 | tf_op jit(solution)/shard_map/ppermute | solution.py:639
  88.6 6.7 %collective-permute-start.14 = (f32[3,8,4,128]{3,2,1,0:T(4,128)S(1)}, f32[3,8,4,128]{3,2,1,0:T(4,128)S(1)}, u32[]{:S(2)}, u32[]{:S(2)}) collective-permute-start(f32[3,8,4,128]{3,2,1,0:T(4,128)S(1)} %get-tuple-element.254), channel_id=1, source_target_pairs={{0,1},{1,0},{2,3},{3,2},{4,5},{5,4},{6,7},{7,6},{8,9},{9,8},{10,11... | collective-permute-start | bytes 147464 | tf_op jit(solution)/shard_map/ppermute | solution.py:640
  88.7 9.9 %collective-permute-start.15 = (f32[3,8,4,128]{3,2,1,0:T(4,128)S(1)}, f32[3,8,4,128]{3,2,1,0:T(4,128)S(1)}, u32[]{:S(2)}, u32[]{:S(2)}) collective-permute-start(f32[3,8,4,128]{3,2,1,0:T(4,128)S(1)} %get-tuple-element.255), channel_id=1, source_target_pairs={{0,15},{1,2},{2,1},{3,4},{4,3},{5,6},{6,5},{7,8},{8,7},{9,10},{10,... | collective-permute-start | bytes 147464 | tf_op jit(solution)/shard_map/ppermute | solution.py:639
  98.7 8.1 %collective-permute-start.17 = (f32[3,8,4,128]{3,2,1,0:T(4,128)S(1)}, f32[3,8,4,128]{3,2,1,0:T(4,128)S(1)}, u32[]{:S(2)}, u32[]{:S(2)}) collective-permute-start(f32[3,8,4,128]{3,2,1,0:T(4,128)S(1)} %get-tuple-element.257), channel_id=1, source_target_pairs={{0,240},{16,32},{32,16},{48,64},{64,48},{80,96},{96,80},{112,128},... | collective-permute-start | bytes 147464 | tf_op jit(solution)/shard_map/ppermute | solution.py:639
  108.7 9.6 %collective-permute-start.19 = (f32[3,8,4,128]{3,2,1,0:T(4,128)S(1)}, f32[3,8,4,128]{3,2,1,0:T(4,128)S(1)}, u32[]{:S(2)}, u32[]{:S(2)}) collective-permute-start(f32[3,8,4,128]{3,2,1,0:T(4,128)S(1)} %get-tuple-element.273), channel_id=1, source_target_pairs={{0,15},{1,2},{2,1},{3,4},{4,3},{5,6},{6,5},{7,8},{8,7},{9,10},{10,... | collective-permute-start | bytes 147464 | tf_op jit(solution)/shard_map/ppermute | solution.py:639
  118.4 6.3 %collective-permute-start.20 = (f32[3,8,4,128]{3,2,1,0:T(4,128)S(1)}, f32[3,8,4,128]{3,2,1,0:T(4,128)S(1)}, u32[]{:S(2)}, u32[]{:S(2)}) collective-permute-start(f32[3,8,4,128]{3,2,1,0:T(4,128)S(1)} %get-tuple-element.274), channel_id=1, source_target_pairs={{0,16},{16,0},{32,48},{48,32},{64,80},{80,64},{96,112},{112,96},{1... | collective-permute-start | bytes 147464 | tf_op jit(solution)/shard_map/ppermute | solution.py:640
  118.5 8.3 %collective-permute-start.21 = (f32[3,8,4,128]{3,2,1,0:T(4,128)S(1)}, f32[3,8,4,128]{3,2,1,0:T(4,128)S(1)}, u32[]{:S(2)}, u32[]{:S(2)}) collective-permute-start(f32[3,8,4,128]{3,2,1,0:T(4,128)S(1)} %get-tuple-element.275), channel_id=1, source_target_pairs={{0,240},{16,32},{32,16},{48,64},{64,48},{80,96},{96,80},{112,128},... | collective-permute-start | bytes 147464 | tf_op jit(solution)/shard_map/ppermute | solution.py:639
  128.7 9.6 %collective-permute-start.23 = (f32[3,8,4,128]{3,2,1,0:T(4,128)S(1)}, f32[3,8,4,128]{3,2,1,0:T(4,128)S(1)}, u32[]{:S(2)}, u32[]{:S(2)}) collective-permute-start(f32[3,8,4,128]{3,2,1,0:T(4,128)S(1)} %get-tuple-element.295), channel_id=1, source_target_pairs={{0,15},{1,2},{2,1},{3,4},{4,3},{5,6},{6,5},{7,8},{8,7},{9,10},{10,... | collective-permute-start | bytes 147464 | tf_op jit(solution)/shard_map/ppermute | solution.py:639
  138.5 8.1 %collective-permute-start.25 = (f32[3,8,4,128]{3,2,1,0:T(4,128)S(1)}, f32[3,8,4,128]{3,2,1,0:T(4,128)S(1)}, u32[]{:S(2)}, u32[]{:S(2)}) collective-permute-start(f32[3,8,4,128]{3,2,1,0:T(4,128)S(1)} %get-tuple-element.300), channel_id=1, source_target_pairs={{0,240},{16,32},{32,16},{48,64},{64,48},{80,96},{96,80},{112,128},... | collective-permute-start | bytes 147464 | tf_op jit(solution)/shard_map/ppermute | solution.py:639
  148.5 9.6 %collective-permute-start.27 = (f32[3,8,4,128]{3,2,1,0:T(4,128)S(1)}, f32[3,8,4,128]{3,2,1,0:T(4,128)S(1)}, u32[]{:S(2)}, u32[]{:S(2)}) collective-permute-start(f32[3,8,4,128]{3,2,1,0:T(4,128)S(1)} %get-tuple-element.319), channel_id=1, source_target_pairs={{0,15},{1,2},{2,1},{3,4},{4,3},{5,6},{6,5},{7,8},{8,7},{9,10},{10,... | collective-permute-start | bytes 147464 | tf_op jit(solution)/shard_map/ppermute | solution.py:639
  158.2 7.1 %collective-permute-start.28 = (f32[3,8,4,128]{3,2,1,0:T(4,128)S(1)}, f32[3,8,4,128]{3,2,1,0:T(4,128)S(1)}, u32[]{:S(2)}, u32[]{:S(2)}) collective-permute-start(f32[3,8,4,128]{3,2,1,0:T(4,128)S(1)} %get-tuple-element.320), channel_id=1, source_target_pairs={{0,16},{16,0},{32,48},{48,32},{64,80},{80,64},{96,112},{112,96},{1... | collective-permute-start | bytes 147464 | tf_op jit(solution)/shard_map/ppermute | solution.py:640
  158.3 8.1 %collective-permute-start.29 = (f32[3,8,4,128]{3,2,1,0:T(4,128)S(1)}, f32[3,8,4,128]{3,2,1,0:T(4,128)S(1)}, u32[]{:S(2)}, u32[]{:S(2)}) collective-permute-start(f32[3,8,4,128]{3,2,1,0:T(4,128)S(1)} %get-tuple-element.321), channel_id=1, source_target_pairs={{0,240},{16,32},{32,16},{48,64},{64,48},{80,96},{96,80},{112,128},... | collective-permute-start | bytes 147464 | tf_op jit(solution)/shard_map/ppermute | solution.py:639
  (16 other events, 145.7 us)

commit v4 on v3

--- a/solution.py
+++ b/solution.py
@@ -81,6 +81,32 @@
             from_odd = to if from_odd is None else from_odd + to
         outs[p] = from_odd + from_even
         outs[DEG - p] = from_odd - from_even
+    return outs
+
+
+def pair_terms(low, high, matrix, i, p):
+    even = float(np.float32((matrix[p, i] + matrix[p, DEG - i]) / 2.0)) * (low + high)
+    odd = float(np.float32((matrix[p, i] - matrix[p, DEG - i]) / 2.0)) * (low - high)
+    return even, odd
+
+
+def inner_sums(vals, matrix):
+    outs = [None] * N
+    for p in range(N // 2):
+        terms = [pair_terms(vals[i - 1], vals[DEG - i - 1], matrix, i, p) for i in range(1, N // 2)]
+        from_even = terms[0][0] + terms[1][0] + terms[2][0]
+        from_odd = terms[0][1] + terms[1][1] + terms[2][1]
+        outs[p] = from_odd + from_even
+        outs[DEG - p] = from_odd - from_even
+    return outs
+
+
+def add_ends(partial, low, high, matrix):
+    outs = [None] * N
+    for p in range(N // 2):
+        from_even, from_odd = pair_terms(low, high, matrix, 0, p)
+        outs[p] = partial[p] + (from_odd + from_even)
+        outs[DEG - p] = partial[DEG - p] + (from_odd - from_even)
     return outs
 
 
@@ -195,9 +221,34 @@
             gz_ref[c, i, at] = both[c, i]
 
 
-def stress(u_at, gx_at, gz_at, lam_ref, mu_ref, wb_ref, sx_ref, fz_ref, fy_ref):
+def inner_slopes(u_ref, gy_ref):
     def plane(i):
-        gy = [line_sums([u_at(c, i, j) for j in range(N)], DERIV) for c in range(3)]
+        for c in range(3):
+            outs = inner_sums([u_ref[c, i, at] for at in range(N - 2)], DERIV)
+            for j in range(N):
+                gy_ref[c, i, j] = outs[j]
+
+    loop(N, plane)
+
+
+def back_yz(sy, sz, i, wb_ref, fz_ref, fy_ref):
+    flat = jnp.concatenate([sz[c][j] for c in range(3) for j in range(N)], 0)
+    both = dot(split_pair(flat), wb_ref[...])
+    for c in range(3):
+        outs = line_sums(sy[c], DERIV.T)
+        for j in range(N):
+            fy_ref[c, i, j] = outs[j]
+    both = (both[:, :128] + both[:, 128:]).reshape(3, N, ROWS, 128)
+    for c in range(3):
+        fz_ref[c, i] = both[c]
+
+
+def stress(tile, edge_ref, gy_ref, gx_at, gz_at, lam_ref, mu_ref, wb_ref, sx_ref, fz_ref, fy_ref):
+    def plane(i, later=False):
+        gy = [
+            add_ends([gy_ref[c, i, j] for j in range(N)], edge_ref[c, i, 0], edge_ref[c, i, 1], DERIV)
+            for c in range(3)
+        ]
         sy = [[None] * N for c in range(3)]
         sz = [[None] * N for c in range(3)]
         for j in range(N):
@@ -218,17 +269,34 @@
             sy[0][j] = sxy
             sy[1][j] = mu2 * gy[1][j] + trace
             sy[2][j] = syz
-        flat = jnp.concatenate([sz[c][j] for c in range(3) for j in range(N)], 0)
-        both = dot(split_pair(flat), wb_ref[...])
-        for c in range(3):
-            outs = line_sums(sy[c], DERIV.T)
-            for j in range(N):
-                fy_ref[c, i, j] = outs[j]
-        both = (both[:, :128] + both[:, 128:]).reshape(3, N, ROWS, 128)
-        for c in range(3):
-            fz_ref[c, i] = both[c]
-
-    loop(N, plane)
+            if later:
+                fy_ref[1, i, j] = sy[1][j]
+                fy_ref[2, i, j] = syz
+                fz_ref[2, i, j] = sz[2][j]
+        if not later:
+            back_yz(sy, sz, i, wb_ref, fz_ref, fy_ref)
+
+    if tile:
+        loop(N, plane)
+    else:
+        plane(0)
+        plane(DEG)
+        loop(N - 2, lambda at: plane(at + 1, True))
+
+
+def late_back(wb_ref, work_0, fz_ref, fy_ref):
+    sx_ref, sz_ref, sy_ref = work_0
+
+    def plane(at):
+        i = at + 1
+        sxy = [sx_ref[1, i, j] for j in range(N)]
+        sxz = [sx_ref[2, i, j] for j in range(N)]
+        syy = [sy_ref[1, i, j] for j in range(N)]
+        syz = [sy_ref[2, i, j] for j in range(N)]
+        szz = [sz_ref[2, i, j] for j in range(N)]
+        back_yz((sxy, syy, syz), (sxz, syz, szz), i, wb_ref, fz_ref, fy_ref)
+
+    loop(N - 2, plane)
 
 
 def back(ws_ref, work, out_ref, nodes, planes):
@@ -291,10 +359,12 @@
     give_faces(ctl_ref, face_ref, 0, xe_ref, xo_ref)
 
 
-def finish_second(ws_ref, work, work_0, inner_ref, au_ref):
+def finish_second(wb_ref, ws_ref, work, work_0, inner_ref, au_ref):
     back_loop(ws_ref, work, au_ref, ALL)
     join_y(au_ref)
-    back_loop(ws_ref, work_0, inner_ref, INSIDE)
+    sx_ref, fz_ref, fy_ref = work
+    late_back(wb_ref, work_0, fz_ref, fy_ref)
+    back_loop(ws_ref, (work_0[0], fz_ref, fy_ref), inner_ref, INSIDE)
     join_y(inner_ref)
 
 
@@ -321,7 +391,7 @@
 
 def first_mid_kernel(wg_ref, xr_ref, t0_ref, t1_ref, *outs):
     for tile, src in enumerate((t0_ref, t1_ref)):
-        u_out, gx_ref, gz_ref = outs[3 * tile : 3 * tile + 3]
+        u_out, gx_ref, gz_ref, gy_ref = outs[4 * tile : 4 * tile + 4]
 
         def plane(at):
             planes = [[with_halo(src, xr_ref, None, c, c, i, at + 1, tile) for i in range(N)] for c in range(3)]
@@ -331,12 +401,13 @@
             gradients(planes, at, wg_ref, gx_ref, gz_ref)
 
         loop(N - 2, plane)
+        inner_slopes(u_out, gy_ref)
 
 
 def first_kernel(tile, *refs):
     refs = list(refs)
     take = lambda count: [refs.pop(0) for _ in range(count)]
-    ctl_ref, wg_ref, wb_ref, ws_ref, lam_ref, mu_ref, src, xr_ref, yr_ref, mid_ref, gx_ref, gz_ref = take(12)
+    ctl_ref, wg_ref, wb_ref, ws_ref, lam_ref, mu_ref, src, xr_ref, yr_ref, gx_ref, gz_ref, gy_ref = take(12)
     if tile == 0:
         (dg_ref,) = take(1)
         u_out, face_ref, xe_ref, xo_ref = take(4)
@@ -351,12 +422,12 @@
             for i in range(N):
                 u_out[c, i, k] = planes[c][i]
         gradients(planes, DEG * k, wg_ref, sx_ref, fz_ref)
-    stress(by_j(mid_ref, u_out), mixed(gx_ref, sx_ref), mixed(gz_ref, fz_ref), lam_ref, mu_ref, wb_ref, *work)
+    stress(tile, u_out, gy_ref, mixed(gx_ref, sx_ref), mixed(gz_ref, fz_ref), lam_ref, mu_ref, wb_ref, *work)
     if tile == 0:
         send_first(ctl_ref, ws_ref, work, face_ref, xe_ref, xo_ref)
         give_faces(ctl_ref, dg_ref, 3, xe_ref, xo_ref)
     else:
-        finish_second(ws_ref, work, work_0, inner_ref, au_ref)
+        finish_second(wb_ref, ws_ref, work, work_0, inner_ref, au_ref)
 
 
 def corner_kernel(ctl_ref, xe_ref, xo_ref, face_ref, inner_ref, au_ref, *refs):
@@ -407,7 +478,7 @@
         ins.append((u_ref, b_ref, None if with_diag else take(1)[0], take(1)[0] if stage else None))
     for tile in range(2):
         u_ref, b_ref, inv_ref, change_ref = ins[tile]
-        u_out, gx_ref, gz_ref = take(3)
+        u_out, gx_ref, gz_ref, gy_ref = take(4)
         change_out = take(1 if stage < CHEB - 1 else 0)
         inv_out = take(1)[0] if with_diag else None
 
@@ -430,6 +501,7 @@
             gradients(planes, at, wg_ref, gx_ref, gz_ref)
 
         loop(N - 2, plane)
+        inner_slopes(u_out, gy_ref)
 
 
 def edge_kernel(tile, stage, with_diag, *refs):
@@ -439,7 +511,7 @@
     faces = take(4)
     parts = (by_i(face_in, inner_in), whole(au_in))
     diag_parts = [whole(ref) for ref in take(2)] if with_diag else None
-    mid_ref, gx_ref, gz_ref, u_ref, b_ref = take(5)
+    gx_ref, gz_ref, gy_ref, u_ref, b_ref = take(5)
     inv_ref = None if with_diag else take(1)[0]
     change_ref = take(1)[0] if stage else None
     work_0 = take(3) if tile else None
@@ -467,11 +539,11 @@
                 u_out[c, i, k] = planes[c][i]
         gradients(planes, j, wg_ref, sx_ref, fz_ref)
 
-    stress(by_j(mid_ref, u_out), mixed(gx_ref, sx_ref), mixed(gz_ref, fz_ref), lam_ref, mu_ref, wb_ref, *work)
+    stress(tile, u_out, gy_ref, mixed(gx_ref, sx_ref), mixed(gz_ref, fz_ref), lam_ref, mu_ref, wb_ref, *work)
     if tile == 0:
         send_first(ctl_ref, ws_ref, work, *outs)
     else:
-        finish_second(ws_ref, work, work_0, *outs)
+        finish_second(wb_ref, ws_ref, work, work_0, *outs)
 
 
 def lane_pick(value, index):
@@ -692,11 +764,11 @@
     work = (FIELD,) * 3
     both_faces = ((6, N, SIDE, 128),) * 2
     diag = tuple(call(diag_kernel, 0, (*coeffs[tile], ratio_i, ratio_z, w_share), (FIELD,))[0] for tile in range(2))
-    got = call(first_mid_kernel, 0, (w_grad, x_halo, *loads[0][:2]), (MID,) * 6)
-    u_mid = [got[0], got[3]]
+    got = call(first_mid_kernel, 0, (w_grad, x_halo, *loads[0][:2]), (MID, MID, MID, FIELD) * 2)
+    u_mid = [got[0], got[4]]
 
     def first(tile, extra, outs, scratch):
-        inputs = (ctl, *weights, *coeffs[tile], loads[0][tile], x_halo, y_halo, *got[3 * tile : 3 * tile + 3], *extra)
+        inputs = (ctl, *weights, *coeffs[tile], loads[0][tile], x_halo, y_halo, *got[4 * tile + 1 : 4 * tile + 4], *extra)
         return call(lambda *refs: first_kernel(tile, *refs), 0, inputs, (EDGE,) + outs, scratch)
 
     edge_0, face, *rest = first(0, diag[:1], (FACE, *both_faces, *work), 0)
@@ -720,22 +792,22 @@
             inputs += (u_mid[tile], b[tile]) + (() if with_diag else (inv_mid[tile],))
             inputs += (change_mid[tile],) if stage else ()
         keep_change = 1 if stage < CHEB - 1 else 0
-        each = 3 + keep_change + keep_inv
-        outs = (MID,) * each * 2
+        each = 4 + keep_change + keep_inv
+        outs = ((MID, MID, MID, FIELD) + (MID,) * (keep_change + keep_inv)) * 2
         results = call(lambda *refs: mid_kernel(stage, with_diag, *refs), 0, inputs, outs)
         slopes = [None, None]
         for tile in range(2):
             got = results[each * tile : each * (tile + 1)]
             u_mid[tile] = got[0]
-            slopes[tile] = got[1:3]
+            slopes[tile] = got[1:4]
             if keep_change:
-                change_mid[tile] = got[3]
+                change_mid[tile] = got[4]
             if with_diag:
                 inv_mid[tile] = got[-1]
 
         for tile in range(2):
             inputs = (ctl, *weights, *coeffs[tile], *sums, *x_got, *y_got) + (diag if with_diag else ())
-            inputs += (u_mid[tile], *slopes[tile], u_edge[tile], b[tile])
+            inputs += (*slopes[tile], u_edge[tile], b[tile])
             inputs += () if with_diag else (inv_edge[tile],)
             inputs += (change_edge[tile],) if stage else ()
             inputs += tuple(work_0) if tile else ()

time: 169 us -> 165 us (0.976)
  starting transfers between devices: 66.8 us -> 59.1 us
  waiting for transfers between devices: 38 us -> 40.2 us
    ppermute x14, starting transfers between devices: 54.6 us -> 46.9 us  [swaps(): lax.ppermute(odd, axis, [(i, ((i + 1 ^ 1) - 1) % size) for i in range(siz...]
    ppermute x14, waiting for transfers between devices: 35.1 us -> 37.3 us  [swaps(): lax.ppermute(odd, axis, [(i, ((i + 1 ^ 1) - 1) % size) for i in range(siz...]
  transfers between devices with their start and end apart: 30 -> 30, of which waited for: 14 -> 14; matrix products, arithmetic and copies ran while one was open for 0% -> 0% of each run, Pallas kernels for 25% -> 29%
where the time goes in v4:
time: 165 us
  Pallas kernels  60.8 us (37%)
  starting transfers between devices  59.1 us (36%)
  waiting for transfers between devices  40.2 us (24%)
  between operations  2.82 us (2%)
    pallas_call x37, Pallas kernels, call(): pl.pallas_call(kernel, in_specs=[SM] * smem + [VM] * (len(inputs) - smem)...  60.8 us
    ppermute x14, starting transfers between devices, swaps(): lax.ppermute(odd, axis, [(i, ((i + 1 ^ 1) - 1) % size) for i in range(siz...  46.9 us
    ppermute x14, waiting for transfers between devices, swaps(): lax.ppermute(odd, axis, [(i, ((i + 1 ^ 1) - 1) % size) for i in range(siz...  37.3 us
    ppermute x2, starting transfers between devices, from_next(): return lax.ppermute(value, axis, [(i, (i - 1) % size) for i in range(size)])  11 us
  transfers between devices with their start and end apart: 30, of which 14 were waited for; matrix products, arithmetic and copies ran while one was open for 0% of the time, Pallas kernels for 29%

profile of v4, /device:TPU:0, one launch (start us, length us, event | category | flops | bytes accessed | tf_op | source)
XLA Modules:
  0.0 164.5 jit_solution(230066460417887984)
XLA Ops:
  6.4 7.4 %collective-permute-start = (f32[6,8,4,128]{3,2,1,0:T(4,128)S(1)}, f32[6,8,4,128]{3,2,1,0:T(4,128)S(1)}, u32[]{:S(2)}, u32[]{:S(2)}) collective-permute-start(f32[6,8,4,128]{3,2,1,0:T(4,128)S(1)} %pad_maximum_fusion), channel_id=1, source_target_pairs={{0,15},{1,0},{2,1},{3,2},{4,3},{5,4},{6,5},{7,6},{8,7},{9,8},{10,9... | collective-permute-start | bytes 294920 | tf_op jit(solution)/shard_map/ppermute | solution.py:725
  16.7 3.5 %collective-permute-start.1 = (f32[6,8,4,128]{3,2,1,0:T(4,128)S(1)}, f32[6,8,4,128]{3,2,1,0:T(4,128)S(1)}, u32[]{:S(2)}, u32[]{:S(2)}) collective-permute-start(f32[6,8,4,128]{3,2,1,0:T(4,128)S(1)} %shard_map.134), channel_id=1, source_target_pairs={{0,240},{16,0},{32,16},{48,32},{64,48},{80,64},{96,80},{112,96},{1... | collective-permute-start | bytes 294920 | tf_op jit(solution)/shard_map/ppermute | solution.py:725
  25.2 7.8 %collective-permute-start.3 = (f32[6,8,4,128]{3,2,1,0:T(4,128)S(1)}, f32[6,8,4,128]{3,2,1,0:T(4,128)S(1)}, u32[]{:S(2)}, u32[]{:S(2)}) collective-permute-start(f32[6,8,4,128]{3,2,1,0:T(4,128)S(1)} %get-tuple-element.199), channel_id=1, source_target_pairs={{0,15},{1,2},{2,1},{3,4},{4,3},{5,6},{6,5},{7,8},{8,7},{9,10},{10,... | collective-permute-start | bytes 294920 | tf_op jit(solution)/shard_map/ppermute | solution.py:711
  34.3 3.9 %shard_map.138 = (f32[3,8,2,8,128]{4,3,2,1,0:T(8,128)S(1)}, f32[3,6,8,8,128]{4,3,2,1,0:T(8,128)S(1)}, f32[3,8,8,8,128]{4,3,2,1,0:T(8,128)S(1)}) custom-call(f32[8,8,128]{2,1,0:T(8,128)S(1)} %broadcast_in_dim.2.ctl_ref.refs_0_, bf16[256,256]{1,0:T(8,128)(2,1)S(1)} %copy-done, bf16[256,256]{1,0:T(8,128)(2,1)S(1)} %copy-done.1, bf16[256,128]{1,0:T(8,128)(2,1)S(1)} %copy-done.2, ...), custom_call_target="tpu_custom_call" | custom-call | tf_op jit(solution)/shard_map/pallas_call | solution.py:699
  38.5 3.8 %collective-permute-start.5 = (f32[6,8,4,128]{3,2,1,0:T(4,128)S(1)}, f32[6,8,4,128]{3,2,1,0:T(4,128)S(1)}, u32[]{:S(2)}, u32[]{:S(2)}) collective-permute-start(f32[6,8,4,128]{3,2,1,0:T(4,128)S(1)} %get-tuple-element.201), channel_id=1, source_target_pairs={{0,240},{16,32},{32,16},{48,64},{64,48},{80,96},{96,80},{112,128},... | collective-permute-start | bytes 294920 | tf_op jit(solution)/shard_map/ppermute | solution.py:711
  48.2 3.8 %collective-permute-start.7 = (f32[3,8,4,128]{3,2,1,0:T(4,128)S(1)}, f32[3,8,4,128]{3,2,1,0:T(4,128)S(1)}, u32[]{:S(2)}, u32[]{:S(2)}) collective-permute-start(f32[3,8,4,128]{3,2,1,0:T(4,128)S(1)} %get-tuple-element.223), channel_id=1, source_target_pairs={{0,15},{1,2},{2,1},{3,4},{4,3},{5,6},{6,5},{7,8},{8,7},{9,10},{10,... | collective-permute-start | bytes 147464 | tf_op jit(solution)/shard_map/ppermute | solution.py:711
  51.9 4.0 %shard_map.144 = (f32[3,8,2,8,128]{4,3,2,1,0:T(8,128)S(1)}, f32[3,8,2,8,128]{4,3,2,1,0:T(8,128)S(1)}, f32[3,8,2,8,128]{4,3,2,1,0:T(8,128)S(1)}, f32[3,6,8,8,128]{4,3,2,1,0:T(8,128)S(1)}, f32[3,8,8,8,128]{4,3,2,1,0:T(8,128)S(1)}) custom-call(f32[8,8,128]{2,1,0:T(8,128)S(1)} %broadcast_in_dim.2.ctl_ref.refs_0_, bf16[256,256]{1,0:T(8,128)(2,1)S(1)} %copy-done, ...), custom_call_target="tpu_custom_call" | custom-call | tf_op jit(solution)/shard_map/pallas_call | solution.py:699
  57.9 4.1 %collective-permute-start.9 = (f32[3,8,4,128]{3,2,1,0:T(4,128)S(1)}, f32[3,8,4,128]{3,2,1,0:T(4,128)S(1)}, u32[]{:S(2)}, u32[]{:S(2)}) collective-permute-start(f32[3,8,4,128]{3,2,1,0:T(4,128)S(1)} %get-tuple-element.225), channel_id=1, source_target_pairs={{0,240},{16,32},{32,16},{48,64},{64,48},{80,96},{96,80},{112,128},... | collective-permute-start | bytes 147464 | tf_op jit(solution)/shard_map/ppermute | solution.py:711
  67.2 2.9 %collective-permute-start.11 = (f32[3,8,4,128]{3,2,1,0:T(4,128)S(1)}, f32[3,8,4,128]{3,2,1,0:T(4,128)S(1)}, u32[]{:S(2)}, u32[]{:S(2)}) collective-permute-start(f32[3,8,4,128]{3,2,1,0:T(4,128)S(1)} %get-tuple-element.251), channel_id=1, source_target_pairs={{0,15},{1,2},{2,1},{3,4},{4,3},{5,6},{6,5},{7,8},{8,7},{9,10},{10,... | collective-permute-start | bytes 147464 | tf_op jit(solution)/shard_map/ppermute | solution.py:711
  70.1 4.0 %shard_map.148 = (f32[3,8,2,8,128]{4,3,2,1,0:T(8,128)S(1)}, f32[3,8,2,8,128]{4,3,2,1,0:T(8,128)S(1)}, f32[3,6,8,8,128]{4,3,2,1,0:T(8,128)S(1)}, f32[3,8,8,8,128]{4,3,2,1,0:T(8,128)S(1)}) custom-call(f32[8,8,128]{2,1,0:T(8,128)S(1)} %broadcast_in_dim.2.ctl_ref.refs_0_, bf16[256,256]{1,0:T(8,128)(2,1)S(1)} %copy-done, bf16[256,256]{1,0:T(8,128)(2,1)S(1)} %copy-done.1, ...), custom_call_target="tpu_custom_call" | custom-call | tf_op jit(solution)/shard_map/pallas_call | solution.py:699
  74.1 3.2 %collective-permute-done.11.xo_ref.refs_6_.refs_10_ = f32[3,8,4,128]{3,2,1,0:T(4,128)S(1)} collective-permute-done((f32[3,8,4,128]{3,2,1,0:T(4,128)S(1)}, f32[3,8,4,128]{3,2,1,0:T(4,128)S(1)}, u32[]{:S(2)}, u32[]{:S(2)}) %collective-permute-start.11) | collective-permute-done | bytes 49184 | tf_op jit(solution)/shard_map/ppermute | solution.py:711
  77.5 3.6 %collective-permute-start.13 = (f32[3,8,4,128]{3,2,1,0:T(4,128)S(1)}, f32[3,8,4,128]{3,2,1,0:T(4,128)S(1)}, u32[]{:S(2)}, u32[]{:S(2)}) collective-permute-start(f32[3,8,4,128]{3,2,1,0:T(4,128)S(1)} %get-tuple-element.253), channel_id=1, source_target_pairs={{0,240},{16,32},{32,16},{48,64},{64,48},{80,96},{96,80},{112,128},... | collective-permute-start | bytes 147464 | tf_op jit(solution)/shard_map/ppermute | solution.py:711
  87.9 4.0 %shard_map.152 = (f32[3,8,2,8,128]{4,3,2,1,0:T(8,128)S(1)}, f32[3,6,8,8,128]{4,3,2,1,0:T(8,128)S(1)}, f32[3,8,8,8,128]{4,3,2,1,0:T(8,128)S(1)}) custom-call(f32[8,8,128]{2,1,0:T(8,128)S(1)} %broadcast_in_dim.2.ctl_ref.refs_0_, bf16[256,256]{1,0:T(8,128)(2,1)S(1)} %copy-done, bf16[256,256]{1,0:T(8,128)(2,1)S(1)} %copy-done.1, bf16[256,128]{1,0:T(8,128)(2,1)S(1)} %copy-done.2, ...), custom_call_target="tpu_custom_call" | custom-call | tf_op jit(solution)/shard_map/pallas_call | solution.py:699
  91.9 4.4 %collective-permute-done.15.xo_ref.refs_6_.refs_10_ = f32[3,8,4,128]{3,2,1,0:T(4,128)S(1)} collective-permute-done((f32[3,8,4,128]{3,2,1,0:T(4,128)S(1)}, f32[3,8,4,128]{3,2,1,0:T(4,128)S(1)}, u32[]{:S(2)}, u32[]{:S(2)}) %collective-permute-start.15) | collective-permute-done | bytes 49184 | tf_op jit(solution)/shard_map/ppermute | solution.py:711
  96.5 3.6 %collective-permute-start.17 = (f32[3,8,4,128]{3,2,1,0:T(4,128)S(1)}, f32[3,8,4,128]{3,2,1,0:T(4,128)S(1)}, u32[]{:S(2)}, u32[]{:S(2)}) collective-permute-start(f32[3,8,4,128]{3,2,1,0:T(4,128)S(1)} %get-tuple-element.277), channel_id=1, source_target_pairs={{0,240},{16,32},{32,16},{48,64},{64,48},{80,96},{96,80},{112,128},... | collective-permute-start | bytes 147464 | tf_op jit(solution)/shard_map/ppermute | solution.py:711
  106.9 4.0 %shard_map.156 = (f32[3,8,2,8,128]{4,3,2,1,0:T(8,128)S(1)}, f32[3,8,2,8,128]{4,3,2,1,0:T(8,128)S(1)}, f32[3,6,8,8,128]{4,3,2,1,0:T(8,128)S(1)}, f32[3,8,8,8,128]{4,3,2,1,0:T(8,128)S(1)}) custom-call(f32[8,8,128]{2,1,0:T(8,128)S(1)} %broadcast_in_dim.2.ctl_ref.refs_0_, bf16[256,256]{1,0:T(8,128)(2,1)S(1)} %copy-done, bf16[256,256]{1,0:T(8,128)(2,1)S(1)} %copy-done.1, ...), custom_call_target="tpu_custom_call" | custom-call | tf_op jit(solution)/shard_map/pallas_call | solution.py:699
  110.8 4.6 %collective-permute-done.19.xo_ref.refs_6_.refs_10_ = f32[3,8,4,128]{3,2,1,0:T(4,128)S(1)} collective-permute-done((f32[3,8,4,128]{3,2,1,0:T(4,128)S(1)}, f32[3,8,4,128]{3,2,1,0:T(4,128)S(1)}, u32[]{:S(2)}, u32[]{:S(2)}) %collective-permute-start.19) | collective-permute-done | bytes 49184 | tf_op jit(solution)/shard_map/ppermute | solution.py:711
  115.6 3.9 %collective-permute-start.21 = (f32[3,8,4,128]{3,2,1,0:T(4,128)S(1)}, f32[3,8,4,128]{3,2,1,0:T(4,128)S(1)}, u32[]{:S(2)}, u32[]{:S(2)}) collective-permute-start(f32[3,8,4,128]{3,2,1,0:T(4,128)S(1)} %get-tuple-element.297), channel_id=1, source_target_pairs={{0,240},{16,32},{32,16},{48,64},{64,48},{80,96},{96,80},{112,128},... | collective-permute-start | bytes 147464 | tf_op jit(solution)/shard_map/ppermute | solution.py:711
  125.9 4.0 %shard_map.160 = (f32[3,8,2,8,128]{4,3,2,1,0:T(8,128)S(1)}, f32[3,8,2,8,128]{4,3,2,1,0:T(8,128)S(1)}, f32[3,6,8,8,128]{4,3,2,1,0:T(8,128)S(1)}, f32[3,8,8,8,128]{4,3,2,1,0:T(8,128)S(1)}) custom-call(f32[8,8,128]{2,1,0:T(8,128)S(1)} %broadcast_in_dim.2.ctl_ref.refs_0_, bf16[256,256]{1,0:T(8,128)(2,1)S(1)} %copy-done, bf16[256,256]{1,0:T(8,128)(2,1)S(1)} %copy-done.1, ...), custom_call_target="tpu_custom_call" | custom-call | tf_op jit(solution)/shard_map/pallas_call | solution.py:699
  129.9 4.6 %collective-permute-done.23.refs_6_.xo_ref.refs_10_ = f32[3,8,4,128]{3,2,1,0:T(4,128)S(1)} collective-permute-done((f32[3,8,4,128]{3,2,1,0:T(4,128)S(1)}, f32[3,8,4,128]{3,2,1,0:T(4,128)S(1)}, u32[]{:S(2)}, u32[]{:S(2)}) %collective-permute-start.23) | collective-permute-done | bytes 49184 | tf_op jit(solution)/shard_map/ppermute | solution.py:711
  134.6 4.1 %collective-permute-start.25 = (f32[3,8,4,128]{3,2,1,0:T(4,128)S(1)}, f32[3,8,4,128]{3,2,1,0:T(4,128)S(1)}, u32[]{:S(2)}, u32[]{:S(2)}) collective-permute-start(f32[3,8,4,128]{3,2,1,0:T(4,128)S(1)} %get-tuple-element.326), channel_id=1, source_target_pairs={{0,240},{16,32},{32,16},{48,64},{64,48},{80,96},{96,80},{112,128},... | collective-permute-start | bytes 147464 | tf_op jit(solution)/shard_map/ppermute | solution.py:711
  144.8 4.0 %shard_map.164 = (f32[3,8,2,8,128]{4,3,2,1,0:T(8,128)S(1)}, f32[3,6,8,8,128]{4,3,2,1,0:T(8,128)S(1)}, f32[3,8,8,8,128]{4,3,2,1,0:T(8,128)S(1)}) custom-call(f32[8,8,128]{2,1,0:T(8,128)S(1)} %broadcast_in_dim.2.ctl_ref.refs_0_, bf16[256,256]{1,0:T(8,128)(2,1)S(1)} %copy-done, bf16[256,256]{1,0:T(8,128)(2,1)S(1)} %copy-done.1, bf16[256,128]{1,0:T(8,128)(2,1)S(1)} %copy-done.2, ...), custom_call_target="tpu_custom_call" | custom-call | tf_op jit(solution)/shard_map/pallas_call | solution.py:699
  148.8 4.7 %collective-permute-done.27.xo_ref.refs_7_ = f32[3,8,4,128]{3,2,1,0:T(4,128)S(1)} collective-permute-done((f32[3,8,4,128]{3,2,1,0:T(4,128)S(1)}, f32[3,8,4,128]{3,2,1,0:T(4,128)S(1)}, u32[]{:S(2)}, u32[]{:S(2)}) %collective-permute-start.27) | collective-permute-done | bytes 49184 | tf_op jit(solution)/shard_map/ppermute | solution.py:711
  153.7 4.5 %collective-permute-start.29 = (f32[3,8,4,128]{3,2,1,0:T(4,128)S(1)}, f32[3,8,4,128]{3,2,1,0:T(4,128)S(1)}, u32[]{:S(2)}, u32[]{:S(2)}) collective-permute-start(f32[3,8,4,128]{3,2,1,0:T(4,128)S(1)} %get-tuple-element.349), channel_id=1, source_target_pairs={{0,240},{16,32},{32,16},{48,64},{64,48},{80,96},{96,80},{112,128},... | collective-permute-start | bytes 147464 | tf_op jit(solution)/shard_map/ppermute | solution.py:711
  (97 shorter events, 59.5 us)
Async XLA Ops:
  6.4 10.4 %collective-permute-start = (f32[6,8,4,128]{3,2,1,0:T(4,128)S(1)}, f32[6,8,4,128]{3,2,1,0:T(4,128)S(1)}, u32[]{:S(2)}, u32[]{:S(2)}) collective-permute-start(f32[6,8,4,128]{3,2,1,0:T(4,128)S(1)} %pad_maximum_fusion), channel_id=1, source_target_pairs={{0,15},{1,0},{2,1},{3,2},{4,3},{5,4},{6,5},{7,6},{8,7},{9,8},{10,9... | collective-permute-start | bytes 294920 | tf_op jit(solution)/shard_map/ppermute | solution.py:725
  16.7 7.4 %collective-permute-start.1 = (f32[6,8,4,128]{3,2,1,0:T(4,128)S(1)}, f32[6,8,4,128]{3,2,1,0:T(4,128)S(1)}, u32[]{:S(2)}, u32[]{:S(2)}) collective-permute-start(f32[6,8,4,128]{3,2,1,0:T(4,128)S(1)} %shard_map.134), channel_id=1, source_target_pairs={{0,240},{16,0},{32,16},{48,32},{64,48},{80,64},{96,80},{112,96},{1... | collective-permute-start | bytes 294920 | tf_op jit(solution)/shard_map/ppermute | solution.py:725
  25.1 13.1 %collective-permute-start.2 = (f32[6,8,4,128]{3,2,1,0:T(4,128)S(1)}, f32[6,8,4,128]{3,2,1,0:T(4,128)S(1)}, u32[]{:S(2)}, u32[]{:S(2)}) collective-permute-start(f32[6,8,4,128]{3,2,1,0:T(4,128)S(1)} %get-tuple-element.198), channel_id=1, source_target_pairs={{0,1},{1,0},{2,3},{3,2},{4,5},{5,4},{6,7},{7,6},{8,9},{9,8},{10,11... | collective-permute-start | bytes 294920 | tf_op jit(solution)/shard_map/ppermute | solution.py:712
  25.2 13.0 %collective-permute-start.3 = (f32[6,8,4,128]{3,2,1,0:T(4,128)S(1)}, f32[6,8,4,128]{3,2,1,0:T(4,128)S(1)}, u32[]{:S(2)}, u32[]{:S(2)}) collective-permute-start(f32[6,8,4,128]{3,2,1,0:T(4,128)S(1)} %get-tuple-element.199), channel_id=1, source_target_pairs={{0,15},{1,2},{2,1},{3,4},{4,3},{5,6},{6,5},{7,8},{8,7},{9,10},{10,... | collective-permute-start | bytes 294920 | tf_op jit(solution)/shard_map/ppermute | solution.py:711
  38.4 6.4 %collective-permute-start.4 = (f32[6,8,4,128]{3,2,1,0:T(4,128)S(1)}, f32[6,8,4,128]{3,2,1,0:T(4,128)S(1)}, u32[]{:S(2)}, u32[]{:S(2)}) collective-permute-start(f32[6,8,4,128]{3,2,1,0:T(4,128)S(1)} %get-tuple-element.200), channel_id=1, source_target_pairs={{0,16},{16,0},{32,48},{48,32},{64,80},{80,64},{96,112},{112,96},{1... | collective-permute-start | bytes 294920 | tf_op jit(solution)/shard_map/ppermute | solution.py:712
  38.5 8.6 %collective-permute-start.5 = (f32[6,8,4,128]{3,2,1,0:T(4,128)S(1)}, f32[6,8,4,128]{3,2,1,0:T(4,128)S(1)}, u32[]{:S(2)}, u32[]{:S(2)}) collective-permute-start(f32[6,8,4,128]{3,2,1,0:T(4,128)S(1)} %get-tuple-element.201), channel_id=1, source_target_pairs={{0,240},{16,32},{32,16},{48,64},{64,48},{80,96},{96,80},{112,128},... | collective-permute-start | bytes 294920 | tf_op jit(solution)/shard_map/ppermute | solution.py:711
  48.1 7.9 %collective-permute-start.6 = (f32[3,8,4,128]{3,2,1,0:T(4,128)S(1)}, f32[3,8,4,128]{3,2,1,0:T(4,128)S(1)}, u32[]{:S(2)}, u32[]{:S(2)}) collective-permute-start(f32[3,8,4,128]{3,2,1,0:T(4,128)S(1)} %get-tuple-element.222), channel_id=1, source_target_pairs={{0,1},{1,0},{2,3},{3,2},{4,5},{5,4},{6,7},{7,6},{8,9},{9,8},{10,11... | collective-permute-start | bytes 147464 | tf_op jit(solution)/shard_map/ppermute | solution.py:712
  48.2 9.6 %collective-permute-start.7 = (f32[3,8,4,128]{3,2,1,0:T(4,128)S(1)}, f32[3,8,4,128]{3,2,1,0:T(4,128)S(1)}, u32[]{:S(2)}, u32[]{:S(2)}) collective-permute-start(f32[3,8,4,128]{3,2,1,0:T(4,128)S(1)} %get-tuple-element.223), channel_id=1, source_target_pairs={{0,15},{1,2},{2,1},{3,4},{4,3},{5,6},{6,5},{7,8},{8,7},{9,10},{10,... | collective-permute-start | bytes 147464 | tf_op jit(solution)/shard_map/ppermute | solution.py:711
  57.8 6.2 %collective-permute-start.8 = (f32[3,8,4,128]{3,2,1,0:T(4,128)S(1)}, f32[3,8,4,128]{3,2,1,0:T(4,128)S(1)}, u32[]{:S(2)}, u32[]{:S(2)}) collective-permute-start(f32[3,8,4,128]{3,2,1,0:T(4,128)S(1)} %get-tuple-element.224), channel_id=1, source_target_pairs={{0,16},{16,0},{32,48},{48,32},{64,80},{80,64},{96,112},{112,96},{1... | collective-permute-start | bytes 147464 | tf_op jit(solution)/shard_map/ppermute | solution.py:712
  57.9 8.3 %collective-permute-start.9 = (f32[3,8,4,128]{3,2,1,0:T(4,128)S(1)}, f32[3,8,4,128]{3,2,1,0:T(4,128)S(1)}, u32[]{:S(2)}, u32[]{:S(2)}) collective-permute-start(f32[3,8,4,128]{3,2,1,0:T(4,128)S(1)} %get-tuple-element.225), channel_id=1, source_target_pairs={{0,240},{16,32},{32,16},{48,64},{64,48},{80,96},{96,80},{112,128},... | collective-permute-start | bytes 147464 | tf_op jit(solution)/shard_map/ppermute | solution.py:711
  67.1 7.0 %collective-permute-start.10 = (f32[3,8,4,128]{3,2,1,0:T(4,128)S(1)}, f32[3,8,4,128]{3,2,1,0:T(4,128)S(1)}, u32[]{:S(2)}, u32[]{:S(2)}) collective-permute-start(f32[3,8,4,128]{3,2,1,0:T(4,128)S(1)} %get-tuple-element.250), channel_id=1, source_target_pairs={{0,1},{1,0},{2,3},{3,2},{4,5},{5,4},{6,7},{7,6},{8,9},{9,8},{10,11... | collective-permute-start | bytes 147464 | tf_op jit(solution)/shard_map/ppermute | solution.py:712
  67.2 10.0 %collective-permute-start.11 = (f32[3,8,4,128]{3,2,1,0:T(4,128)S(1)}, f32[3,8,4,128]{3,2,1,0:T(4,128)S(1)}, u32[]{:S(2)}, u32[]{:S(2)}) collective-permute-start(f32[3,8,4,128]{3,2,1,0:T(4,128)S(1)} %get-tuple-element.251), channel_id=1, source_target_pairs={{0,15},{1,2},{2,1},{3,4},{4,3},{5,6},{6,5},{7,8},{8,7},{9,10},{10,... | collective-permute-start | bytes 147464 | tf_op jit(solution)/shard_map/ppermute | solution.py:711
  77.5 8.1 %collective-permute-start.13 = (f32[3,8,4,128]{3,2,1,0:T(4,128)S(1)}, f32[3,8,4,128]{3,2,1,0:T(4,128)S(1)}, u32[]{:S(2)}, u32[]{:S(2)}) collective-permute-start(f32[3,8,4,128]{3,2,1,0:T(4,128)S(1)} %get-tuple-element.253), channel_id=1, source_target_pairs={{0,240},{16,32},{32,16},{48,64},{64,48},{80,96},{96,80},{112,128},... | collective-permute-start | bytes 147464 | tf_op jit(solution)/shard_map/ppermute | solution.py:711
  86.6 9.7 %collective-permute-start.15 = (f32[3,8,4,128]{3,2,1,0:T(4,128)S(1)}, f32[3,8,4,128]{3,2,1,0:T(4,128)S(1)}, u32[]{:S(2)}, u32[]{:S(2)}) collective-permute-start(f32[3,8,4,128]{3,2,1,0:T(4,128)S(1)} %get-tuple-element.275), channel_id=1, source_target_pairs={{0,15},{1,2},{2,1},{3,4},{4,3},{5,6},{6,5},{7,8},{8,7},{9,10},{10,... | collective-permute-start | bytes 147464 | tf_op jit(solution)/shard_map/ppermute | solution.py:711
  96.5 8.1 %collective-permute-start.17 = (f32[3,8,4,128]{3,2,1,0:T(4,128)S(1)}, f32[3,8,4,128]{3,2,1,0:T(4,128)S(1)}, u32[]{:S(2)}, u32[]{:S(2)}) collective-permute-start(f32[3,8,4,128]{3,2,1,0:T(4,128)S(1)} %get-tuple-element.277), channel_id=1, source_target_pairs={{0,240},{16,32},{32,16},{48,64},{64,48},{80,96},{96,80},{112,128},... | collective-permute-start | bytes 147464 | tf_op jit(solution)/shard_map/ppermute | solution.py:711
  105.6 9.9 %collective-permute-start.19 = (f32[3,8,4,128]{3,2,1,0:T(4,128)S(1)}, f32[3,8,4,128]{3,2,1,0:T(4,128)S(1)}, u32[]{:S(2)}, u32[]{:S(2)}) collective-permute-start(f32[3,8,4,128]{3,2,1,0:T(4,128)S(1)} %get-tuple-element.295), channel_id=1, source_target_pairs={{0,15},{1,2},{2,1},{3,4},{4,3},{5,6},{6,5},{7,8},{8,7},{9,10},{10,... | collective-permute-start | bytes 147464 | tf_op jit(solution)/shard_map/ppermute | solution.py:711
  115.5 6.1 %collective-permute-start.20 = (f32[3,8,4,128]{3,2,1,0:T(4,128)S(1)}, f32[3,8,4,128]{3,2,1,0:T(4,128)S(1)}, u32[]{:S(2)}, u32[]{:S(2)}) collective-permute-start(f32[3,8,4,128]{3,2,1,0:T(4,128)S(1)} %get-tuple-element.296), channel_id=1, source_target_pairs={{0,16},{16,0},{32,48},{48,32},{64,80},{80,64},{96,112},{112,96},{1... | collective-permute-start | bytes 147464 | tf_op jit(solution)/shard_map/ppermute | solution.py:712
  115.6 8.1 %collective-permute-start.21 = (f32[3,8,4,128]{3,2,1,0:T(4,128)S(1)}, f32[3,8,4,128]{3,2,1,0:T(4,128)S(1)}, u32[]{:S(2)}, u32[]{:S(2)}) collective-permute-start(f32[3,8,4,128]{3,2,1,0:T(4,128)S(1)} %get-tuple-element.297), channel_id=1, source_target_pairs={{0,240},{16,32},{32,16},{48,64},{64,48},{80,96},{96,80},{112,128},... | collective-permute-start | bytes 147464 | tf_op jit(solution)/shard_map/ppermute | solution.py:711
  124.7 9.7 %collective-permute-start.23 = (f32[3,8,4,128]{3,2,1,0:T(4,128)S(1)}, f32[3,8,4,128]{3,2,1,0:T(4,128)S(1)}, u32[]{:S(2)}, u32[]{:S(2)}) collective-permute-start(f32[3,8,4,128]{3,2,1,0:T(4,128)S(1)} %get-tuple-element.319), channel_id=1, source_target_pairs={{0,15},{1,2},{2,1},{3,4},{4,3},{5,6},{6,5},{7,8},{8,7},{9,10},{10,... | collective-permute-start | bytes 147464 | tf_op jit(solution)/shard_map/ppermute | solution.py:711
  134.5 6.3 %collective-permute-start.24 = (f32[3,8,4,128]{3,2,1,0:T(4,128)S(1)}, f32[3,8,4,128]{3,2,1,0:T(4,128)S(1)}, u32[]{:S(2)}, u32[]{:S(2)}) collective-permute-start(f32[3,8,4,128]{3,2,1,0:T(4,128)S(1)} %get-tuple-element.325), channel_id=1, source_target_pairs={{0,16},{16,0},{32,48},{48,32},{64,80},{80,64},{96,112},{112,96},{1... | collective-permute-start | bytes 147464 | tf_op jit(solution)/shard_map/ppermute | solution.py:712
  134.6 8.1 %collective-permute-start.25 = (f32[3,8,4,128]{3,2,1,0:T(4,128)S(1)}, f32[3,8,4,128]{3,2,1,0:T(4,128)S(1)}, u32[]{:S(2)}, u32[]{:S(2)}) collective-permute-start(f32[3,8,4,128]{3,2,1,0:T(4,128)S(1)} %get-tuple-element.326), channel_id=1, source_target_pairs={{0,240},{16,32},{32,16},{48,64},{64,48},{80,96},{96,80},{112,128},... | collective-permute-start | bytes 147464 | tf_op jit(solution)/shard_map/ppermute | solution.py:711
  143.8 9.7 %collective-permute-start.27 = (f32[3,8,4,128]{3,2,1,0:T(4,128)S(1)}, f32[3,8,4,128]{3,2,1,0:T(4,128)S(1)}, u32[]{:S(2)}, u32[]{:S(2)}) collective-permute-start(f32[3,8,4,128]{3,2,1,0:T(4,128)S(1)} %get-tuple-element.347), channel_id=1, source_target_pairs={{0,15},{1,2},{2,1},{3,4},{4,3},{5,6},{6,5},{7,8},{8,7},{9,10},{10,... | collective-permute-start | bytes 147464 | tf_op jit(solution)/shard_map/ppermute | solution.py:711
  153.6 7.4 %collective-permute-start.28 = (f32[3,8,4,128]{3,2,1,0:T(4,128)S(1)}, f32[3,8,4,128]{3,2,1,0:T(4,128)S(1)}, u32[]{:S(2)}, u32[]{:S(2)}) collective-permute-start(f32[3,8,4,128]{3,2,1,0:T(4,128)S(1)} %get-tuple-element.348), channel_id=1, source_target_pairs={{0,16},{16,0},{32,48},{48,32},{64,80},{80,64},{96,112},{112,96},{1... | collective-permute-start | bytes 147464 | tf_op jit(solution)/shard_map/ppermute | solution.py:712
  153.7 8.1 %collective-permute-start.29 = (f32[3,8,4,128]{3,2,1,0:T(4,128)S(1)}, f32[3,8,4,128]{3,2,1,0:T(4,128)S(1)}, u32[]{:S(2)}, u32[]{:S(2)}) collective-permute-start(f32[3,8,4,128]{3,2,1,0:T(4,128)S(1)} %get-tuple-element.349), channel_id=1, source_target_pairs={{0,240},{16,32},{32,16},{48,64},{64,48},{80,96},{96,80},{112,128},... | collective-permute-start | bytes 147464 | tf_op jit(solution)/shard_map/ppermute | solution.py:711
  (16 other events, 146.6 us)

commit v5 on v4

--- a/solution.py
+++ b/solution.py
@@ -553,7 +553,22 @@
 TILES = ((0, 8), (8, 16), (16, 24), (20, 28))
 
 
-def load_kernel(ctl_ref, in_ref, t0_ref, t1_ref, xl_ref, yb_ref, work_ref):
+def plane_kernel(nodes_z, buf_ref, xl_ref, work_ref):
+    lane = lax.broadcasted_iota(jnp.int32, (ROWS, 128), 1)
+    node = DEG * (lane // N) + lane % N - 1
+    free = (node >= 0) & (node < nodes_z)
+    node = jnp.clip(node, 0, nodes_z - 1)
+    for n in range(2):
+        for c in range(3):
+            at = 3 * n + c
+            work_ref[at, pl.ds(24, 8)] = jnp.zeros((ROWS, 128), F32)
+            for low, high in TILES:
+                work_ref[at, low:high] = jnp.where(free, lane_pick(buf_ref[n, c, low:high], node), 0.0)
+            for j in range(N):
+                xl_ref[3 * n + (1, 0, 2)[c], j] = work_ref[at, pl.ds(j, SIDE, stride=DEG)]
+
+
+def load_kernel(ctl_ref, in_ref, t0_ref, t1_ref, yb_ref, work_ref):
     nodes_x, width = in_ref.shape[1], in_ref.shape[2]
     nodes_z = width // nodes_x
     outs = (t0_ref, t1_ref)
@@ -591,8 +606,6 @@
                     if j == 0:
                         yb_ref[out_c, i, pl.ds(2 * which, 1)] = value[:1]
                         yb_ref[out_c, i, pl.ds(2 * which + 1, 1)] = value[SIDE : SIDE + 1]
-                    if i == 0 and which == 0:
-                        xl_ref[out_c, j] = value[:SIDE]
         return carry
 
     lax.fori_loop(0, 3, component, 0)
@@ -751,11 +764,16 @@
     coeffs = call(coeff_kernel, 1, (lame, ctl, material, weight_z), (grid,) * 4)
     coeffs = [coeffs[:2], coeffs[2:]]
 
+    corner = jnp.stack([guess[:, :, :128], right_side[:, :, :128]])
+    nodes_z = DEG * elems_z - 1
+    (first_plane,) = call(
+        lambda *refs: plane_kernel(nodes_z, *refs), 0, (corner,), ((6, N, SIDE, 128),), 1, (6, nodes_y + SIDE, 128)
+    )
+    x_halo = from_next(first_plane, "gy")
     plane = (3, N, SIDE, 128)
     staged = (nodes_y + 1, nodes_y + SIDE, 128)
-    loads = [call(load_kernel, 0, (ctl, value), (FIELD, FIELD, plane, plane), 1, staged) for value in (guess, right_side)]
-    x_halo = from_next(jnp.concatenate([load[2] for load in loads], 0), "gy")
-    y_halo = jnp.concatenate([load[3] for load in loads], 0)
+    loads = [call(load_kernel, 0, (ctl, value), (FIELD, FIELD, plane), 1, staged) for value in (guess, right_side)]
+    y_halo = jnp.concatenate([load[2] for load in loads], 0)
     (y_halo,) = call(halo_corner_kernel, 0, (x_halo, y_halo), (y_halo.shape,))
     y_halo = from_next(y_halo, "gx")
     ratio_z = jnp.asarray(np.tile(RATIO, (ROWS, elems_z)), F32)

time: 165 us -> 162 us (0.982)
  waiting for transfers between devices: 40.2 us -> 36.9 us
  local copies, waits for them, and re-layouts: 1.53 us -> 3.61 us
  starting transfers between devices: 59.1 us -> 57.2 us
    ppermute x2, waiting for transfers between devices: 2.88 us -> 0.01 us  [from_next(): return lax.ppermute(value, axis, [(i, (i - 1) % size) for i in range(size)])]
    ppermute x14, starting transfers between devices: 46.9 us -> 44.3 us  [swaps(): lax.ppermute(odd, axis, [(i, ((i + 1 ^ 1) - 1) % size) for i in range(siz...]
    pallas_call x37 -> x38, Pallas kernels: 60.8 us -> 60.9 us  [call(): pl.pallas_call(kernel, in_specs=[SM] * smem + [VM] * (len(inputs) - smem)...]
  transfers between devices with their start and end apart: 30 -> 30, of which waited for: 14 -> 14; matrix products, arithmetic and copies ran while one was open for 0% -> 0% of each run, Pallas kernels for 29% -> 32%
where the time goes in v5:
time: 162 us
  Pallas kernels  60.9 us (38%)
  starting transfers between devices  57.2 us (35%)
  waiting for transfers between devices  36.9 us (23%)
  local copies, waits for them, and re-layouts  3.61 us (2%)
  between operations  2.81 us (2%)
    pallas_call x38, Pallas kernels, call(): pl.pallas_call(kernel, in_specs=[SM] * smem + [VM] * (len(inputs) - smem)...  60.9 us
    ppermute x14, starting transfers between devices, swaps(): lax.ppermute(odd, axis, [(i, ((i + 1 ^ 1) - 1) % size) for i in range(siz...  44.3 us
    ppermute x14, waiting for transfers between devices, swaps(): lax.ppermute(odd, axis, [(i, ((i + 1 ^ 1) - 1) % size) for i in range(siz...  36.9 us
    ppermute x2, starting transfers between devices, from_next(): return lax.ppermute(value, axis, [(i, (i - 1) % size) for i in range(size)])  11.6 us
  transfers between devices with their start and end apart: 30, of which 14 were waited for; matrix products, arithmetic and copies ran while one was open for 0% of the time, Pallas kernels for 32%

profile of v5, /device:TPU:0, one launch (start us, length us, event | category | flops | bytes accessed | tf_op | source)
XLA Modules:
  0.0 161.5 jit_solution(6568544140334886521)
XLA Ops:
  1.6 7.4 %collective-permute-start = (f32[6,8,4,128]{3,2,1,0:T(4,128)S(1)}, f32[6,8,4,128]{3,2,1,0:T(4,128)S(1)}, u32[]{:S(2)}, u32[]{:S(2)}) collective-permute-start(f32[6,8,4,128]{3,2,1,0:T(4,128)S(1)} %shard_map.133), channel_id=1, source_target_pairs={{0,15},{1,0},{2,1},{3,2},{4,3},{5,4},{6,5},{7,6},{8,7},{9,8},{10,9... | collective-permute-start | bytes 294920 | tf_op jit(solution)/shard_map/ppermute | solution.py:738
  16.1 4.2 %collective-permute-start.1 = (f32[6,8,4,128]{3,2,1,0:T(4,128)S(1)}, f32[6,8,4,128]{3,2,1,0:T(4,128)S(1)}, u32[]{:S(2)}, u32[]{:S(2)}) collective-permute-start(f32[6,8,4,128]{3,2,1,0:T(4,128)S(1)} %shard_map.135), channel_id=1, source_target_pairs={{0,240},{16,0},{32,16},{48,32},{64,48},{80,64},{96,80},{112,96},{1... | collective-permute-start | bytes 294920 | tf_op jit(solution)/shard_map/ppermute | solution.py:738
  25.2 3.4 %collective-permute-start.3 = (f32[6,8,4,128]{3,2,1,0:T(4,128)S(1)}, f32[6,8,4,128]{3,2,1,0:T(4,128)S(1)}, u32[]{:S(2)}, u32[]{:S(2)}) collective-permute-start(f32[6,8,4,128]{3,2,1,0:T(4,128)S(1)} %get-tuple-element.195), channel_id=1, source_target_pairs={{0,15},{1,2},{2,1},{3,4},{4,3},{5,6},{6,5},{7,8},{8,7},{9,10},{10,... | collective-permute-start | bytes 294920 | tf_op jit(solution)/shard_map/ppermute | solution.py:724
  30.0 3.9 %shard_map.139 = (f32[3,8,2,8,128]{4,3,2,1,0:T(8,128)S(1)}, f32[3,6,8,8,128]{4,3,2,1,0:T(8,128)S(1)}, f32[3,8,8,8,128]{4,3,2,1,0:T(8,128)S(1)}) custom-call(f32[8,8,128]{2,1,0:T(8,128)S(1)} %broadcast_in_dim.2.ctl_ref.refs_0_, bf16[256,256]{1,0:T(8,128)(2,1)S(1)} %copy-done, bf16[256,256]{1,0:T(8,128)(2,1)S(1)} %copy-done.1, bf16[256,128]{1,0:T(8,128)(2,1)S(1)} %copy-done.2, ...), custom_call_target="tpu_custom_call" | custom-call | tf_op jit(solution)/shard_map/pallas_call | solution.py:712
  35.7 4.9 %collective-permute-start.5 = (f32[6,8,4,128]{3,2,1,0:T(4,128)S(1)}, f32[6,8,4,128]{3,2,1,0:T(4,128)S(1)}, u32[]{:S(2)}, u32[]{:S(2)}) collective-permute-start(f32[6,8,4,128]{3,2,1,0:T(4,128)S(1)} %get-tuple-element.197), channel_id=1, source_target_pairs={{0,240},{16,32},{32,16},{48,64},{64,48},{80,96},{96,80},{112,128},... | collective-permute-start | bytes 294920 | tf_op jit(solution)/shard_map/ppermute | solution.py:724
  47.6 4.0 %shard_map.145 = (f32[3,8,2,8,128]{4,3,2,1,0:T(8,128)S(1)}, f32[3,8,2,8,128]{4,3,2,1,0:T(8,128)S(1)}, f32[3,8,2,8,128]{4,3,2,1,0:T(8,128)S(1)}, f32[3,6,8,8,128]{4,3,2,1,0:T(8,128)S(1)}, f32[3,8,8,8,128]{4,3,2,1,0:T(8,128)S(1)}) custom-call(f32[8,8,128]{2,1,0:T(8,128)S(1)} %broadcast_in_dim.2.ctl_ref.refs_0_, bf16[256,256]{1,0:T(8,128)(2,1)S(1)} %copy-done, ...), custom_call_target="tpu_custom_call" | custom-call | tf_op jit(solution)/shard_map/pallas_call | solution.py:712
  51.6 3.6 %collective-permute-done.7.xo_ref.refs_6_.refs_10_ = f32[3,8,4,128]{3,2,1,0:T(4,128)S(1)} collective-permute-done((f32[3,8,4,128]{3,2,1,0:T(4,128)S(1)}, f32[3,8,4,128]{3,2,1,0:T(4,128)S(1)}, u32[]{:S(2)}, u32[]{:S(2)}) %collective-permute-start.7) | collective-permute-done | bytes 49184 | tf_op jit(solution)/shard_map/ppermute | solution.py:724
  55.4 4.8 %collective-permute-start.9 = (f32[3,8,4,128]{3,2,1,0:T(4,128)S(1)}, f32[3,8,4,128]{3,2,1,0:T(4,128)S(1)}, u32[]{:S(2)}, u32[]{:S(2)}) collective-permute-start(f32[3,8,4,128]{3,2,1,0:T(4,128)S(1)} %get-tuple-element.221), channel_id=1, source_target_pairs={{0,240},{16,32},{32,16},{48,64},{64,48},{80,96},{96,80},{112,128},... | collective-permute-start | bytes 147464 | tf_op jit(solution)/shard_map/ppermute | solution.py:724
  65.8 4.0 %shard_map.149 = (f32[3,8,2,8,128]{4,3,2,1,0:T(8,128)S(1)}, f32[3,8,2,8,128]{4,3,2,1,0:T(8,128)S(1)}, f32[3,6,8,8,128]{4,3,2,1,0:T(8,128)S(1)}, f32[3,8,8,8,128]{4,3,2,1,0:T(8,128)S(1)}) custom-call(f32[8,8,128]{2,1,0:T(8,128)S(1)} %broadcast_in_dim.2.ctl_ref.refs_0_, bf16[256,256]{1,0:T(8,128)(2,1)S(1)} %copy-done, bf16[256,256]{1,0:T(8,128)(2,1)S(1)} %copy-done.1, ...), custom_call_target="tpu_custom_call" | custom-call | tf_op jit(solution)/shard_map/pallas_call | solution.py:712
  69.8 4.5 %collective-permute-done.11.xo_ref.refs_6_.refs_10_ = f32[3,8,4,128]{3,2,1,0:T(4,128)S(1)} collective-permute-done((f32[3,8,4,128]{3,2,1,0:T(4,128)S(1)}, f32[3,8,4,128]{3,2,1,0:T(4,128)S(1)}, u32[]{:S(2)}, u32[]{:S(2)}) %collective-permute-start.11) | collective-permute-done | bytes 49184 | tf_op jit(solution)/shard_map/ppermute | solution.py:724
  74.5 4.7 %collective-permute-start.13 = (f32[3,8,4,128]{3,2,1,0:T(4,128)S(1)}, f32[3,8,4,128]{3,2,1,0:T(4,128)S(1)}, u32[]{:S(2)}, u32[]{:S(2)}) collective-permute-start(f32[3,8,4,128]{3,2,1,0:T(4,128)S(1)} %get-tuple-element.249), channel_id=1, source_target_pairs={{0,240},{16,32},{32,16},{48,64},{64,48},{80,96},{96,80},{112,128},... | collective-permute-start | bytes 147464 | tf_op jit(solution)/shard_map/ppermute | solution.py:724
  84.8 4.0 %shard_map.153 = (f32[3,8,2,8,128]{4,3,2,1,0:T(8,128)S(1)}, f32[3,6,8,8,128]{4,3,2,1,0:T(8,128)S(1)}, f32[3,8,8,8,128]{4,3,2,1,0:T(8,128)S(1)}) custom-call(f32[8,8,128]{2,1,0:T(8,128)S(1)} %broadcast_in_dim.2.ctl_ref.refs_0_, bf16[256,256]{1,0:T(8,128)(2,1)S(1)} %copy-done, bf16[256,256]{1,0:T(8,128)(2,1)S(1)} %copy-done.1, bf16[256,128]{1,0:T(8,128)(2,1)S(1)} %copy-done.2, ...), custom_call_target="tpu_custom_call" | custom-call | tf_op jit(solution)/shard_map/pallas_call | solution.py:712
  88.7 4.5 %collective-permute-done.15.xo_ref.refs_6_.refs_10_ = f32[3,8,4,128]{3,2,1,0:T(4,128)S(1)} collective-permute-done((f32[3,8,4,128]{3,2,1,0:T(4,128)S(1)}, f32[3,8,4,128]{3,2,1,0:T(4,128)S(1)}, u32[]{:S(2)}, u32[]{:S(2)}) %collective-permute-start.15) | collective-permute-done | bytes 49184 | tf_op jit(solution)/shard_map/ppermute | solution.py:724
  93.4 4.8 %collective-permute-start.17 = (f32[3,8,4,128]{3,2,1,0:T(4,128)S(1)}, f32[3,8,4,128]{3,2,1,0:T(4,128)S(1)}, u32[]{:S(2)}, u32[]{:S(2)}) collective-permute-start(f32[3,8,4,128]{3,2,1,0:T(4,128)S(1)} %get-tuple-element.273), channel_id=1, source_target_pairs={{0,240},{16,32},{32,16},{48,64},{64,48},{80,96},{96,80},{112,128},... | collective-permute-start | bytes 147464 | tf_op jit(solution)/shard_map/ppermute | solution.py:724
  103.9 4.0 %shard_map.157 = (f32[3,8,2,8,128]{4,3,2,1,0:T(8,128)S(1)}, f32[3,8,2,8,128]{4,3,2,1,0:T(8,128)S(1)}, f32[3,6,8,8,128]{4,3,2,1,0:T(8,128)S(1)}, f32[3,8,8,8,128]{4,3,2,1,0:T(8,128)S(1)}) custom-call(f32[8,8,128]{2,1,0:T(8,128)S(1)} %broadcast_in_dim.2.ctl_ref.refs_0_, bf16[256,256]{1,0:T(8,128)(2,1)S(1)} %copy-done, bf16[256,256]{1,0:T(8,128)(2,1)S(1)} %copy-done.1, ...), custom_call_target="tpu_custom_call" | custom-call | tf_op jit(solution)/shard_map/pallas_call | solution.py:712
  107.8 4.6 %collective-permute-done.19.xo_ref.refs_6_.refs_10_ = f32[3,8,4,128]{3,2,1,0:T(4,128)S(1)} collective-permute-done((f32[3,8,4,128]{3,2,1,0:T(4,128)S(1)}, f32[3,8,4,128]{3,2,1,0:T(4,128)S(1)}, u32[]{:S(2)}, u32[]{:S(2)}) %collective-permute-start.19) | collective-permute-done | bytes 49184 | tf_op jit(solution)/shard_map/ppermute | solution.py:724
  112.6 4.7 %collective-permute-start.21 = (f32[3,8,4,128]{3,2,1,0:T(4,128)S(1)}, f32[3,8,4,128]{3,2,1,0:T(4,128)S(1)}, u32[]{:S(2)}, u32[]{:S(2)}) collective-permute-start(f32[3,8,4,128]{3,2,1,0:T(4,128)S(1)} %get-tuple-element.293), channel_id=1, source_target_pairs={{0,240},{16,32},{32,16},{48,64},{64,48},{80,96},{96,80},{112,128},... | collective-permute-start | bytes 147464 | tf_op jit(solution)/shard_map/ppermute | solution.py:724
  122.8 4.0 %shard_map.161 = (f32[3,8,2,8,128]{4,3,2,1,0:T(8,128)S(1)}, f32[3,8,2,8,128]{4,3,2,1,0:T(8,128)S(1)}, f32[3,6,8,8,128]{4,3,2,1,0:T(8,128)S(1)}, f32[3,8,8,8,128]{4,3,2,1,0:T(8,128)S(1)}) custom-call(f32[8,8,128]{2,1,0:T(8,128)S(1)} %broadcast_in_dim.2.ctl_ref.refs_0_, bf16[256,256]{1,0:T(8,128)(2,1)S(1)} %copy-done, bf16[256,256]{1,0:T(8,128)(2,1)S(1)} %copy-done.1, ...), custom_call_target="tpu_custom_call" | custom-call | tf_op jit(solution)/shard_map/pallas_call | solution.py:712
  126.8 4.7 %collective-permute-done.23.refs_6_.xo_ref.refs_10_ = f32[3,8,4,128]{3,2,1,0:T(4,128)S(1)} collective-permute-done((f32[3,8,4,128]{3,2,1,0:T(4,128)S(1)}, f32[3,8,4,128]{3,2,1,0:T(4,128)S(1)}, u32[]{:S(2)}, u32[]{:S(2)}) %collective-permute-start.23) | collective-permute-done | bytes 49184 | tf_op jit(solution)/shard_map/ppermute | solution.py:724
  131.6 4.6 %collective-permute-start.25 = (f32[3,8,4,128]{3,2,1,0:T(4,128)S(1)}, f32[3,8,4,128]{3,2,1,0:T(4,128)S(1)}, u32[]{:S(2)}, u32[]{:S(2)}) collective-permute-start(f32[3,8,4,128]{3,2,1,0:T(4,128)S(1)} %get-tuple-element.322), channel_id=1, source_target_pairs={{0,240},{16,32},{32,16},{48,64},{64,48},{80,96},{96,80},{112,128},... | collective-permute-start | bytes 147464 | tf_op jit(solution)/shard_map/ppermute | solution.py:724
  141.8 4.0 %shard_map.165 = (f32[3,8,2,8,128]{4,3,2,1,0:T(8,128)S(1)}, f32[3,6,8,8,128]{4,3,2,1,0:T(8,128)S(1)}, f32[3,8,8,8,128]{4,3,2,1,0:T(8,128)S(1)}) custom-call(f32[8,8,128]{2,1,0:T(8,128)S(1)} %broadcast_in_dim.2.ctl_ref.refs_0_, bf16[256,256]{1,0:T(8,128)(2,1)S(1)} %copy-done, bf16[256,256]{1,0:T(8,128)(2,1)S(1)} %copy-done.1, bf16[256,128]{1,0:T(8,128)(2,1)S(1)} %copy-done.2, ...), custom_call_target="tpu_custom_call" | custom-call | tf_op jit(solution)/shard_map/pallas_call | solution.py:712
  145.8 4.7 %collective-permute-done.27.xo_ref.refs_7_ = f32[3,8,4,128]{3,2,1,0:T(4,128)S(1)} collective-permute-done((f32[3,8,4,128]{3,2,1,0:T(4,128)S(1)}, f32[3,8,4,128]{3,2,1,0:T(4,128)S(1)}, u32[]{:S(2)}, u32[]{:S(2)}) %collective-permute-start.27) | collective-permute-done | bytes 49184 | tf_op jit(solution)/shard_map/ppermute | solution.py:724
  150.6 4.6 %collective-permute-start.29 = (f32[3,8,4,128]{3,2,1,0:T(4,128)S(1)}, f32[3,8,4,128]{3,2,1,0:T(4,128)S(1)}, u32[]{:S(2)}, u32[]{:S(2)}) collective-permute-start(f32[3,8,4,128]{3,2,1,0:T(4,128)S(1)} %get-tuple-element.345), channel_id=1, source_target_pairs={{0,240},{16,32},{32,16},{48,64},{64,48},{80,96},{96,80},{112,128},... | collective-permute-start | bytes 147464 | tf_op jit(solution)/shard_map/ppermute | solution.py:724
  158.7 2.8 %shard_map.168 = f32[3,28,3108]{2,1,0:T(8,128)} custom-call(f32[8,8,128]{2,1,0:T(8,128)S(1)} %broadcast_in_dim.2.ctl_ref.refs_0_, f32[3,8,8,8,128]{4,3,2,1,0:T(8,128)S(1)} %get-tuple-element.201.refs_10_.refs_19_.refs_8_.refs_17_.refs_1_, f32[3,8,8,8,128]{4,3,2,1,0:T(8,128)S(1)} %get-tuple-element.203.refs_12_.refs_19_.refs_17_.refs_11_.refs_2_, ...), custom_call_target="tpu_custom_call" | custom-call | tf_op jit(solution)/shard_map/pallas_call | solution.py:712
  (99 shorter events, 53.5 us)
Async XLA Ops:
  1.6 14.4 %collective-permute-start = (f32[6,8,4,128]{3,2,1,0:T(4,128)S(1)}, f32[6,8,4,128]{3,2,1,0:T(4,128)S(1)}, u32[]{:S(2)}, u32[]{:S(2)}) collective-permute-start(f32[6,8,4,128]{3,2,1,0:T(4,128)S(1)} %shard_map.133), channel_id=1, source_target_pairs={{0,15},{1,0},{2,1},{3,2},{4,3},{5,4},{6,5},{7,6},{8,7},{9,8},{10,9... | collective-permute-start | bytes 294920 | tf_op jit(solution)/shard_map/ppermute | solution.py:738
  16.1 8.1 %collective-permute-start.1 = (f32[6,8,4,128]{3,2,1,0:T(4,128)S(1)}, f32[6,8,4,128]{3,2,1,0:T(4,128)S(1)}, u32[]{:S(2)}, u32[]{:S(2)}) collective-permute-start(f32[6,8,4,128]{3,2,1,0:T(4,128)S(1)} %shard_map.135), channel_id=1, source_target_pairs={{0,240},{16,0},{32,16},{48,32},{64,48},{80,64},{96,80},{112,96},{1... | collective-permute-start | bytes 294920 | tf_op jit(solution)/shard_map/ppermute | solution.py:738
  25.1 8.8 %collective-permute-start.2 = (f32[6,8,4,128]{3,2,1,0:T(4,128)S(1)}, f32[6,8,4,128]{3,2,1,0:T(4,128)S(1)}, u32[]{:S(2)}, u32[]{:S(2)}) collective-permute-start(f32[6,8,4,128]{3,2,1,0:T(4,128)S(1)} %get-tuple-element.194), channel_id=1, source_target_pairs={{0,1},{1,0},{2,3},{3,2},{4,5},{5,4},{6,7},{7,6},{8,9},{9,8},{10,11... | collective-permute-start | bytes 294920 | tf_op jit(solution)/shard_map/ppermute | solution.py:725
  25.2 10.2 %collective-permute-start.3 = (f32[6,8,4,128]{3,2,1,0:T(4,128)S(1)}, f32[6,8,4,128]{3,2,1,0:T(4,128)S(1)}, u32[]{:S(2)}, u32[]{:S(2)}) collective-permute-start(f32[6,8,4,128]{3,2,1,0:T(4,128)S(1)} %get-tuple-element.195), channel_id=1, source_target_pairs={{0,15},{1,2},{2,1},{3,4},{4,3},{5,6},{6,5},{7,8},{8,7},{9,10},{10,... | collective-permute-start | bytes 294920 | tf_op jit(solution)/shard_map/ppermute | solution.py:724
  35.6 7.4 %collective-permute-start.4 = (f32[6,8,4,128]{3,2,1,0:T(4,128)S(1)}, f32[6,8,4,128]{3,2,1,0:T(4,128)S(1)}, u32[]{:S(2)}, u32[]{:S(2)}) collective-permute-start(f32[6,8,4,128]{3,2,1,0:T(4,128)S(1)} %get-tuple-element.196), channel_id=1, source_target_pairs={{0,16},{16,0},{32,48},{48,32},{64,80},{80,64},{96,112},{112,96},{1... | collective-permute-start | bytes 294920 | tf_op jit(solution)/shard_map/ppermute | solution.py:725
  35.7 8.7 %collective-permute-start.5 = (f32[6,8,4,128]{3,2,1,0:T(4,128)S(1)}, f32[6,8,4,128]{3,2,1,0:T(4,128)S(1)}, u32[]{:S(2)}, u32[]{:S(2)}) collective-permute-start(f32[6,8,4,128]{3,2,1,0:T(4,128)S(1)} %get-tuple-element.197), channel_id=1, source_target_pairs={{0,240},{16,32},{32,16},{48,64},{64,48},{80,96},{96,80},{112,128},... | collective-permute-start | bytes 294920 | tf_op jit(solution)/shard_map/ppermute | solution.py:724
  45.5 9.7 %collective-permute-start.7 = (f32[3,8,4,128]{3,2,1,0:T(4,128)S(1)}, f32[3,8,4,128]{3,2,1,0:T(4,128)S(1)}, u32[]{:S(2)}, u32[]{:S(2)}) collective-permute-start(f32[3,8,4,128]{3,2,1,0:T(4,128)S(1)} %get-tuple-element.219), channel_id=1, source_target_pairs={{0,15},{1,2},{2,1},{3,4},{4,3},{5,6},{6,5},{7,8},{8,7},{9,10},{10,... | collective-permute-start | bytes 147464 | tf_op jit(solution)/shard_map/ppermute | solution.py:724
  55.3 7.0 %collective-permute-start.8 = (f32[3,8,4,128]{3,2,1,0:T(4,128)S(1)}, f32[3,8,4,128]{3,2,1,0:T(4,128)S(1)}, u32[]{:S(2)}, u32[]{:S(2)}) collective-permute-start(f32[3,8,4,128]{3,2,1,0:T(4,128)S(1)} %get-tuple-element.220), channel_id=1, source_target_pairs={{0,16},{16,0},{32,48},{48,32},{64,80},{80,64},{96,112},{112,96},{1... | collective-permute-start | bytes 147464 | tf_op jit(solution)/shard_map/ppermute | solution.py:725
  55.4 8.3 %collective-permute-start.9 = (f32[3,8,4,128]{3,2,1,0:T(4,128)S(1)}, f32[3,8,4,128]{3,2,1,0:T(4,128)S(1)}, u32[]{:S(2)}, u32[]{:S(2)}) collective-permute-start(f32[3,8,4,128]{3,2,1,0:T(4,128)S(1)} %get-tuple-element.221), channel_id=1, source_target_pairs={{0,240},{16,32},{32,16},{48,64},{64,48},{80,96},{96,80},{112,128},... | collective-permute-start | bytes 147464 | tf_op jit(solution)/shard_map/ppermute | solution.py:724
  64.7 9.6 %collective-permute-start.11 = (f32[3,8,4,128]{3,2,1,0:T(4,128)S(1)}, f32[3,8,4,128]{3,2,1,0:T(4,128)S(1)}, u32[]{:S(2)}, u32[]{:S(2)}) collective-permute-start(f32[3,8,4,128]{3,2,1,0:T(4,128)S(1)} %get-tuple-element.247), channel_id=1, source_target_pairs={{0,15},{1,2},{2,1},{3,4},{4,3},{5,6},{6,5},{7,8},{8,7},{9,10},{10,... | collective-permute-start | bytes 147464 | tf_op jit(solution)/shard_map/ppermute | solution.py:724
  74.4 6.9 %collective-permute-start.12 = (f32[3,8,4,128]{3,2,1,0:T(4,128)S(1)}, f32[3,8,4,128]{3,2,1,0:T(4,128)S(1)}, u32[]{:S(2)}, u32[]{:S(2)}) collective-permute-start(f32[3,8,4,128]{3,2,1,0:T(4,128)S(1)} %get-tuple-element.248), channel_id=1, source_target_pairs={{0,16},{16,0},{32,48},{48,32},{64,80},{80,64},{96,112},{112,96},{1... | collective-permute-start | bytes 147464 | tf_op jit(solution)/shard_map/ppermute | solution.py:725
  74.5 8.1 %collective-permute-start.13 = (f32[3,8,4,128]{3,2,1,0:T(4,128)S(1)}, f32[3,8,4,128]{3,2,1,0:T(4,128)S(1)}, u32[]{:S(2)}, u32[]{:S(2)}) collective-permute-start(f32[3,8,4,128]{3,2,1,0:T(4,128)S(1)} %get-tuple-element.249), channel_id=1, source_target_pairs={{0,240},{16,32},{32,16},{48,64},{64,48},{80,96},{96,80},{112,128},... | collective-permute-start | bytes 147464 | tf_op jit(solution)/shard_map/ppermute | solution.py:724
  83.6 9.7 %collective-permute-start.15 = (f32[3,8,4,128]{3,2,1,0:T(4,128)S(1)}, f32[3,8,4,128]{3,2,1,0:T(4,128)S(1)}, u32[]{:S(2)}, u32[]{:S(2)}) collective-permute-start(f32[3,8,4,128]{3,2,1,0:T(4,128)S(1)} %get-tuple-element.271), channel_id=1, source_target_pairs={{0,15},{1,2},{2,1},{3,4},{4,3},{5,6},{6,5},{7,8},{8,7},{9,10},{10,... | collective-permute-start | bytes 147464 | tf_op jit(solution)/shard_map/ppermute | solution.py:724
  93.3 6.9 %collective-permute-start.16 = (f32[3,8,4,128]{3,2,1,0:T(4,128)S(1)}, f32[3,8,4,128]{3,2,1,0:T(4,128)S(1)}, u32[]{:S(2)}, u32[]{:S(2)}) collective-permute-start(f32[3,8,4,128]{3,2,1,0:T(4,128)S(1)} %get-tuple-element.272), channel_id=1, source_target_pairs={{0,16},{16,0},{32,48},{48,32},{64,80},{80,64},{96,112},{112,96},{1... | collective-permute-start | bytes 147464 | tf_op jit(solution)/shard_map/ppermute | solution.py:725
  93.4 8.1 %collective-permute-start.17 = (f32[3,8,4,128]{3,2,1,0:T(4,128)S(1)}, f32[3,8,4,128]{3,2,1,0:T(4,128)S(1)}, u32[]{:S(2)}, u32[]{:S(2)}) collective-permute-start(f32[3,8,4,128]{3,2,1,0:T(4,128)S(1)} %get-tuple-element.273), channel_id=1, source_target_pairs={{0,240},{16,32},{32,16},{48,64},{64,48},{80,96},{96,80},{112,128},... | collective-permute-start | bytes 147464 | tf_op jit(solution)/shard_map/ppermute | solution.py:724
  102.5 9.9 %collective-permute-start.19 = (f32[3,8,4,128]{3,2,1,0:T(4,128)S(1)}, f32[3,8,4,128]{3,2,1,0:T(4,128)S(1)}, u32[]{:S(2)}, u32[]{:S(2)}) collective-permute-start(f32[3,8,4,128]{3,2,1,0:T(4,128)S(1)} %get-tuple-element.291), channel_id=1, source_target_pairs={{0,15},{1,2},{2,1},{3,4},{4,3},{5,6},{6,5},{7,8},{8,7},{9,10},{10,... | collective-permute-start | bytes 147464 | tf_op jit(solution)/shard_map/ppermute | solution.py:724
  112.5 6.9 %collective-permute-start.20 = (f32[3,8,4,128]{3,2,1,0:T(4,128)S(1)}, f32[3,8,4,128]{3,2,1,0:T(4,128)S(1)}, u32[]{:S(2)}, u32[]{:S(2)}) collective-permute-start(f32[3,8,4,128]{3,2,1,0:T(4,128)S(1)} %get-tuple-element.292), channel_id=1, source_target_pairs={{0,16},{16,0},{32,48},{48,32},{64,80},{80,64},{96,112},{112,96},{1... | collective-permute-start | bytes 147464 | tf_op jit(solution)/shard_map/ppermute | solution.py:725
  112.6 8.1 %collective-permute-start.21 = (f32[3,8,4,128]{3,2,1,0:T(4,128)S(1)}, f32[3,8,4,128]{3,2,1,0:T(4,128)S(1)}, u32[]{:S(2)}, u32[]{:S(2)}) collective-permute-start(f32[3,8,4,128]{3,2,1,0:T(4,128)S(1)} %get-tuple-element.293), channel_id=1, source_target_pairs={{0,240},{16,32},{32,16},{48,64},{64,48},{80,96},{96,80},{112,128},... | collective-permute-start | bytes 147464 | tf_op jit(solution)/shard_map/ppermute | solution.py:724
  121.7 9.7 %collective-permute-start.23 = (f32[3,8,4,128]{3,2,1,0:T(4,128)S(1)}, f32[3,8,4,128]{3,2,1,0:T(4,128)S(1)}, u32[]{:S(2)}, u32[]{:S(2)}) collective-permute-start(f32[3,8,4,128]{3,2,1,0:T(4,128)S(1)} %get-tuple-element.315), channel_id=1, source_target_pairs={{0,15},{1,2},{2,1},{3,4},{4,3},{5,6},{6,5},{7,8},{8,7},{9,10},{10,... | collective-permute-start | bytes 147464 | tf_op jit(solution)/shard_map/ppermute | solution.py:724
  131.5 6.8 %collective-permute-start.24 = (f32[3,8,4,128]{3,2,1,0:T(4,128)S(1)}, f32[3,8,4,128]{3,2,1,0:T(4,128)S(1)}, u32[]{:S(2)}, u32[]{:S(2)}) collective-permute-start(f32[3,8,4,128]{3,2,1,0:T(4,128)S(1)} %get-tuple-element.321), channel_id=1, source_target_pairs={{0,16},{16,0},{32,48},{48,32},{64,80},{80,64},{96,112},{112,96},{1... | collective-permute-start | bytes 147464 | tf_op jit(solution)/shard_map/ppermute | solution.py:725
  131.6 8.1 %collective-permute-start.25 = (f32[3,8,4,128]{3,2,1,0:T(4,128)S(1)}, f32[3,8,4,128]{3,2,1,0:T(4,128)S(1)}, u32[]{:S(2)}, u32[]{:S(2)}) collective-permute-start(f32[3,8,4,128]{3,2,1,0:T(4,128)S(1)} %get-tuple-element.322), channel_id=1, source_target_pairs={{0,240},{16,32},{32,16},{48,64},{64,48},{80,96},{96,80},{112,128},... | collective-permute-start | bytes 147464 | tf_op jit(solution)/shard_map/ppermute | solution.py:724
  140.8 9.7 %collective-permute-start.27 = (f32[3,8,4,128]{3,2,1,0:T(4,128)S(1)}, f32[3,8,4,128]{3,2,1,0:T(4,128)S(1)}, u32[]{:S(2)}, u32[]{:S(2)}) collective-permute-start(f32[3,8,4,128]{3,2,1,0:T(4,128)S(1)} %get-tuple-element.343), channel_id=1, source_target_pairs={{0,15},{1,2},{2,1},{3,4},{4,3},{5,6},{6,5},{7,8},{8,7},{9,10},{10,... | collective-permute-start | bytes 147464 | tf_op jit(solution)/shard_map/ppermute | solution.py:724
  150.5 7.5 %collective-permute-start.28 = (f32[3,8,4,128]{3,2,1,0:T(4,128)S(1)}, f32[3,8,4,128]{3,2,1,0:T(4,128)S(1)}, u32[]{:S(2)}, u32[]{:S(2)}) collective-permute-start(f32[3,8,4,128]{3,2,1,0:T(4,128)S(1)} %get-tuple-element.344), channel_id=1, source_target_pairs={{0,16},{16,0},{32,48},{48,32},{64,80},{80,64},{96,112},{112,96},{1... | collective-permute-start | bytes 147464 | tf_op jit(solution)/shard_map/ppermute | solution.py:725
  150.6 8.1 %collective-permute-start.29 = (f32[3,8,4,128]{3,2,1,0:T(4,128)S(1)}, f32[3,8,4,128]{3,2,1,0:T(4,128)S(1)}, u32[]{:S(2)}, u32[]{:S(2)}) collective-permute-start(f32[3,8,4,128]{3,2,1,0:T(4,128)S(1)} %get-tuple-element.345), channel_id=1, source_target_pairs={{0,240},{16,32},{32,16},{48,64},{64,48},{80,96},{96,80},{112,128},... | collective-permute-start | bytes 147464 | tf_op jit(solution)/shard_map/ppermute | solution.py:724
  (16 other events, 94.1 us)
